TPU v7x, 32 devices: a whole 2x2x4 slice. The times are simulated.
32 devices in a mesh: seq: 4 (over y, x), fsdp: 8 (over z, core).
Axes of the slice: x: 2, y: 2, z: 4, core: 2. Of those that a mesh axis runs over, the one named last changes fastest.
Arguments:
- tokens: bfloat16 [8, 1024, 1024], P('fsdp', 'seq'), may hold values from -6 to 6
- lengths: int32 [8, 8], P('fsdp'), may hold values from 1 to 512, 1024 in all within a row
- packing: int32 [8, 1024], P('fsdp'), may hold values from 0 to 1023, as said below
- norm_in: bfloat16 [1024], P('fsdp'), may hold values from 0.25 to 1.75
- w_query: bfloat16 [1024, 2048], P('fsdp'), may hold values from -0.1875 to 0.1875
- key_projection: bfloat16 [1024, 1024], P('fsdp'), may hold values from -0.1875 to 0.1875
- value_projection: bfloat16 [1024, 1024], P('fsdp'), may hold values from -0.1875 to 0.1875
- norm_query: bfloat16 [128], P('fsdp'), may hold values from 1 to 1.796875
- norm_key: bfloat16 [128], P('fsdp'), may hold values from 1 to 1.796875
- w_out: bfloat16 [2048, 1024], P('fsdp'), may hold values from -1 to 1
- norm_post: bfloat16 [1024], P('fsdp'), may hold values from 0.25 to 1.75
- w_gate: bfloat16 [1024, 3072], P('fsdp'), may hold values from -0.1875 to 0.1875
- w_up: bfloat16 [1024, 3072], P('fsdp'), may hold values from -0.1875 to 0.1875
- w_down: bfloat16 [3072, 1024], P('fsdp'), may hold values from -0.109375 to 0.109375
- cotangent: bfloat16 [8, 1024, 1024], P('fsdp', 'seq'), may hold values from -6 to 6
Outputs:
- output: bfloat16 [8, 1024, 1024], P('fsdp', 'seq')
- input_grad: bfloat16 [8, 1024, 1024], P('fsdp', 'seq')
- grad_norm_in: float32 [1024], P('fsdp')
- grad_w_query: float32 [1024, 2048], P('fsdp')
- grad_w_key: float32 [1024, 1024], P('fsdp')
- grad_w_value: float32 [1024, 1024], P('fsdp')
- grad_norm_query: float32 [128], P('fsdp')
- grad_norm_key: float32 [128], P('fsdp')
- grad_w_out: float32 [2048, 1024], P('fsdp')
- grad_norm_post: float32 [1024], P('fsdp')
- grad_w_gate: float32 [1024, 3072], P('fsdp')
- grad_w_up: float32 [1024, 3072], P('fsdp')
- grad_w_down: float32 [3072, 1024], P('fsdp')
Inputs may be any that keep to these rules, and one draw needn't show every extreme that they name: The 8 lengths of each row add up to 1024, and the longest is exactly 512. Each row of packing names every token of its row once. Of the given-order positions s * 256 to (s + 1) * 256 - 1, exactly 64 are named in each aligned block of 256 packed positions.
All inputs are finite; a program needn't handle non-finite values.
Results may differ from a plain program's by a relative error of at most 0.02.
Values may be sent and summed in bfloat16 or wider, within the bound.
A program may use at most 192 MiB of HBM per device.

v0:
```python
import jax
import jax.numpy as jnp
from jax import lax
from jax.sharding import PartitionSpec as P

HQ = 16
KEY_VALUE_HEADS = 8
HEAD_SIZE = 128


ROPE_BASE = 1000000.0
EPSILON = 1e-06
MASKED = -1e30


def matrix_product(left, right):
    return jnp.dot(left, right, preferred_element_type=jnp.float32)


def outer_sum(left, right):
    return lax.dot_general(
        left, right, (((0,), (0,)), ((), ())), preferred_element_type=jnp.float32
    )


def back_matmul(left, right):
    return lax.dot_general(
        left, right, (((1,), (1,)), ((), ())), preferred_element_type=jnp.float32
    )


def rms_scale(value_tensor, gain_values):
    return (
        value_tensor
        * lax.rsqrt(jnp.mean(value_tensor * value_tensor, axis=-1, keepdims=True) + EPSILON)
        * gain_values
    )


def rotary(value_tensor, start_offset):
    half_width = value_tensor.shape[-1] // 2
    inv_freq = ROPE_BASE ** (-jnp.arange(half_width, dtype=jnp.float32) / half_width)
    angles = start_offset.astype(jnp.float32)[:, None] * inv_freq[None, :]
    cosine = jnp.cos(angles)[:, None, :]
    sine_part = jnp.sin(angles)[:, None, :]
    first_half = value_tensor[..., :half_width]
    second = value_tensor[..., half_width:]
    return jnp.concatenate(
        [first_half * cosine - second * sine_part, second * cosine + first_half * sine_part],
        axis=-1,
    )


def head_front(pre_values, gain_values, start_offset):
    return rotary(rms_scale(pre_values, gain_values), start_offset)


def row_lookup_tables(row_lengths, count_of_rows):
    places = jnp.arange(count_of_rows, dtype=jnp.int32)
    doc_ends = jnp.cumsum(row_lengths)
    passed = (places[:, None] >= doc_ends[None, :]).astype(jnp.int32)
    document_segment = jnp.sum(passed, axis=1)
    start_offset = places - jnp.sum(passed * row_lengths[None, :], axis=1)
    return (document_segment, start_offset)


def masked_scores(
    grouped, key_heads, document_segment, segment_block, place_block, places, score_scale
):
    scores = (
        jnp.einsum("qkgd,skd->kgqs", grouped, key_heads, preferred_element_type=jnp.float32)
        * score_scale
    )
    allowed = (segment_block[:, None] == document_segment[None, :]) & (
        place_block[:, None] >= places[None, :]
    )
    return jnp.where(allowed[None, None, :, :], scores, MASKED)


def attend_forward(query_heads, key_heads, value_heads, document_segment):
    count_of_rows, head_count, head_width = query_heads.shape
    kv_count = key_heads.shape[1]
    group_size = head_count // kv_count
    block_rows = min(512, count_of_rows)
    block_count = count_of_rows // block_rows
    score_scale = head_width ** (-0.5)
    places = jnp.arange(count_of_rows, dtype=jnp.int32)

    def one_block(pieces):
        query_block, segment_block, place_block = pieces
        grouped = query_block.reshape(block_rows, kv_count, group_size, head_width)
        scores = masked_scores(
            grouped, key_heads, document_segment, segment_block, place_block, places, score_scale
        )
        row_top = jnp.max(scores, axis=-1, keepdims=True)
        exp_values = jnp.exp(scores - row_top)
        row_total = jnp.sum(exp_values, axis=-1, keepdims=True)
        weights = (exp_values / row_total).astype(jnp.bfloat16)
        output = jnp.einsum(
            "kgqs,skd->qkgd", weights, value_heads, preferred_element_type=jnp.float32
        )
        return (
            output.reshape(block_rows, head_count, head_width).astype(jnp.bfloat16),
            row_top[..., 0] + jnp.log(row_total[..., 0]),
        )

    outputs, log_sums = lax.map(
        one_block,
        (
            query_heads.reshape(block_count, block_rows, head_count, head_width),
            document_segment.reshape(block_count, block_rows),
            places.reshape(block_count, block_rows),
        ),
    )
    return (outputs.reshape(count_of_rows, head_count, head_width), log_sums)


def attend_backward(query_heads, key_heads, value_heads, grad_heads, document_segment):
    count_of_rows, head_count, head_width = query_heads.shape
    kv_count = key_heads.shape[1]
    group_size = head_count // kv_count
    block_rows = min(512, count_of_rows)
    block_count = count_of_rows // block_rows
    score_scale = head_width ** (-0.5)
    places = jnp.arange(count_of_rows, dtype=jnp.int32)

    def one_block(carried, pieces):
        key_grad, value_grad = carried
        query_block, grad_block, segment_block, place_block = pieces[:4]
        grouped = query_block.reshape(block_rows, kv_count, group_size, head_width)
        grad_grouped = grad_block.reshape(block_rows, kv_count, group_size, head_width)
        scores = masked_scores(
            grouped, key_heads, document_segment, segment_block, place_block, places, score_scale
        )
        row_top = jnp.max(scores, axis=-1, keepdims=True)
        exp_values = jnp.exp(scores - row_top)
        weights = exp_values / jnp.sum(exp_values, axis=-1, keepdims=True)
        rounded = weights.astype(jnp.bfloat16)
        grad_weights = jnp.einsum(
            "qkgd,skd->kgqs", grad_grouped, value_heads, preferred_element_type=jnp.float32
        )
        row_delta = jnp.sum(weights * grad_weights, axis=-1, keepdims=True)
        grad_scores = (weights * (grad_weights - row_delta)).astype(jnp.bfloat16)
        query_grad = (
            jnp.einsum("kgqs,skd->qkgd", grad_scores, key_heads, preferred_element_type=jnp.float32)
            * score_scale
        )
        key_grad = (
            key_grad
            + jnp.einsum("kgqs,qkgd->skd", grad_scores, grouped, preferred_element_type=jnp.float32)
            * score_scale
        )
        value_grad = value_grad + jnp.einsum(
            "kgqs,qkgd->skd", rounded, grad_grouped, preferred_element_type=jnp.float32
        )
        results = (query_grad.reshape(block_rows, head_count, head_width).astype(jnp.bfloat16),)
        output = jnp.einsum(
            "kgqs,skd->qkgd", rounded, value_heads, preferred_element_type=jnp.float32
        )
        results = results + (
            output.reshape(block_rows, head_count, head_width).astype(jnp.bfloat16),
        )
        return ((key_grad, value_grad), results)

    inputs = (
        query_heads.reshape(block_count, block_rows, head_count, head_width),
        grad_heads.reshape(block_count, block_rows, head_count, head_width),
        document_segment.reshape(block_count, block_rows),
        places.reshape(block_count, block_rows),
    )
    zeros_start = jnp.zeros((count_of_rows, kv_count, head_width), jnp.float32)
    (key_grad, value_grad), results = lax.scan(one_block, (zeros_start, zeros_start), inputs)
    query_grad = results[0].reshape(count_of_rows, head_count, head_width)
    parts = (query_grad, key_grad.astype(jnp.bfloat16), value_grad.astype(jnp.bfloat16))
    parts = parts + (results[1].reshape(count_of_rows, head_count, head_width),)
    return parts


def on_device(
    tokens,
    lengths,
    packing,
    norm_in,
    w_query,
    key_projection,
    value_projection,
    norm_query,
    norm_key,
    w_out,
    norm_post,
    w_gate,
    w_up,
    w_down,
    cotangent,
):
    seq_count = lax.axis_size("seq")
    seq_place = lax.axis_index("seq")
    resident_rows = tokens.shape[1]
    row_length = resident_rows * seq_count
    order_row = packing[0]
    sources = order_row // resident_rows
    all_places = jnp.arange(row_length, dtype=jnp.int32)
    mine_first = jnp.argsort(
        jnp.where(sources == seq_place, all_places, all_places + row_length), stable=True
    )[:resident_rows]
    sent_rows = jnp.take(order_row, mine_first) - seq_place * resident_rows
    received_tokens, received_grad = (
        lax.all_to_all(
            jnp.take(tokens[0], sent_rows, axis=0), "seq", split_axis=0, concat_axis=0, tiled=True
        ),
        lax.all_to_all(
            jnp.take(cotangent[0], sent_rows, axis=0),
            "seq",
            split_axis=0,
            concat_axis=0,
            tiled=True,
        ),
    )
    my_sources = lax.dynamic_slice_in_dim(sources, seq_place * resident_rows, resident_rows)
    by_source = jnp.argsort(
        my_sources * row_length + jnp.arange(resident_rows, dtype=jnp.int32), stable=True
    )
    arrival = jnp.argsort(by_source, stable=True)
    inputs = jnp.take(received_tokens, arrival, axis=0).astype(jnp.float32)
    out_grad = jnp.take(received_grad, arrival, axis=0).astype(jnp.float32)
    (
        gain_in,
        query_weight,
        key_matrix,
        value_matrix,
        gain_query,
        gain_key,
        out_weight,
        gain_post,
        gate_weight,
        up_weight,
        down_weight,
    ) = (
        lax.all_gather(norm_in, "fsdp", axis=0, tiled=True),
        lax.all_gather(w_query, "fsdp", axis=0, tiled=True),
        lax.all_gather(key_projection, "fsdp", axis=0, tiled=True),
        lax.all_gather(value_projection, "fsdp", axis=0, tiled=True),
        lax.all_gather(norm_query, "fsdp", axis=0, tiled=True),
        lax.all_gather(norm_key, "fsdp", axis=0, tiled=True),
        lax.all_gather(w_out, "fsdp", axis=0, tiled=True),
        lax.all_gather(norm_post, "fsdp", axis=0, tiled=True),
        lax.all_gather(w_gate, "fsdp", axis=0, tiled=True),
        lax.all_gather(w_up, "fsdp", axis=0, tiled=True),
        lax.all_gather(w_down, "fsdp", axis=0, tiled=True),
    )
    gain_in = gain_in.astype(jnp.float32)
    gain_query = gain_query.astype(jnp.float32)
    gain_key = gain_key.astype(jnp.float32)
    gain_post = gain_post.astype(jnp.float32)
    document_segment, start_offset = row_lookup_tables(lengths[0], row_length)
    my_offset = lax.dynamic_slice_in_dim(start_offset, seq_place * resident_rows, resident_rows)

    def project(normalized_rows):
        query_pre = matrix_product(normalized_rows, query_weight).reshape(
            resident_rows, HQ, HEAD_SIZE
        )
        key_before_norm = matrix_product(normalized_rows, key_matrix).reshape(
            resident_rows, KEY_VALUE_HEADS, HEAD_SIZE
        )
        row_values = (
            matrix_product(normalized_rows, value_matrix)
            .reshape(resident_rows, KEY_VALUE_HEADS, HEAD_SIZE)
            .astype(jnp.bfloat16)
        )
        query_rows = head_front(query_pre, gain_query, my_offset).astype(jnp.bfloat16)
        key_rows = head_front(key_before_norm, gain_key, my_offset).astype(jnp.bfloat16)
        return (query_pre, key_before_norm, query_rows, key_rows, row_values)

    normalized = rms_scale(inputs, gain_in).astype(jnp.bfloat16)
    query_pre, key_before_norm, query_rows, key_rows, row_values = project(normalized)
    query_heads, key_heads, value_heads = (
        lax.all_to_all(query_rows, "seq", split_axis=1, concat_axis=0, tiled=True),
        lax.all_to_all(key_rows, "seq", split_axis=1, concat_axis=0, tiled=True),
        lax.all_to_all(row_values, "seq", split_axis=1, concat_axis=0, tiled=True),
    )
    attended, log_sums = attend_forward(query_heads, key_heads, value_heads, document_segment)
    attended_rows = lax.all_to_all(
        attended, "seq", split_axis=0, concat_axis=1, tiled=True
    ).reshape(resident_rows, HQ * HEAD_SIZE)
    middle = inputs + matrix_product(attended_rows, out_weight)
    normed_post = rms_scale(middle, gain_post).astype(jnp.bfloat16)
    gate_sum = matrix_product(normed_post, gate_weight)
    up_sum = matrix_product(normed_post, up_weight)
    hidden = (gate_sum / (1.0 + jnp.exp(-gate_sum)) * up_sum).astype(jnp.bfloat16)
    result = middle + matrix_product(hidden, down_weight)
    grad_mlp = out_grad.astype(jnp.bfloat16)
    grad_down = outer_sum(hidden, grad_mlp)
    grad_hidden = back_matmul(grad_mlp, down_weight)
    logistic = 1.0 / (1.0 + jnp.exp(-gate_sum))
    grad_gate = (grad_hidden * up_sum * (logistic + gate_sum * logistic * (1.0 - logistic))).astype(
        jnp.bfloat16
    )
    grad_up = (grad_hidden * gate_sum * logistic).astype(jnp.bfloat16)
    grad_gate_weight = outer_sum(normed_post, grad_gate)
    grad_up_weight = outer_sum(normed_post, grad_up)
    grad_normed_post = back_matmul(grad_gate, gate_weight) + back_matmul(grad_up, up_weight)
    post_pull = jax.vjp(rms_scale, middle, gain_post)[1]
    grad_middle_norm, grad_gain_post = post_pull(grad_normed_post)
    grad_middle = out_grad + grad_middle_norm
    grad_branch = grad_middle.astype(jnp.bfloat16)
    grad_attended = (
        back_matmul(grad_branch, out_weight)
        .astype(jnp.bfloat16)
        .reshape(resident_rows, HQ, HEAD_SIZE)
    )
    query_pre, key_before_norm, query_rows, key_rows, row_values = project(normalized)
    query_heads, key_heads, value_heads, grad_heads = (
        lax.all_to_all(query_rows, "seq", split_axis=1, concat_axis=0, tiled=True),
        lax.all_to_all(key_rows, "seq", split_axis=1, concat_axis=0, tiled=True),
        lax.all_to_all(row_values, "seq", split_axis=1, concat_axis=0, tiled=True),
        lax.all_to_all(grad_attended, "seq", split_axis=1, concat_axis=0, tiled=True),
    )
    query_grad, key_grad, value_grad, attended = attend_backward(
        query_heads, key_heads, value_heads, grad_heads, document_segment
    )
    query_back, key_back, value_backward, attended_again = (
        lax.all_to_all(query_grad, "seq", split_axis=0, concat_axis=1, tiled=True),
        lax.all_to_all(key_grad, "seq", split_axis=0, concat_axis=1, tiled=True),
        lax.all_to_all(value_grad, "seq", split_axis=0, concat_axis=1, tiled=True),
        lax.all_to_all(attended, "seq", split_axis=0, concat_axis=1, tiled=True),
    )
    attended_rows = attended_again.reshape(resident_rows, HQ * HEAD_SIZE)
    grad_out_weight = outer_sum(attended_rows, grad_branch)

    def front_query(pre_values, gain_values):
        return head_front(pre_values, gain_values, my_offset)

    query_pull = jax.vjp(front_query, query_pre, gain_query)[1]
    grad_query_pre, grad_gain_query = query_pull(query_back.astype(jnp.float32))
    key_pull = jax.vjp(front_query, key_before_norm, gain_key)[1]
    gradient_key_before, grad_gain_key = key_pull(key_back.astype(jnp.float32))
    grad_query_pre = grad_query_pre.astype(jnp.bfloat16).reshape(resident_rows, HQ * HEAD_SIZE)
    gradient_key_before = gradient_key_before.astype(jnp.bfloat16).reshape(
        resident_rows, KEY_VALUE_HEADS * HEAD_SIZE
    )
    value_backward = value_backward.reshape(resident_rows, KEY_VALUE_HEADS * HEAD_SIZE)
    grad_query_weight = outer_sum(normalized, grad_query_pre)
    grad_key_weight = outer_sum(normalized, gradient_key_before)
    grad_value_weight = outer_sum(normalized, value_backward)
    grad_normed = (
        back_matmul(grad_query_pre, query_weight)
        + back_matmul(gradient_key_before, key_matrix)
        + back_matmul(value_backward, value_matrix)
    )
    in_pull = jax.vjp(rms_scale, inputs, gain_in)[1]
    grad_inputs_norm, grad_gain_in = in_pull(grad_normed)
    grad_inputs = grad_middle + grad_inputs_norm
    back_result, back_input_grad = (
        lax.all_to_all(
            jnp.take(result.astype(jnp.bfloat16), by_source, axis=0),
            "seq",
            split_axis=0,
            concat_axis=0,
            tiled=True,
        ),
        lax.all_to_all(
            jnp.take(grad_inputs.astype(jnp.bfloat16), by_source, axis=0),
            "seq",
            split_axis=0,
            concat_axis=0,
            tiled=True,
        ),
    )
    homeward = jnp.argsort(sent_rows, stable=True)
    output = jnp.take(back_result, homeward, axis=0)[None]
    input_grad = jnp.take(back_input_grad, homeward, axis=0)[None]
    (
        share_in,
        share_query,
        share_key,
        share_value,
        share_gquery,
        share_gkey,
        share_out,
        share_post,
        share_gate,
        share_up,
        share_down,
    ) = (
        lax.psum_scatter(
            grad_gain_in.astype(jnp.bfloat16), "fsdp", scatter_dimension=0, tiled=True
        ).astype(jnp.float32),
        lax.psum_scatter(
            grad_query_weight.astype(jnp.bfloat16), "fsdp", scatter_dimension=0, tiled=True
        ).astype(jnp.float32),
        lax.psum_scatter(
            grad_key_weight.astype(jnp.bfloat16), "fsdp", scatter_dimension=0, tiled=True
        ).astype(jnp.float32),
        lax.psum_scatter(
            grad_value_weight.astype(jnp.bfloat16), "fsdp", scatter_dimension=0, tiled=True
        ).astype(jnp.float32),
        lax.psum_scatter(
            grad_gain_query.astype(jnp.bfloat16), "fsdp", scatter_dimension=0, tiled=True
        ).astype(jnp.float32),
        lax.psum_scatter(
            grad_gain_key.astype(jnp.bfloat16), "fsdp", scatter_dimension=0, tiled=True
        ).astype(jnp.float32),
        lax.psum_scatter(
            grad_out_weight.astype(jnp.bfloat16), "fsdp", scatter_dimension=0, tiled=True
        ).astype(jnp.float32),
        lax.psum_scatter(
            grad_gain_post.astype(jnp.bfloat16), "fsdp", scatter_dimension=0, tiled=True
        ).astype(jnp.float32),
        lax.psum_scatter(
            grad_gate_weight.astype(jnp.bfloat16), "fsdp", scatter_dimension=0, tiled=True
        ).astype(jnp.float32),
        lax.psum_scatter(
            grad_up_weight.astype(jnp.bfloat16), "fsdp", scatter_dimension=0, tiled=True
        ).astype(jnp.float32),
        lax.psum_scatter(
            grad_down.astype(jnp.bfloat16), "fsdp", scatter_dimension=0, tiled=True
        ).astype(jnp.float32),
    )
    (
        final_in,
        final_query,
        final_key,
        final_value,
        final_gquery,
        final_gkey,
        final_out,
        final_post,
        final_gate,
        final_up,
        final_down,
    ) = (
        lax.psum(share_in.astype(jnp.bfloat16), "seq").astype(jnp.float32),
        lax.psum(share_query.astype(jnp.bfloat16), "seq").astype(jnp.float32),
        lax.psum(share_key.astype(jnp.bfloat16), "seq").astype(jnp.float32),
        lax.psum(share_value.astype(jnp.bfloat16), "seq").astype(jnp.float32),
        lax.psum(share_gquery.astype(jnp.bfloat16), "seq").astype(jnp.float32),
        lax.psum(share_gkey.astype(jnp.bfloat16), "seq").astype(jnp.float32),
        lax.psum(share_out.astype(jnp.bfloat16), "seq").astype(jnp.float32),
        lax.psum(share_post.astype(jnp.bfloat16), "seq").astype(jnp.float32),
        lax.psum(share_gate.astype(jnp.bfloat16), "seq").astype(jnp.float32),
        lax.psum(share_up.astype(jnp.bfloat16), "seq").astype(jnp.float32),
        lax.psum(share_down.astype(jnp.bfloat16), "seq").astype(jnp.float32),
    )
    return (
        output,
        input_grad,
        final_in,
        final_query,
        final_key,
        final_value,
        final_gquery,
        final_gkey,
        final_out,
        final_post,
        final_gate,
        final_up,
        final_down,
    )


def solution(mesh):
    in_specs = (
        P("fsdp", "seq", None),
        P("fsdp", None),
        P("fsdp", None),
        P("fsdp"),
        P("fsdp", None),
        P("fsdp", None),
        P("fsdp", None),
        P("fsdp"),
        P("fsdp"),
        P("fsdp", None),
        P("fsdp"),
        P("fsdp", None),
        P("fsdp", None),
        P("fsdp", None),
        P("fsdp", "seq", None),
    )
    out_specs = (
        P("fsdp", "seq", None),
        P("fsdp", "seq", None),
        P("fsdp"),
        P("fsdp", None),
        P("fsdp", None),
        P("fsdp", None),
        P("fsdp"),
        P("fsdp"),
        P("fsdp", None),
        P("fsdp"),
        P("fsdp", None),
        P("fsdp", None),
        P("fsdp", None),
    )
    return jax.shard_map(
        on_device, mesh=mesh, in_specs=in_specs, out_specs=out_specs, check_vma=False
    )
```

profile of v0, /device:TPU:0, one launch (start us, length us, event | category | flops | bytes accessed | tf_op | source)
XLA Modules:
  0.0 980.0 jit_solution(8319103294171731283)
XLA Ops:
  11.2 4.4 sort.62
  21.1 5.2 all-to-all-start
  35.9 16.4 %all-reduce.11 = (bf16[128]{0:T(256)(128)(2,1)S(1)}, bf16[128]{0:T(256)(128)(2,1)S(1)}) all-reduce(bf16[128]{0:T(256)(128)(2,1)S(1)} %dynamic-update-slice, bf16[128]{0:T(256)(128)(2,1)S(1)} %dynamic-update-slice.1), channel_id=1, replica_groups=mesh['seq'=4,'fsdp'=8] {'fsdp'}, use_global_device_ids=true, to_apply=%add.4 | all-reduce | flops 256 | bytes 1024
  53.3 8.7 all-gather
  78.8 40.9 %all-gather.10.cloned.1.call-done = bf16[1024,2048]{1,0:T(8,128)(2,1)} async-done(((bf16[128,2048]{1,0:T(8,128)(2,1)}), bf16[1024,2048]{1,0:T(8,128)(2,1)}) %all-gather.10.cloned.1.call-update) | async-done | bytes 4194320 | tf_op jit(solution)/shard_map/all_gather | solution.py:240
  127.4 3.9 all-to-all-start.2
  135.8 3.9 all-to-all-done.2
  144.9 11.6 %all-to-all-done.1 = bf16[256,16,128]{2,0,1:T(8,128)(2,1)S(1)} async-done(((bf16[256,16,128]{2,0,1:T(8,128)(2,1)}), bf16[256,16,128]{2,0,1:T(8,128)(2,1)S(1)}, u32[]{:S(2)}, u32[]{:S(2)}) %all-to-all-start.1) | async-done | bytes 1048608 | tf_op jit(solution)/shard_map/all_to_all | solution.py:277
  161.3 27.9 %while.28 = (s32[]{:T(128)}, bf16[2,512,4,128]{3,1,0,2:T(8,128)(2,1)}, s32[2,512]{1,0:T(2,128)S(1)}, s32[1024]{0:T(1024)S(1)}, s32[2,512]{1,0:T(2,128)S(1)}, /*i...) while((s32[]{:T(128)}, ...), condition=%wide.region_12.14_spmd.clone, body=%wide.region_9.13_spmd.clone.sunk | while | flops 1088160768 | bytes 30441640 | solution.py:107
  162.0 7.3 fusion.194
  169.3 4.8 fusion.195
  175.9 7.4 fusion.194
  183.2 4.9 fusion.195
  192.3 4.3 all-to-all-start.4
  196.5 10.4 %all-gather.1 = bf16[8,1,128]{2,1,0:T(2,128)(2,1)S(1)} all-gather(bf16[1,1,128]{2,1,0:T(2,128)(2,1)S(1)} %bitcast.386), channel_id=1, replica_groups=mesh['seq'=4,'fsdp'=8] {'fsdp'}, dimensions={0}, use_global_device_ids=true | all-gather | bytes 2304 | tf_op jit(solution)/shard_map/all_gather | solution.py:246
  214.8 3.9 multiply_reduce_fusion.6
  219.9 11.9 %all-gather.20.cloned.1.call-done = bf16[1024,3072]{1,0:T(8,128)(2,1)} async-done(((bf16[128,3072]{1,0:T(8,128)(2,1)}), bf16[1024,3072]{1,0:T(8,128)(2,1)}) %all-gather.20.cloned.1.call-update) | async-done | bytes 6291472 | tf_op jit(solution)/shard_map/all_gather | solution.py:248
  231.8 6.2 fusion.118
  238.1 58.6 %all-gather.18.cloned.1.call-done = bf16[1024,3072]{1,0:T(8,128)(2,1)} async-done(((bf16[128,3072]{1,0:T(8,128)(2,1)}), bf16[1024,3072]{1,0:T(8,128)(2,1)}) %all-gather.18.cloned.1.call-update) | async-done | bytes 6291472 | tf_op jit(solution)/shard_map/all_gather | solution.py:247
  296.7 6.2 fusion.117
  302.9 58.8 %all-gather.22.cloned.1.call-done = bf16[3072,1024]{1,0:T(8,128)(2,1)} async-done(((bf16[384,1024]{1,0:T(8,128)(2,1)}), bf16[3072,1024]{1,0:T(8,128)(2,1)}) %all-gather.22.cloned.1.call-update) | async-done | bytes 6291472 | tf_op jit(solution)/shard_map/all_gather | solution.py:249
  361.7 9.7 multiply_convert_fusion
  373.4 5.8 multiply_reduce_fusion.2
  382.3 4.3 all-to-all-start.7
  386.8 14.1 %all-to-all-done.7 = bf16[256,16,128]{2,0,1:T(8,128)(2,1)} async-done(((bf16[256,16,128]{2,0,1:T(8,128)(2,1)}), bf16[256,16,128]{2,0,1:T(8,128)(2,1)}, u32[]{:S(2)}, u32[]{:S(2)}) %all-to-all-start.7) | async-done | bytes 1048608 | tf_op jit(solution)/shard_map/all_to_all | solution.py:316
  405.5 50.3 %while.29 = (s32[]{:T(128)}, f32[1024,2,128]{0,2,1:T(8,128)S(1)}, f32[1024,2,128]{0,2,1:T(8,128)}, bf16[2,512,4,128]{3,1,0,2:T(8,128)(2,1)}, bf16[2,512,4,128]{3...) while((s32[]{:T(128)}, f32[1024,2,128]{0,2,1:T(8,128)S(1)}, ...), condition=%wide.region_20.22_spmd.clone, body=%wide.region_16.21_spmd.clone.sunk | while | flops 3256351744 | bytes 151069152 | solution.py:172
  408.0 7.3 fusion.208
  415.3 4.9 fusion.213
  433.2 7.3 fusion.208
  440.5 4.9 fusion.213
  457.4 10.7 %all_to_all.192 = bf16[1024,2,128]{2,1,0:T(2,128)(2,1)S(1)} all-to-all(bf16[1024,2,128]{2,1,0:T(2,128)(2,1)S(1)} %copy.330), channel_id=1, replica_groups=mesh['seq'=4,'fsdp'=8] {'seq'}, dimensions={0} | all-to-all | bytes 1048576 | tf_op jit(solution)/shard_map/all_to_all | solution.py:324
  471.5 10.4 %all_to_all.193 = bf16[1024,2,128]{2,1,0:T(2,128)(2,1)} all-to-all(bf16[1024,2,128]{2,1,0:T(2,128)(2,1)S(1)} %copy.326), channel_id=1, replica_groups=mesh['seq'=4,'fsdp'=8] {'seq'}, dimensions={0} | all-to-all | bytes 1048576 | tf_op jit(solution)/shard_map/all_to_all | solution.py:323
  488.2 14.3 %all_to_all.194 = bf16[1024,4,128]{2,1,0:T(4,128)(2,1)S(1)} all-to-all(bf16[1024,4,128]{2,1,0:T(4,128)(2,1)S(1)} %copy.334), channel_id=1, replica_groups=mesh['seq'=4,'fsdp'=8] {'seq'}, dimensions={0} | all-to-all | bytes 2097152 | tf_op jit(solution)/shard_map/all_to_all | solution.py:325
  510.4 13.1 %all_to_all.195 = bf16[1024,4,128]{2,1,0:T(4,128)(2,1)S(1)} all-to-all(bf16[1024,4,128]{2,1,0:T(4,128)(2,1)S(1)} %copy.320), channel_id=1, replica_groups=mesh['seq'=4,'fsdp'=8] {'seq'}, dimensions={0} | all-to-all | bytes 2097152 | tf_op jit(solution)/shard_map/all_to_all | solution.py:322
  537.8 6.0 convolution_convert_fusion
  544.9 5.9 convolution_convert_fusion.1
  550.8 6.0 convolution_convert_fusion.2
  557.4 34.4 %reduce-scatter.14.cloned.1.call-done = bf16[256,1024]{1,0:T(8,128)(2,1)} async-done(((bf16[2048,1024]{1,0:T(8,128)(2,1)}), bf16[256,1024]{1,0:T(8,128)(2,1)}) %reduce-scatter.14.cloned.1.call-update) | async-done | bytes 524304 | tf_op jit(solution)/shard_map/reduce_scatter | solution.py:403
  591.8 50.7 %reduce-scatter.8.cloned.1.call-done = bf16[128,2048]{1,0:T(8,128)(2,1)} async-done(((bf16[1024,2048]{1,0:T(8,128)(2,1)}), bf16[128,2048]{1,0:T(8,128)(2,1)}) %reduce-scatter.8.cloned.1.call-update) | async-done | bytes 524304 | tf_op jit(solution)/shard_map/reduce_scatter | solution.py:388
  642.5 70.4 %reduce-scatter.20.cloned.1.call-done = bf16[384,1024]{1,0:T(8,128)(2,1)} async-done(((bf16[3072,1024]{1,0:T(8,128)(2,1)}), bf16[384,1024]{1,0:T(8,128)(2,1)}) %reduce-scatter.20.cloned.1.call-update) | async-done | bytes 786448 | tf_op jit(solution)/shard_map/reduce_scatter | solution.py:415
  712.9 70.5 %reduce-scatter.18.cloned.1.call-done = bf16[128,3072]{1,0:T(8,128)(2,1)} async-done(((bf16[1024,3072]{1,0:T(8,128)(2,1)}), bf16[128,3072]{1,0:T(8,128)(2,1)}) %reduce-scatter.18.cloned.1.call-update) | async-done | bytes 786448 | tf_op jit(solution)/shard_map/reduce_scatter | solution.py:412
  783.4 70.4 %reduce-scatter.16.cloned.1.call-done = bf16[128,3072]{1,0:T(8,128)(2,1)} async-done(((bf16[1024,3072]{1,0:T(8,128)(2,1)}), bf16[128,3072]{1,0:T(8,128)(2,1)}) %reduce-scatter.16.cloned.1.call-update) | async-done | bytes 786448 | tf_op jit(solution)/shard_map/reduce_scatter | solution.py:409
  853.9 5.1 fusion.76
  860.9 4.7 fusion.120
  878.2 10.4 %all-to-all-done.5 = bf16[4,64,1024]{2,1,0:T(8,128)(2,1)S(1)} async-done(((bf16[4,64,1024]{2,1,0:T(8,128)(2,1)}), bf16[4,64,1024]{2,1,0:T(8,128)(2,1)S(1)}, u32[]{:S(2)}, u32[]{:S(2)}) %all-to-all-start.5) | async-done | bytes 524320 | tf_op jit(solution)/shard_map/all_to_all | solution.py:354
  893.5 13.9 %all-reduce.10 = (bf16[1024]{0:T(1024)(128)(2,1)S(1)}, bf16[128]{0:T(256)(128)(2,1)S(1)}, bf16[128]{0:T(256)(128)(2,1)S(1)}, bf16[1024]{0:T(1024)(128)(2,1)S(1)}) all-reduce(bf16[1024]{0:T(1024)(128)(2,1)S(1)} %get-tuple-element.389, bf16[128]{0:T(256)(128)(2,1)S(1)} %get-tuple-element.383, ...), channel_id=2, replica_groups=mesh['seq'=4,'fsdp'=8] {'fsdp'}, use_global_device_ids=true, to_apply=%region_25.27.clone | all-reduce | flops 2304 | bytes 9216
  907.7 10.3 %all-reduce.12 = (bf16[128]{0:T(256)(128)(2,1)S(1)}, bf16[16]{0:T(256)(128)(2,1)S(1)}, bf16[16]{0:T(256)(128)(2,1)S(1)}, bf16[128]{0:T(256)(128)(2,1)S(1)}) all-reduce(bf16[128]{0:T(256)(128)(2,1)S(1)} %dynamic-slice.3, bf16[16]{0:T(256)(128)(2,1)S(1)} %dynamic-slice.5, ...), channel_id=1, replica_groups=mesh['seq'=4,'fsdp'=8] {'seq'}, use_global_device_ids=true, to_apply=%region_26.28 | all-reduce | flops 288 | bytes 1152 | tf_op jit(solution)/shard_map/psum | solution.py:432
  923.6 38.6 %all-reduce.16.cloned.1.call-done = (bf16[128,2048]{1,0:T(8,128)(2,1)}, bf16[128,1024]{1,0:T(8,128)(2,1)}, bf16[128,1024]{1,0:T(8,128)(2,1)}, bf16[256,1024]{1,0...) async-done(((bf16[128,2048]{1,0:T(8,128)(2,1)}, bf16[128,1024]{1,0:T(8,128)(2,1)}, bf16[128,1024]{1,0:T(8,128)(2,1)}, ...) | async-done | bytes 3932176 | tf_op jit(solution)/shard_map/psum | solution.py:433
  (414 shorter events, 178.2 us)
Async XLA Ops:
  7.2 57.1 %all-gather.14.cloned.1.call-start = ((), (), s32[]{:S(2)}) async-start(), calls=%async_computation.22 | async-start | bytes 2359296 | tf_op jit(solution)/shard_map/all_gather | solution.py:242
  7.9 63.8 %all-gather.12.cloned.1.call-start = ((), (), s32[]{:S(2)}) async-start(), calls=%async_computation.21 | async-start | bytes 2359296 | tf_op jit(solution)/shard_map/all_gather | solution.py:241
  8.7 110.9 %all-gather.10.cloned.1.call-start = ((), (), s32[]{:S(2)}) async-start(), calls=%async_computation.20 | async-start | bytes 4718592 | tf_op jit(solution)/shard_map/all_gather | solution.py:240
  9.4 205.4 %all-gather.16.cloned.1.call-start = ((), (), s32[]{:S(2)}) async-start(), calls=%async_computation.23 | async-start | bytes 4718592 | tf_op jit(solution)/shard_map/all_gather | solution.py:245
  10.0 221.8 %all-gather.20.cloned.1.call-start = ((), (), s32[]{:S(2)}) async-start(), calls=%async_computation.25 | async-start | bytes 7077888 | tf_op jit(solution)/shard_map/all_gather | solution.py:248
  10.6 286.1 %all-gather.18.cloned.1.call-start = ((), (), s32[]{:S(2)}) async-start(), calls=%async_computation.24 | async-start | bytes 7077888 | tf_op jit(solution)/shard_map/all_gather | solution.py:247
  19.9 14.2 %copy-start.78 = (u32[32]{0:T(128)S(1)}, u32[32]{0:T(128)}, u32[]{:S(2)}) copy-start(u32[32]{0:T(128)} %constant.145) | copy-start | bytes 388
  19.9 15.5 %copy-start.86 = (bf16[16]{0:T(256)(128)(2,1)S(1)}, bf16[16]{0:T(256)(128)(2,1)}, u32[]{:S(2)}) copy-start(bf16[16]{0:T(256)(128)(2,1)} %param.28) | copy-start | bytes 100
  19.9 15.7 %copy-start.87 = (bf16[16]{0:T(256)(128)(2,1)S(1)}, bf16[16]{0:T(256)(128)(2,1)}, u32[]{:S(2)}) copy-start(bf16[16]{0:T(256)(128)(2,1)} %param.29) | copy-start | bytes 100
  19.9 33.4 %copy-start.81 = (bf16[128]{0:T(256)(128)(2,1)S(1)}, bf16[128]{0:T(256)(128)(2,1)}, u32[]{:S(2)}) copy-start(bf16[128]{0:T(256)(128)(2,1)} %param.24) | copy-start | bytes 772
  21.1 41.2 %all-to-all-start = ((bf16[4,64,1024]{2,1,0:T(8,128)(2,1)}), bf16[4,64,1024]{2,1,0:T(8,128)(2,1)S(1)}, u32[]{:S(2)}, u32[]{:S(2)}) async-start(bf16[4,64,1024]{2,1,0:T(8,128)(2,1)} %bitcast.2), calls=%async_computation | async-start | bytes 1048576 | tf_op jit(solution)/shard_map/all_to_all | solution.py:208
  26.2 335.4 %all-gather.22.cloned.1.call-start = ((), (), s32[]{:S(2)}) async-start(), calls=%async_computation.26 | async-start | bytes 7077888 | tf_op jit(solution)/shard_map/all_gather | solution.py:249
  34.0 43.5 %copy-start.45 = (f32[256,64]{0,1:T(8,128)}, f32[256,64]{0,1:T(8,128)S(1)}, u32[]{:S(2)}) copy-start(f32[256,64]{0,1:T(8,128)S(1)} %get-tuple-element.475) | copy-start | bytes 196612
  34.1 43.5 %copy-start.47 = (f32[256,64]{0,1:T(8,128)}, f32[256,64]{0,1:T(8,128)S(1)}, u32[]{:S(2)}) copy-start(f32[256,64]{0,1:T(8,128)S(1)} %get-tuple-element.476) | copy-start | bytes 196612
  62.0 57.7 %copy-start.55 = (f32[8,1,128]{2,1,0:T(1,128)}, f32[8,1,128]{2,1,0:T(1,128)S(1)}, u32[]{:S(2)}) copy-start(f32[8,1,128]{2,1,0:T(1,128)S(1)} %convert_element_type.308) | copy-start | bytes 12292
  62.1 69.2 %copy-start.39 = (f32[256,64]{1,0:T(8,128)}, f32[256,64]{1,0:T(8,128)S(1)}, u32[]{:S(2)}) copy-start(f32[256,64]{1,0:T(8,128)S(1)} %copy.301) | copy-start | bytes 196612
  62.2 69.1 %copy-start.41 = (f32[256,64]{1,0:T(8,128)}, f32[256,64]{1,0:T(8,128)S(1)}, u32[]{:S(2)}) copy-start(f32[256,64]{1,0:T(8,128)S(1)} %copy.302) | copy-start | bytes 196612
  62.2 317.0 %copy-start.66 = (pred[256]{0:T(512)(128)(4,1)}, pred[256]{0:T(512)(128)(4,1)S(1)}, u32[]{:S(2)}) copy-start(pred[256]{0:T(512)(128)(4,1)S(1)} %compare_and_fusion.2) | copy-start | bytes 772
  63.4 151.4 %copy-start.7 = (bf16[256,1024]{1,0:T(8,128)(2,1)}, bf16[256,1024]{1,0:T(8,128)(2,1)S(1)}, u32[]{:S(2)}) copy-start(bf16[256,1024]{1,0:T(8,128)(2,1)S(1)} %gather_fusion.2) | copy-start | bytes 1572868
  64.3 55.4 %copy-start.64 = (f32[256]{0:T(256)}, f32[256]{0:T(256)S(1)}, u32[]{:S(2)}) copy-start(f32[256]{0:T(256)S(1)} %fusion.95) | copy-start | bytes 3076
  67.6 59.8 %all-to-all-start.3 = ((bf16[256,8,128]{2,0,1:T(8,128)(2,1)}), bf16[256,8,128]{2,0,1:T(8,128)(2,1)S(1)}, u32[]{:S(2)}, u32[]{:S(2)}) async-start(bf16[256,8,128]{2,0,1:T(8,128)(2,1)} %bitcast.262), calls=%async_computation.3 | async-start | bytes 1048576 | tf_op jit(solution)/shard_map/all_to_all | solution.py:279
  127.4 12.3 %all-to-all-start.2 = ((bf16[256,8,128]{2,0,1:T(8,128)(2,1)}), bf16[256,8,128]{2,0,1:T(8,128)(2,1)S(1)}, u32[]{:S(2)}, u32[]{:S(2)}) async-start(bf16[256,8,128]{2,0,1:T(8,128)(2,1)} %copy.306), calls=%async_computation.2 | async-start | bytes 1048576 | tf_op jit(solution)/shard_map/all_to_all | solution.py:278
  139.7 16.8 %all-to-all-start.1 = ((bf16[256,16,128]{2,0,1:T(8,128)(2,1)}), bf16[256,16,128]{2,0,1:T(8,128)(2,1)S(1)}, u32[]{:S(2)}, u32[]{:S(2)}) async-start(bf16[256,16,128]{2,0,1:T(8,128)(2,1)} %pad_maximum_fusion), calls=%async_computation.1 | async-start | bytes 2097152 | tf_op jit(solution)/shard_map/all_to_all | solution.py:277
  156.6 35.7 %all-to-all-start.6 = ((bf16[4,64,1024]{2,1,0:T(8,128)(2,1)}), bf16[4,64,1024]{2,1,0:T(8,128)(2,1)S(1)}, u32[]{:S(2)}, u32[]{:S(2)}) async-start(bf16[4,64,1024]{2,1,0:T(8,128)(2,1)} %bitcast.29), calls=%async_computation.6 | async-start | bytes 1048576 | tf_op jit(solution)/shard_map/all_to_all | solution.py:211
  192.3 17.5 %all-to-all-start.4 = ((bf16[1024,4,128]{2,1,0:T(4,128)(2,1)}), bf16[1024,4,128]{2,1,0:T(4,128)(2,1)}, u32[]{:S(2)}, u32[]{:S(2)}) async-start(bf16[1024,4,128]{2,1,0:T(4,128)(2,1)} %copy.312), calls=%async_computation.4 | async-start | bytes 2097152 | tf_op jit(solution)/shard_map/all_to_all | solution.py:282
  208.3 171.0 %copy-start.16 = (bf16[256,1024]{1,0:T(8,128)(2,1)}, bf16[256,1024]{1,0:T(8,128)(2,1)S(1)}, u32[]{:S(2)}) copy-start(bf16[256,1024]{1,0:T(8,128)(2,1)S(1)} %gather_fusion.6) | copy-start | bytes 1572868
  219.9 76.8 %copy-start.14 = (bf16[256,1024]{1,0:T(8,128)(2,1)}, bf16[256,1024]{1,0:T(8,128)(2,1)S(1)}, u32[]{:S(2)}) copy-start(bf16[256,1024]{1,0:T(8,128)(2,1)S(1)} %multiply_convert_fusion.3) | copy-start | bytes 1572868
  382.3 18.6 %all-to-all-start.7 = ((bf16[256,16,128]{2,0,1:T(8,128)(2,1)}), bf16[256,16,128]{2,0,1:T(8,128)(2,1)}, u32[]{:S(2)}, u32[]{:S(2)}) async-start(bf16[256,16,128]{2,0,1:T(8,128)(2,1)} %bitcast.261), calls=%async_computation.7 | async-start | bytes 2097152 | tf_op jit(solution)/shard_map/all_to_all | solution.py:316
  386.5 170.9 %reduce-scatter.12.cloned.1.call-start = ((), (), s32[]{:S(2)}) async-start(), calls=%async_computation.29 | async-start | bytes 2359296 | tf_op jit(solution)/shard_map/reduce_scatter | solution.py:394
  455.8 12.7 %copy-start.8 = (bf16[256,1024]{1,0:T(8,128)(2,1)S(1)}, bf16[256,1024]{1,0:T(8,128)(2,1)}, u32[]{:S(2)}) copy-start(bf16[256,1024]{1,0:T(8,128)(2,1)} %copy-done.7) | copy-start | bytes 1572868
  455.8 12.7 %copy-start.56 = (f32[8,1,128]{2,1,0:T(1,128)S(1)}, f32[8,1,128]{2,1,0:T(1,128)}, u32[]{:S(2)}) copy-start(f32[8,1,128]{2,1,0:T(1,128)} %copy-done.55) | copy-start | bytes 12292
  455.8 12.7 %copy-start.65 = (f32[256]{0:T(256)S(1)}, f32[256]{0:T(256)}, u32[]{:S(2)}) copy-start(f32[256]{0:T(256)} %copy-done.64) | copy-start | bytes 3076
  455.8 12.7 %copy-start.67 = (pred[256]{0:T(512)(128)(4,1)S(1)}, pred[256]{0:T(512)(128)(4,1)}, u32[]{:S(2)}) copy-start(pred[256]{0:T(512)(128)(4,1)} %copy-done.66) | copy-start | bytes 772
  470.8 86.6 %reduce-scatter.10.cloned.1.call-start = ((), (), s32[]{:S(2)}) async-start(), calls=%async_computation.28 | async-start | bytes 2359296 | tf_op jit(solution)/shard_map/reduce_scatter | solution.py:391
  470.9 12.6 %copy-start.10 = (f32[256,8,128]{0,2,1:T(8,128)S(1)}, f32[256,8,128]{0,2,1:T(8,128)}, u32[]{:S(2)}) copy-start(f32[256,8,128]{0,2,1:T(8,128)} %copy-done.9) | copy-start | bytes 3145732
  470.9 12.6 %copy-start.61 = (f32[256,8]{0,1:T(8,128)S(1)}, f32[256,8]{0,1:T(8,128)}, u32[]{:S(2)}) copy-start(f32[256,8]{0,1:T(8,128)} %copy-done.60) | copy-start | bytes 24580
  470.9 12.6 %copy-start.73 = (f32[128]{0:T(128)S(1)}, f32[128]{0:T(128)}, u32[]{:S(2)}) copy-start(f32[128]{0:T(128)} %convert_element_type.255) | copy-start | bytes 1540
  487.3 104.5 %reduce-scatter.14.cloned.1.call-start = ((), (), s32[]{:S(2)}) async-start(), calls=%async_computation.30 | async-start | bytes 4718592 | tf_op jit(solution)/shard_map/reduce_scatter | solution.py:403
  488.2 16.9 %copy-start.13 = (f32[256,1024]{1,0:T(8,128)S(1)}, f32[256,1024]{1,0:T(8,128)}, u32[]{:S(2)}) copy-start(f32[256,1024]{1,0:T(8,128)} %copy-done.12) | copy-start | bytes 3145732
  508.4 134.2 %reduce-scatter.8.cloned.1.call-start = ((), (), s32[]{:S(2)}) async-start(), calls=%async_computation.27 | async-start | bytes 4718592 | tf_op jit(solution)/shard_map/reduce_scatter | solution.py:388
  536.8 176.1 %reduce-scatter.20.cloned.1.call-start = ((), (), s32[]{:S(2)}) async-start(), calls=%async_computation.33 | async-start | bytes 7077888 | tf_op jit(solution)/shard_map/reduce_scatter | solution.py:415
  543.9 239.6 %reduce-scatter.18.cloned.1.call-start = ((), (), s32[]{:S(2)}) async-start(), calls=%async_computation.32 | async-start | bytes 7077888 | tf_op jit(solution)/shard_map/reduce_scatter | solution.py:412
  550.8 303.0 %reduce-scatter.16.cloned.1.call-start = ((), (), s32[]{:S(2)}) async-start(), calls=%async_computation.31 | async-start | bytes 7077888 | tf_op jit(solution)/shard_map/reduce_scatter | solution.py:409
  556.8 297.1 %copy-start.30 = (f32[256,1024]{1,0:T(8,128)S(1)}, f32[256,1024]{1,0:T(8,128)}, u32[]{:S(2)}) copy-start(f32[256,1024]{1,0:T(8,128)} %copy-done.28) | copy-start | bytes 3145732
  556.8 405.4 %all-reduce.16.cloned.1.call-start = ((), (), s32[]{:S(2)}) async-start(), calls=%async_computation.34 | async-start | bytes 7864320 | tf_op jit(solution)/shard_map/psum | solution.py:433
  870.0 23.4 %copy-start.79 = (bf16[1024]{0:T(1024)(128)(2,1)S(1)}, bf16[1024]{0:T(1024)(128)(2,1)}, u32[]{:S(2)}) copy-start(bf16[1024]{0:T(1024)(128)(2,1)} %get-tuple-element.385) | copy-start | bytes 6148
  871.2 17.5 %all-to-all-start.5 = ((bf16[4,64,1024]{2,1,0:T(8,128)(2,1)}), bf16[4,64,1024]{2,1,0:T(8,128)(2,1)S(1)}, u32[]{:S(2)}, u32[]{:S(2)}) async-start(bf16[4,64,1024]{2,1,0:T(8,128)(2,1)} %bitcast.25), calls=%async_computation.5 | async-start | bytes 1048576 | tf_op jit(solution)/shard_map/all_to_all | solution.py:354
  888.7 32.6 %all-to-all-start.11 = ((bf16[4,64,1024]{2,1,0:T(8,128)(2,1)}), bf16[4,64,1024]{2,1,0:T(8,128)(2,1)S(1)}, u32[]{:S(2)}, u32[]{:S(2)}) async-start(bf16[4,64,1024]{2,1,0:T(8,128)(2,1)} %bitcast.47), calls=%async_computation.11 | async-start | bytes 1048576 | tf_op jit(solution)/shard_map/all_to_all | solution.py:361
  (76 other events, 249.8 us)
Sparse Core Ops, SparseCore 0:
  9.6 31.8 all-gather.13
  43.1 28.5 all-gather.11
  73.3 46.2 all-gather.9
  121.1 45.6 all-gather.15
  168.3 63.5 all-gather.19
  233.3 63.2 all-gather.17
  298.3 63.3 all-gather.21
  470.9 33.3 reduce-scatter.11
  506.6 34.5 reduce-scatter.9
  543.3 48.4 reduce-scatter.13
  594.1 48.3 reduce-scatter.7
  644.7 68.1 reduce-scatter.19
  715.2 68.1 reduce-scatter.17
  785.6 68.1 reduce-scatter.15
  857.6 104.5 all-reduce.15
where the time goes:
time: 990 us; the launch traced here: 980 us
  waiting for transfers between devices  552 us (56%)
  matrix products  144 us (15%)
  blocking collectives  108 us (11%)
  local copies, waits for them, and re-layouts  66.7 us (7%)
  other arithmetic  54.3 us (5%)
  starting transfers between devices  36.7 us (4%)
  between operations  17.6 us (2%)
    reduce_scatter x1, waiting for transfers between devices, on_device(): lax.psum_scatter(grad_up_weight.astype(jnp.bfloat16), 'fsdp', scatter_dim...  70.5 us
    reduce_scatter x1, waiting for transfers between devices, on_device(): lax.psum_scatter(grad_down.astype(jnp.bfloat16), 'fsdp', scatter_dimensio...  70.4 us
    reduce_scatter x1, waiting for transfers between devices, on_device(): lax.psum_scatter(grad_gate_weight.astype(jnp.bfloat16), 'fsdp', scatter_d...  70.4 us
    all_gather x1, waiting for transfers between devices, on_device(): lax.all_gather(w_down, 'fsdp', axis=0, tiled=True)  58.8 us
    all_gather x1, waiting for transfers between devices, on_device(): lax.all_gather(w_gate, 'fsdp', axis=0, tiled=True)  58.6 us
    reduce_scatter x1, waiting for transfers between devices, on_device(): lax.psum_scatter(grad_query_weight.astype(jnp.bfloat16), 'fsdp', scatter_...  50.7 us
    all_gather x1, waiting for transfers between devices, on_device(): lax.all_gather(w_query, 'fsdp', axis=0, tiled=True)  40.9 us
    psum x1, waiting for transfers between devices, on_device(): lax.psum(share_query.astype(jnp.bfloat16), 'seq').astype(jnp.float32)  38.6 us
  transfers between devices with their start and end apart: 24, of which 16 were waited for; matrix products, arithmetic and copies ran while one was open for 17% of the time, Pallas kernels for 0%

commit v1 on v0

v1 whole, which is shorter than its diff:
```python
import functools

import jax
import jax.numpy as jnp
from jax import lax
from jax.experimental import pallas as pl
from jax.experimental.pallas import tpu as pltpu
from jax.sharding import PartitionSpec as P

HQ = 16
KEY_VALUE_HEADS = 8
HEAD_SIZE = 128
GROUP = HQ // KEY_VALUE_HEADS

ROPE_BASE = 1000000.0
EPSILON = 1e-06
MASKED = -1e30
SCALE = HEAD_SIZE ** (-0.5)
MESH = pl.DeviceIdType.MESH
QUERY_BLOCK = 256
BF16 = jnp.bfloat16
F32 = jnp.float32


def matrix_product(left, right):
    return jnp.dot(left, right, preferred_element_type=F32)


def outer_sum(left, right):
    return lax.dot_general(left, right, (((0,), (0,)), ((), ())), preferred_element_type=F32)


def back_matmul(left, right):
    return lax.dot_general(left, right, (((1,), (1,)), ((), ())), preferred_element_type=F32)


def inverse_rms(values):
    return lax.rsqrt(jnp.mean(values * values, axis=-1, keepdims=True) + EPSILON)


def rms_backward(values, gain, grad):
    c = inverse_rms(values)
    scaled = grad * gain
    inner = jnp.mean(values * scaled, axis=-1, keepdims=True)
    return c * scaled - values * (c * c * c) * inner, grad * values * c


def greet(n):
    me = lax.axis_index("seq")
    barrier = pltpu.get_barrier_semaphore()
    for step in range(1, n):
        pl.semaphore_signal(
            barrier, inc=1, device_id={"seq": lax.rem(me + step, n)}, device_id_type=MESH
        )
    pl.semaphore_wait(barrier, n - 1)
    return me


def gather_kernel(n, x_ref, o_ref, send_sem, recv_sem):
    me = greet(n)
    rows = x_ref.shape[0]
    mine = pl.ds(pl.multiple_of(me * rows, rows), rows)
    copies = []
    for step in range(1, n):
        copy = pltpu.make_async_remote_copy(
            src_ref=x_ref,
            dst_ref=o_ref.at[mine],
            send_sem=send_sem.at[step - 1],
            recv_sem=recv_sem.at[step - 1],
            device_id={"seq": lax.rem(me + step, n)},
            device_id_type=MESH,
        )
        copy.start()
        copies.append(copy)
    o_ref[mine, :] = x_ref[...]
    for copy in copies:
        copy.wait()


def gather_rows(x, n, call_id):
    rows, width = x.shape
    return pl.pallas_call(
        functools.partial(gather_kernel, n),
        out_shape=jax.ShapeDtypeStruct((n * rows, width), x.dtype),
        in_specs=[pl.BlockSpec(memory_space=pltpu.VMEM)],
        out_specs=pl.BlockSpec(memory_space=pltpu.VMEM),
        scratch_shapes=[pltpu.SemaphoreType.DMA((n - 1,)), pltpu.SemaphoreType.DMA((n - 1,))],
        compiler_params=pltpu.CompilerParams(collective_id=call_id, has_side_effects=True),
        name=f"gather_rows_{call_id}",
    )(x)


def scatter_kernel(n, p_ref, o_ref, landed, send_sem, recv_sem):
    me = greet(n)
    rows = o_ref.shape[0]
    copies = []
    for step in range(1, n):
        peer = lax.rem(me + step, n)
        copy = pltpu.make_async_remote_copy(
            src_ref=p_ref.at[pl.ds(pl.multiple_of(peer * rows, rows), rows)],
            dst_ref=landed.at[step - 1],
            send_sem=send_sem.at[step - 1],
            recv_sem=recv_sem.at[step - 1],
            device_id={"seq": peer},
            device_id_type=MESH,
        )
        copy.start()
        copies.append(copy)
    o_ref[...] = p_ref[pl.ds(pl.multiple_of(me * rows, rows), rows), :].astype(F32)
    for step, copy in enumerate(copies):
        copy.wait()
        o_ref[...] += landed[step].astype(F32)


def scatter_sum(partial, n, call_id):
    total, width = partial.shape
    rows = total // n
    return pl.pallas_call(
        functools.partial(scatter_kernel, n),
        out_shape=jax.ShapeDtypeStruct((rows, width), F32),
        in_specs=[pl.BlockSpec(memory_space=pltpu.VMEM)],
        out_specs=pl.BlockSpec(memory_space=pltpu.VMEM),
        scratch_shapes=[
            pltpu.VMEM((n - 1, rows, width), partial.dtype),
            pltpu.SemaphoreType.DMA((n - 1,)),
            pltpu.SemaphoreType.DMA((n - 1,)),
        ],
        compiler_params=pltpu.CompilerParams(collective_id=call_id, has_side_effects=True),
        name=f"scatter_sum_{call_id}",
    )(partial)


def rope(values, cosine, sine):
    return values * cosine + pltpu.roll(values, HEAD_SIZE // 2, 1) * sine


def rope_back(grad, cosine, sine):
    return grad * cosine - pltpu.roll(grad, HEAD_SIZE // 2, 1) * sine


def forward_kernel(
    q_pre, k_pre, v_ref, gain_q, gain_k, cos_q, sin_q, cos_k, sin_k, place_k, place_q, start_q,
    out_ref, p_ref, q_ref, k_ref, v_turned,
):
    @pl.when((pl.program_id(1) == 0) & (pl.program_id(2) == 0))
    def _():
        pre = k_pre[...]
        k_ref[...] = rope(pre * inverse_rms(pre) * gain_k[...], cos_k[...], sin_k[...]).astype(BF16)
        v_turned[...] = v_ref[...].astype(F32).T.astype(BF16)

    pre = q_pre[...]
    query = rope(pre * inverse_rms(pre) * gain_q[...], cos_q[...], sin_q[...]).astype(BF16)
    q_ref[...] = query
    scores = back_matmul(k_ref[...], query) * SCALE
    keys = place_k[...]
    allowed = (keys <= place_q[...]) & (keys >= start_q[...])
    scores = jnp.where(allowed, scores, MASKED)
    top = jnp.max(scores, axis=0, keepdims=True)
    weights = jnp.exp(scores - top)
    total = jnp.sum(weights, axis=0, keepdims=True)
    weights = (weights * (1.0 / total)).astype(BF16)
    p_ref[0] = weights
    out_ref[...] = matrix_product(v_turned[...], weights).T.astype(BF16)


def attend_forward(q_pre, k_pre, value, gain_q, gain_k, cosine, sine, place, start):
    rows = q_pre.shape[0]
    heads = q_pre.shape[1] // HEAD_SIZE
    kv = heads // GROUP
    block = QUERY_BLOCK
    q_spec = pl.BlockSpec((block, HEAD_SIZE), lambda k, g, b: (b, k * GROUP + g))
    k_spec = pl.BlockSpec((rows, HEAD_SIZE), lambda k, g, b: (0, k))
    gain_spec = pl.BlockSpec((1, HEAD_SIZE), lambda k, g, b: (0, 0))
    trig_q = pl.BlockSpec((block, HEAD_SIZE), lambda k, g, b: (b, 0))
    trig_k = pl.BlockSpec((rows, HEAD_SIZE), lambda k, g, b: (0, 0))
    column = pl.BlockSpec((rows, 1), lambda k, g, b: (0, 0))
    row = pl.BlockSpec((1, block), lambda k, g, b: (0, b))
    return pl.pallas_call(
        forward_kernel,
        grid=(kv, GROUP, rows // block),
        out_shape=(
            jax.ShapeDtypeStruct((rows, heads * HEAD_SIZE), BF16),
            jax.ShapeDtypeStruct((heads, rows, rows), BF16),
            jax.ShapeDtypeStruct((rows, heads * HEAD_SIZE), BF16),
            jax.ShapeDtypeStruct((rows, kv * HEAD_SIZE), BF16),
        ),
        in_specs=[
            q_spec, k_spec, k_spec, gain_spec, gain_spec, trig_q, trig_q, trig_k, trig_k,
            column, row, row,
        ],
        out_specs=(
            q_spec,
            pl.BlockSpec((1, rows, block), lambda k, g, b: (k * GROUP + g, 0, b)),
            q_spec,
            k_spec,
        ),
        scratch_shapes=[pltpu.VMEM((HEAD_SIZE, rows), BF16)],
        name="attend_forward",
    )(
        q_pre, k_pre, value, gain_q, gain_k, cosine, sine, cosine, sine,
        place[:, None], place[None, :], start[None, :],
    )


def backward_kernel(
    p_ref, q_ref, k_ref, v_ref, grad_ref, q_pre, k_pre, gain_q, gain_k, cos_q, sin_q, cos_k, sin_k,
    dq_ref, dk_ref, dv_ref, dgain_q, dgain_k, k_turned, dk_sum, dv_sum,
):
    kv, group, block = pl.program_id(0), pl.program_id(1), pl.program_id(2)
    first = (group == 0) & (block == 0)
    last = (group == pl.num_programs(1) - 1) & (block == pl.num_programs(2) - 1)

    @pl.when(first & (kv == 0))
    def _():
        dgain_q[...] = jnp.zeros_like(dgain_q)
        dgain_k[...] = jnp.zeros_like(dgain_k)

    @pl.when(first)
    def _():
        k_turned[...] = k_ref[...].astype(F32).T.astype(BF16)
        dk_sum[...] = jnp.zeros_like(dk_sum)
        dv_sum[...] = jnp.zeros_like(dv_sum)

    rounded = p_ref[0]
    weights = rounded.astype(F32)
    grad = grad_ref[...]
    grad_weights = back_matmul(v_ref[...], grad)
    delta = jnp.sum(weights * grad_weights, axis=0, keepdims=True)
    grad_scores = (weights * (grad_weights - delta)).astype(BF16)
    dk_sum[...] += matrix_product(grad_scores, q_ref[...])
    dv_sum[...] += matrix_product(rounded, grad)
    dq = (matrix_product(k_turned[...], grad_scores).T * SCALE).astype(BF16).astype(F32)
    dq, gain_rows = rms_backward(q_pre[...], gain_q[...], rope_back(dq, cos_q[...], sin_q[...]))
    dq_ref[...] = dq.astype(BF16)
    dgain_q[...] += jnp.sum(gain_rows, axis=0, keepdims=True)

    @pl.when(last)
    def _():
        dk = (dk_sum[...] * SCALE).astype(BF16).astype(F32)
        dk, gain_rows = rms_backward(k_pre[...], gain_k[...], rope_back(dk, cos_k[...], sin_k[...]))
        dk_ref[...] = dk.astype(BF16)
        dgain_k[...] += jnp.sum(gain_rows, axis=0, keepdims=True)
        dv_ref[...] = dv_sum[...].astype(BF16)


def attend_backward(weights, query, key, value, grad, q_pre, k_pre, gain_q, gain_k, cosine, sine):
    rows = q_pre.shape[0]
    heads = q_pre.shape[1] // HEAD_SIZE
    kv = heads // GROUP
    block = QUERY_BLOCK
    q_spec = pl.BlockSpec((block, HEAD_SIZE), lambda k, g, b: (b, k * GROUP + g))
    k_spec = pl.BlockSpec((rows, HEAD_SIZE), lambda k, g, b: (0, k))
    gain_spec = pl.BlockSpec((1, HEAD_SIZE), lambda k, g, b: (0, 0))
    trig_q = pl.BlockSpec((block, HEAD_SIZE), lambda k, g, b: (b, 0))
    trig_k = pl.BlockSpec((rows, HEAD_SIZE), lambda k, g, b: (0, 0))
    return pl.pallas_call(
        backward_kernel,
        grid=(kv, GROUP, rows // block),
        out_shape=(
            jax.ShapeDtypeStruct((rows, heads * HEAD_SIZE), BF16),
            jax.ShapeDtypeStruct((rows, kv * HEAD_SIZE), BF16),
            jax.ShapeDtypeStruct((rows, kv * HEAD_SIZE), BF16),
            jax.ShapeDtypeStruct((1, HEAD_SIZE), F32),
            jax.ShapeDtypeStruct((1, HEAD_SIZE), F32),
        ),
        in_specs=[
            pl.BlockSpec((1, rows, block), lambda k, g, b: (k * GROUP + g, 0, b)),
            q_spec, k_spec, k_spec, q_spec, q_spec, k_spec, gain_spec, gain_spec,
            trig_q, trig_q, trig_k, trig_k,
        ],
        out_specs=(q_spec, k_spec, k_spec, gain_spec, gain_spec),
        scratch_shapes=[
            pltpu.VMEM((HEAD_SIZE, rows), BF16),
            pltpu.VMEM((rows, HEAD_SIZE), F32),
            pltpu.VMEM((rows, HEAD_SIZE), F32),
        ],
        name="attend_backward",
    )(weights, query, key, value, grad, q_pre, k_pre, gain_q, gain_k, cosine, sine, cosine, sine)


def on_device(
    tokens, lengths, packing, norm_in, w_query, key_projection, value_projection, norm_query,
    norm_key, w_out, norm_post, w_gate, w_up, w_down, cotangent,
):
    n = lax.axis_size("seq")
    shards = lax.axis_size("fsdp")
    me = lax.axis_index("seq")
    mine = lax.axis_index("fsdp")
    resident = tokens.shape[1]
    width = tokens.shape[2]
    rows = resident * n
    heads = HQ // n
    kv = KEY_VALUE_HEADS // n
    hidden_piece = w_down.shape[0] // n
    out_piece = width // n

    def columns(weight, pieces):
        size = weight.shape[1] // pieces
        return lax.dynamic_slice_in_dim(weight, me * size, size, axis=1)

    def spread_columns(weight):
        pieces = weight.reshape(weight.shape[0], shards, n, hidden_piece)
        return lax.dynamic_index_in_dim(pieces, me, axis=2, keepdims=False).reshape(
            weight.shape[0], shards * hidden_piece
        )

    gains = lax.all_gather(
        jnp.concatenate([norm_in, norm_post, norm_query, norm_key])[None, :], "fsdp", axis=0, tiled=True
    ).astype(F32)
    part, small = norm_in.shape[0], norm_query.shape[0]
    gain_in = gains[:, :part].reshape(1, -1)
    gain_post = gains[:, part : 2 * part].reshape(1, -1)
    gain_query = gains[:, 2 * part : 2 * part + small].reshape(1, -1)
    gain_key = gains[:, 2 * part + small :].reshape(1, -1)

    qkv_weight = lax.all_gather(
        jnp.concatenate(
            [columns(w_query, n), columns(key_projection, n), columns(value_projection, n)], axis=1
        ),
        "fsdp", axis=0, tiled=True,
    )
    out_columns = lax.all_gather(columns(w_out, n), "fsdp", axis=0, tiled=True)
    gate_up_weight = lax.all_gather(
        jnp.concatenate([spread_columns(w_gate), spread_columns(w_up)], axis=1), "fsdp", axis=0, tiled=True
    )
    down_weight = lax.all_gather(
        lax.dynamic_slice_in_dim(w_down, me * hidden_piece, hidden_piece, axis=0),
        "fsdp", axis=0, tiled=True,
    )
    out_weight = lax.all_to_all(out_columns, "seq", split_axis=0, concat_axis=1, tiled=True)

    order = packing[0]
    places = jnp.arange(rows, dtype=jnp.int32)
    place = jnp.sum(jnp.where(order[None, :] == places[:, None], places[None, :], 0), axis=1)
    ends = jnp.cumsum(lengths[0])
    start = jnp.sum(jnp.where(place[:, None] >= ends[None, :], lengths[0][None, :], 0), axis=1)
    half = HEAD_SIZE // 2
    inv_freq = ROPE_BASE ** (-jnp.arange(half, dtype=F32) / half)
    angles = (place - start).astype(F32)[:, None] * inv_freq[None, :]
    cosine, sine = jnp.cos(angles), jnp.sin(angles)
    cosine = jnp.concatenate([cosine, cosine], axis=1)
    sine = jnp.concatenate([-sine, sine], axis=1)

    whole = gather_rows(tokens[0], n, 0)
    inputs = tokens[0].astype(F32)
    whole_f32 = whole.astype(F32)
    unit = whole_f32 * inverse_rms(whole_f32)
    normalized = (unit * gain_in).astype(BF16)
    qkv = matrix_product(normalized, qkv_weight)
    split = heads * HEAD_SIZE
    q_pre = qkv[:, :split]
    k_pre = qkv[:, split : split + kv * HEAD_SIZE]
    value = qkv[:, split + kv * HEAD_SIZE :].astype(BF16)
    attended, weights, query, key = attend_forward(
        q_pre, k_pre, value, gain_query, gain_key, cosine, sine, place, start
    )
    middle = inputs + scatter_sum(matrix_product(attended, out_weight).astype(BF16), n, 1)
    normed_post_mine = (middle * inverse_rms(middle) * gain_post).astype(BF16)
    normed_post = gather_rows(normed_post_mine, n, 2)
    grad_mlp = gather_rows(cotangent[0], n, 3)

    gate_up = matrix_product(normed_post, gate_up_weight)
    units = shards * hidden_piece
    gate, up = gate_up[:, :units], gate_up[:, units:]
    logistic = 1.0 / (1.0 + jnp.exp(-gate))
    hidden = (gate / (1.0 + jnp.exp(-gate)) * up).astype(BF16)
    result = middle + scatter_sum(matrix_product(hidden, down_weight).astype(BF16), n, 4)
    output = result.astype(BF16)[None]

    grad_hidden = back_matmul(grad_mlp, down_weight)
    grad_down = outer_sum(hidden, grad_mlp).astype(BF16)
    grad_gate = (grad_hidden * up * (logistic + gate * logistic * (1.0 - logistic))).astype(BF16)
    grad_up = (grad_hidden * gate * logistic).astype(BF16)
    grad_gate_up = jnp.concatenate([grad_gate, grad_up], axis=1)
    grad_gate_up_weight = outer_sum(normed_post, grad_gate_up).astype(BF16)
    grad_normed_post = scatter_sum(back_matmul(grad_gate_up, gate_up_weight).astype(BF16), n, 5)
    grad_middle, gain_rows = rms_backward(middle, gain_post, grad_normed_post)
    grad_middle = cotangent[0].astype(F32) + grad_middle
    grad_gain_post = jnp.sum(gain_rows, axis=0)
    grad_branch = gather_rows(grad_middle.astype(BF16), n, 6)

    grad_out = outer_sum(attended, grad_branch).astype(BF16)
    grad_attended = back_matmul(grad_branch, out_weight).astype(BF16)
    grad_q, grad_k, grad_v, grad_gain_query, grad_gain_key = attend_backward(
        weights, query, key, value, grad_attended, q_pre, k_pre, gain_query, gain_key, cosine, sine
    )
    grad_qkv = jnp.concatenate([grad_q, grad_k, grad_v], axis=1)
    grad_qkv_weight = outer_sum(normalized, grad_qkv).astype(BF16)
    partial = back_matmul(grad_qkv, qkv_weight)
    grad_gain_in = jnp.sum(partial * unit, axis=0)
    grad_normed = scatter_sum(partial.astype(BF16), n, 7)
    grad_inputs, _ = rms_backward(inputs, gain_in, grad_normed)
    input_grad = (grad_middle + grad_inputs).astype(BF16)[None]

    def shared(grad):
        return lax.all_gather(
            lax.psum_scatter(grad, "fsdp", scatter_dimension=0, tiled=True), "seq", axis=0
        ).astype(F32)

    def beside(pieces):
        return jnp.swapaxes(pieces, 0, 1).reshape(pieces.shape[1], -1)

    final_down = shared(grad_down).reshape(-1, width)
    gate_up_all = shared(grad_gate_up_weight)

    def spread_back(pieces):
        pieces = pieces.reshape(n, pieces.shape[1], shards, hidden_piece)
        return jnp.transpose(pieces, (1, 2, 0, 3)).reshape(pieces.shape[1], -1)

    final_gate = spread_back(gate_up_all[:, :, :units])
    final_up = spread_back(gate_up_all[:, :, units:])
    final_out = beside(
        shared(lax.all_to_all(grad_out, "seq", split_axis=1, concat_axis=0, tiled=True))
    )
    qkv_all = shared(grad_qkv_weight)
    final_query = beside(qkv_all[:, :, :split])
    final_key = beside(qkv_all[:, :, split : split + kv * HEAD_SIZE])
    final_value = beside(qkv_all[:, :, split + kv * HEAD_SIZE :])

    sums = lax.psum(
        jnp.concatenate([grad_gain_in, grad_gain_post, grad_gain_query[0], grad_gain_key[0]]),
        ("seq", "fsdp"),
    )

    def share(offset, size):
        return lax.dynamic_slice_in_dim(sums, offset + mine * size, size)

    return (
        output,
        input_grad,
        share(0, part),
        final_query,
        final_key,
        final_value,
        share(2 * width, small),
        share(2 * width + HEAD_SIZE, small),
        final_out,
        share(width, part),
        final_gate,
        final_up,
        final_down,
    )


def solution(mesh):
    flat, wide = P("fsdp"), P("fsdp", None)
    whole = P("fsdp", "seq", None)
    in_specs = (
        whole, wide, wide, flat, wide, wide, wide, flat, flat, wide, flat, wide, wide, wide, whole,
    )
    out_specs = (whole, whole, flat, wide, wide, wide, flat, flat, wide, flat, wide, wide, wide)
    return jax.shard_map(
        on_device, mesh=mesh, in_specs=in_specs, out_specs=out_specs, check_vma=False
    )
```

time: 990 us -> 597 us (0.60)
  waiting for transfers between devices: 552 us -> 68.8 us
  Pallas kernels: 0 us -> 274 us
  matrix products: 144 us -> 64.4 us
  other arithmetic: 54.3 us -> 18.9 us
  starting transfers between devices: 36.7 us -> 4.91 us
  local copies, waits for them, and re-layouts: 66.7 us -> 39.7 us
    pallas_call x0 -> x10, Pallas kernels: none -> 274 us  [the longest x4 115 us: gather_rows(): pl.pallas_call(functools.partial(gather_kernel, n), out_shape=jax.ShapeDt...]
    reduce_scatter x7 -> x4, waiting for transfers between devices: 296 us -> 44.7 us  [shared(): lax.psum_scatter(grad, 'fsdp', scatter_dimension=0, tiled=True)]
    all_gather x7 -> x6, waiting for transfers between devices: 171 us -> 23.9 us  [the longest x2 23.9 us: shared(): lax.all_gather(lax.psum_scatter(grad, 'fsdp', scatter_dimension=0, tiled=...]
    all_to_all x9 -> x1, waiting for transfers between devices: 41.5 us -> 0.01 us  [on_device(): lax.all_to_all(out_columns, 'seq', split_axis=0, concat_axis=1, tiled=True)]
    dot_general x19 -> x4, matrix products: 60.7 us -> 19.7 us  [matrix_product(): return jnp.dot(left, right, preferred_element_type=F32)]
    psum x1 -> x0, waiting for transfers between devices: 38.6 us -> none  [on_device(): lax.psum(share_query.astype(jnp.bfloat16), 'seq').astype(jnp.float32)]
    all_to_all x4 -> x1, blocking collectives: 48.5 us -> 16.1 us  [on_device(): lax.all_to_all(grad_out, 'seq', split_axis=1, concat_axis=0, tiled=True)]
    all_to_all x9 -> x1, starting transfers between devices: 35.7 us -> 4.24 us  [on_device(): lax.all_to_all(out_columns, 'seq', split_axis=0, concat_axis=1, tiled=True)]
  transfers between devices with their start and end apart: 24 -> 11, of which waited for: 16 -> 3; matrix products, arithmetic and copies ran while one was open for 17% -> 12% of each run, Pallas kernels for 0% -> 28%
where the time goes in v1:
time: 597 us; the launch traced here: 589 us
  Pallas kernels  274 us (46%)
  blocking collectives  102 us (17%)
  waiting for transfers between devices  68.8 us (12%)
  matrix products  64.4 us (11%)
  local copies, waits for them, and re-layouts  39.7 us (7%)
  other arithmetic  18.9 us (3%)
  between operations  15.9 us (3%)
    pallas_call x4, Pallas kernels, gather_rows(): pl.pallas_call(functools.partial(gather_kernel, n), out_shape=jax.ShapeDt...  115 us
    pallas_call x4, Pallas kernels, scatter_sum(): pl.pallas_call(functools.partial(scatter_kernel, n), out_shape=jax.ShapeD...  110 us
    reduce_scatter x4, waiting for transfers between devices, shared(): lax.psum_scatter(grad, 'fsdp', scatter_dimension=0, tiled=True)  44.7 us
    psum x1, blocking collectives, on_device(): lax.psum(jnp.concatenate([grad_gain_in, grad_gain_post, grad_gain_query[0...  40.7 us
    all_gather x2, blocking collectives, shared(): lax.all_gather(lax.psum_scatter(grad, 'fsdp', scatter_dimension=0, tiled=...  25.9 us
    pallas_call x1, Pallas kernels, attend_backward(): pl.pallas_call(backward_kernel, grid=(kv, GROUP, rows // block), out_shap...  25.4 us
    dot_general x4, matrix products, back_matmul(): lax.dot_general(left, right, (((1,), (1,)), ((), ())), preferred_element_...  24.9 us
    pallas_call x1, Pallas kernels, attend_forward(): pl.pallas_call(forward_kernel, grid=(kv, GROUP, rows // block), out_shape...  24.3 us
  transfers between devices with their start and end apart: 11, of which 3 were waited for; matrix products, arithmetic and copies ran while one was open for 12% of the time, Pallas kernels for 28%

profile of v1, /device:TPU:0, one launch (start us, length us, event | category | flops | bytes accessed | tf_op | source)
XLA Modules:
  0.0 588.8 jit_solution(2743125424651261624)
XLA Ops:
  7.3 1.7 constant_dynamic-slice_fusion.3
  15.7 19.0 %all-reduce = bf16[2304]{0:T(1024)(128)(2,1)S(1)} all-reduce(bf16[2304]{0:T(1024)(128)(2,1)S(1)} %dynamic-update-slice), channel_id=2, replica_groups=mesh['seq'=4,'fsdp'=8] {'fsdp'}, use_global_device_ids=true, to_apply=%add | all-reduce | flops 2304 | bytes 9216
  34.8 25.2 %gather_rows_0.1 = bf16[1024,1024]{1,0:T(8,128)(2,1)} custom-call(bf16[256,1024]{1,0:T(8,128)(2,1)} %bitcast.101), custom_call_target="tpu_custom_call" | custom-call | tf_op jit(solution)/shard_map/gather_rows_0/pallas_call | solution.py:82
  60.0 2.1 fusion.4
  63.0 4.2 all-to-all-start
  69.5 35.7 %gather_rows_3.1 = bf16[1024,1024]{1,0:T(8,128)(2,1)} custom-call(bf16[256,1024]{1,0:T(8,128)(2,1)} %bitcast.111), custom_call_target="tpu_custom_call" | custom-call | tf_op jit(solution)/shard_map/gather_rows_3/pallas_call | solution.py:82
  105.2 1.9 fusion.23
  108.5 2.3 copy.66
  110.8 4.0 fusion.19
  114.7 1.5 slice.58.q_pre
  118.2 24.3 %attend_forward.1 = (bf16[1024,512]{1,0:T(8,128)(2,1)}, bf16[4,1024,1024]{2,1,0:T(8,128)(2,1)}, bf16[1024,512]{1,0:T(8,128)(2,1)}, bf16[1024,256]{1,0:T(8,128)(2,1)}) custom-call(f32[1024,512]{1,0:T(8,128)} %slice.58.q_pre, f32[1024,256]{1,0:T(8,128)} %slice.59.k_pre, bf16[1024,256]{1,0:T(8,128)(2,1)} %slice.82.v_ref, f32[1,128]{1,0:T(1,128)} %reshape.170.gain_q, ...), custom_call_target="tpu_custom_call" | custom-call | tf_op jit(solution)/shard_map/attend_forward/pallas_call | solution.py:178
  142.5 3.9 convolution_convert_fusion.2.p_ref
  146.4 28.1 %scatter_sum_1.1 = f32[256,1024]{1,0:T(8,128)} custom-call(bf16[1024,1024]{1,0:T(8,128)(2,1)} %convolution_convert_fusion.2.p_ref), custom_call_target="tpu_custom_call" | custom-call | tf_op jit(solution)/shard_map/scatter_sum_1/pallas_call | solution.py:118
  174.5 1.4 multiply_reduce_fusion.2
  176.9 27.5 %gather_rows_2.1 = bf16[1024,1024]{1,0:T(8,128)(2,1)} custom-call(bf16[256,1024]{1,0:T(8,128)(2,1)} %multiply_convert_fusion.1.x_ref), custom_call_target="tpu_custom_call" | custom-call | tf_op jit(solution)/shard_map/gather_rows_2/pallas_call | solution.py:82
  204.5 8.7 %fusion.31 = f32[1024,1536]{1,0:T(8,128)} fusion(bf16[1024,1024]{1,0:T(8,128)(2,1)} %gather_rows_2.1, bf16[1024,1536]{0,1:T(8,128)(2,1)} %all-gather.16.cloned.1.call-done), kind=kOutput, calls=%fused_computation.91 | convolution fusion | flops 3221225472 | bytes 11534336 | tf_op jit(solution)/shard_map/dot_general | solution.py:26
  213.2 7.9 %fusion.6 = (bf16[1024,768]{1,0:T(8,128)(2,1)S(1)}, bf16[1024,768]{1,0:T(8,128)(2,1)}, bf16[1024,768]{1,0:T(8,128)(2,1)S(1)}) fusion(f32[1024,1536]{1,0:T(8,128)} %fusion.31, bf16[768,1024]{1,0:T(8,128)(2,1)} %all-gather.18.cloned.1.call-done, bf16[1024,1024]{1,0:T(8,128)(2,1)} %gather_rows_3.1), kind=kOutput, calls=%fused_computation.14 | convolution fusion | flops 1623195648 | bytes 14680064 | tf_op jit(solution)/shard_map/dot_general | solution.py:34
  222.2 3.2 convolution_convert_fusion.3.p_ref
  225.4 27.9 %scatter_sum_4.1 = f32[256,1024]{1,0:T(8,128)} custom-call(bf16[1024,1024]{1,0:T(8,128)(2,1)} %convolution_convert_fusion.3.p_ref), custom_call_target="tpu_custom_call" | custom-call | tf_op jit(solution)/shard_map/scatter_sum_4/pallas_call | solution.py:118
  253.3 7.1 %fusion.11.p_ref = bf16[1024,1024]{1,0:T(8,128)(2,1)} fusion(bf16[1024,1536]{0,1:T(8,128)(2,1)} %all-gather.16.cloned.1.call-done, bf16[1024,768]{1,0:T(8,128)(2,1)} %get-tuple-element.79, bf16[1024,768]{1,0:T(8,128)(2,1)S(1)} %get-tuple-element.78), kind=kOutput, calls=%fused_computation.23 | convolution fusion | flops 3228565504 | bytes 8388608 | tf_op jit(solution)/shard_map/dot_general | solution.py:34
  260.4 27.1 %scatter_sum_5.1 = f32[256,1024]{1,0:T(8,128)} custom-call(bf16[1024,1024]{1,0:T(8,128)(2,1)} %fusion.11.p_ref), custom_call_target="tpu_custom_call" | custom-call | tf_op jit(solution)/shard_map/scatter_sum_5/pallas_call | solution.py:118
  287.5 1.6 multiply_reduce_fusion
  289.1 1.7 fusion.26
  290.9 26.8 %gather_rows_6.1 = bf16[1024,1024]{1,0:T(8,128)(2,1)} custom-call(bf16[256,1024]{1,0:T(8,128)(2,1)} %get-tuple-element.74.x_ref), custom_call_target="tpu_custom_call" | custom-call | tf_op jit(solution)/shard_map/gather_rows_6/pallas_call | solution.py:82
  317.7 3.8 convolution_convert_fusion.6.grad_ref
  321.6 25.4 %attend_backward.1 = (bf16[1024,512]{1,0:T(8,128)(2,1)}, bf16[1024,256]{1,0:T(8,128)(2,1)}, bf16[1024,256]{1,0:T(8,128)(2,1)}, f32[1,128]{1,0:T(1,128)}, f32[1,128]{1,0:T(1,128)}) custom-call(bf16[4,1024,1024]{2,1,0:T(8,128)(2,1)} %get-tuple-element.23.p_ref, bf16[1024,512]{1,0:T(8,128)(2,1)} %get-tuple-element.24.q_ref, ...), custom_call_target="tpu_custom_call" | custom-call | tf_op jit(solution)/shard_map/attend_backward/pallas_call | solution.py:256
  347.0 1.5 constant_dynamic-update-slice_fusion.2
  348.6 1.4 copy-done.14
  350.0 4.0 convolution_convert_fusion.1
  354.0 7.6 %convolution_convert_fusion = bf16[1024,1536]{1,0:T(8,128)(2,1)} fusion(bf16[1024,1024]{1,0:T(8,128)(2,1)} %gather_rows_2.1, bf16[1024,768]{1,0:T(8,128)(2,1)} %get-tuple-element.79, bf16[1024,768]{1,0:T(8,128)(2,1)} %copy-done.29), kind=kOutput, calls=%fused_computation.9 | convolution fusion | flops 3229089792 | bytes 8388608 | tf_op jit(solution)/shard_map/dot_general | solution.py:30
  361.7 3.2 convolution_convert_fusion.5
  365.0 16.1 %all_to_all.38 = bf16[512,4,256]{2,0,1:T(8,128)(2,1)} all-to-all(bf16[512,4,256]{2,0,1:T(8,128)(2,1)S(1)} %bitcast.108), channel_id=1, replica_groups=mesh['seq'=4,'fsdp'=8] {'seq'}, dimensions={1} | all-to-all | bytes 2097152 | tf_op jit(solution)/shard_map/all_to_all | solution.py:413
  381.2 5.1 convolution_convert_fusion.4
  386.3 3.9 reduce-scatter.5.cloned.1.call-done
  390.5 40.8 %reduce-scatter.9.cloned.1.call-done = bf16[128,1536]{1,0:T(8,128)(2,1)} async-done(((bf16[1024,1536]{1,0:T(8,128)(2,1)}), bf16[128,1536]{1,0:T(8,128)(2,1)}) %reduce-scatter.9.cloned.1.call-update) | async-done | bytes 393232 | tf_op jit(solution)/shard_map/reduce_scatter | solution.py:397
  431.4 6.0 %fusion.3 = (f32[1024]{0:T(1024)S(1)}, bf16[1024,1024]{1,0:T(8,128)(2,1)}) fusion(bf16[1024,1024]{1,0:T(8,128)(2,1)S(1)} %copy-done.6, f32[1024]{0:T(1024)S(1)} %add_rsqrt_fusion, bf16[1024,1024]{1,0:T(8,128)(2,1)} %copy-done.14, bf16[1024,1024]{1,0:T(8,128)(2,1)} %all-gather.12.cloned.1.call-done), kind=kOutput, calls=%fused_computation.5 | convolution fusion | flops 2152725504 | bytes 8396800 | tf_op jit(solution)/shard_map/dot_general | solution.py:34
  437.4 26.5 %scatter_sum_7.1 = f32[256,1024]{1,0:T(8,128)} custom-call(bf16[1024,1024]{1,0:T(8,128)(2,1)} %get-tuple-element.82.p_ref), custom_call_target="tpu_custom_call" | custom-call | tf_op jit(solution)/shard_map/scatter_sum_7/pallas_call | solution.py:118
  463.9 40.7 %psum.7 = f32[2304]{0:T(1024)S(1)} all-reduce(f32[2304]{0:T(1024)S(1)} %pad_maximum_fusion.9), channel_id=1, replica_groups=mesh['seq'=4,'fsdp'=8] {'seq','fsdp'}, use_global_device_ids=true, to_apply=%region_10.11 | all-reduce | flops 2304 | bytes 18432 | tf_op jit(solution)/shard_map/psum | solution.py:420
  505.8 1.5 fusion.12
  508.4 12.2 %all-gather.2 = bf16[1024,256]{1,0:T(8,128)(2,1)S(1)} all-gather(bf16[256,256]{1,0:T(8,128)(2,1)} %reduce-scatter.7.cloned.1.call-done), channel_id=4, replica_groups=mesh['seq'=4,'fsdp'=8] {'seq'}, dimensions={0}, use_global_device_ids=true | all-gather | bytes 655360 | tf_op jit(solution)/shard_map/all_gather | solution.py:396
  522.4 13.7 %all-gather.4 = bf16[384,1024]{1,0:T(8,128)(2,1)S(1)} all-gather(bf16[96,1024]{1,0:T(8,128)(2,1)} %reduce-scatter.11.cloned.1.call-done), channel_id=6, replica_groups=mesh['seq'=4,'fsdp'=8] {'seq'}, dimensions={0}, use_global_device_ids=true | all-gather | bytes 983040 | tf_op jit(solution)/shard_map/all_gather | solution.py:396
  537.4 1.5 convert.7
  541.8 23.9 %all-gather.22.cloned.1.call-done = bf16[512,1536]{1,0:T(8,128)(2,1)} async-done(((bf16[128,1536]{1,0:T(8,128)(2,1)}), bf16[512,1536]{1,0:T(8,128)(2,1)}) %all-gather.22.cloned.1.call-update) | async-done | bytes 1572880 | tf_op jit(solution)/shard_map/all_gather | solution.py:396
  565.7 3.3 fusion.27
  569.0 1.9 copy.83
  572.2 3.0 copy.80
  575.3 1.9 copy.84
  578.5 3.0 copy.81
  (139 shorter events, 26.3 us)
Async XLA Ops:
  7.2 6.2 %copy-start = (bf16[384,1024]{1,0:T(8,128)(2,1)S(1)}, bf16[384,1024]{1,0:T(8,128)(2,1)}, u32[]{:S(2)}) copy-start(bf16[384,1024]{1,0:T(8,128)(2,1)} %param.28) | copy-start | bytes 2359300
  7.2 4.5 copy-start.12
  7.2 4.9 copy-start.13
  7.2 55.8 %all-gather.14.cloned.1.call-start = ((), (), s32[]{:S(2)}) async-start(), calls=%async_computation.7 | async-start | bytes 1179648 | tf_op jit(solution)/shard_map/all_gather | solution.py:322
  9.0 101.7 %all-gather.12.cloned.1.call-start = ((), (), s32[]{:S(2)}) async-start(), calls=%async_computation.6 | async-start | bytes 2359296 | tf_op jit(solution)/shard_map/all_gather | solution.py:316
  11.6 192.9 %all-gather.16.cloned.1.call-start = ((), (), s32[]{:S(2)}) async-start(), calls=%async_computation.8 | async-start | bytes 3538944 | tf_op jit(solution)/shard_map/all_gather | solution.py:323
  12.1 2.1 copy-start.28
  12.1 3.3 copy-start.22
  12.1 3.3 copy-start.23
  12.1 3.3 copy-start.24
  12.1 3.3 copy-start.25
  13.4 199.8 %all-gather.18.cloned.1.call-start = ((), (), s32[]{:S(2)}) async-start(), calls=%async_computation.9 | async-start | bytes 1769472 | tf_op jit(solution)/shard_map/all_gather | solution.py:326
  34.8 27.3 %copy-start.27 = (s32[1,1024]{1,0:T(1,128)S(1)}, s32[1,1024]{1,0:T(1,128)}, u32[]{:S(2)}) copy-start(s32[1,1024]{1,0:T(1,128)} %param.17) | copy-start | bytes 12292
  34.8 27.8 %copy-start.19 = (s32[1,8]{1,0:T(1,128)S(1)}, s32[1,8]{1,0:T(1,128)}, u32[]{:S(2)}) copy-start(s32[1,8]{1,0:T(1,128)} %param.16) | copy-start | bytes 100
  62.6 42.6 %copy-start.17 = (s32[1024]{0:T(1024)}, s32[1024]{0:T(1024)S(1)}, u32[]{:S(2)}) copy-start(s32[1024]{0:T(1024)S(1)} %select_reduce_fusion) | copy-start | bytes 12292
  62.9 42.3 %copy-start.18 = (s32[1024]{0:T(1024)}, s32[1024]{0:T(1024)S(1)}, u32[]{:S(2)}) copy-start(s32[1024]{0:T(1024)S(1)} %select_reduce_fusion.1) | copy-start | bytes 12292
  63.0 45.5 %all-to-all-start = ((bf16[4,512,256]{2,1,0:T(8,128)(2,1)}), bf16[4,512,256]{2,1,0:T(8,128)(2,1)}, u32[]{:S(2)}, u32[]{:S(2)}) async-start(bf16[4,512,256]{2,1,0:T(8,128)(2,1)} %bitcast.116), calls=%async_computation | async-start | bytes 2097152 | tf_op jit(solution)/shard_map/all_to_all | solution.py:330
  67.2 322.9 %reduce-scatter.5.cloned.1.call-start = ((), (), s32[]{:S(2)}) async-start(), calls=%async_computation.10 | async-start | bytes 2359296 | tf_op jit(solution)/shard_map/reduce_scatter | solution.py:397
  107.1 3.6 copy-start.5
  118.2 24.3 %copy-start.10 = (bf16[512,4,256]{0,2,1:T(8,128)(2,1)S(1)}, bf16[512,4,256]{0,2,1:T(8,128)(2,1)}, u32[]{:S(2)}) copy-start(bf16[512,4,256]{0,2,1:T(8,128)(2,1)} %copy.66) | copy-start | bytes 3145732
  146.4 28.1 %copy-start.4 = (bf16[1,256,1024]{2,1,0:T(8,128)(2,1)S(1)}, bf16[1,256,1024]{2,1,0:T(8,128)(2,1)}, u32[]{:S(2)}) copy-start(bf16[1,256,1024]{2,1,0:T(8,128)(2,1)} %param.15) | copy-start | bytes 1572868
  213.2 9.1 %copy-start.26 = (bf16[768,1024]{1,0:T(8,128)(2,1)S(1)}, bf16[768,1024]{1,0:T(8,128)(2,1)}, u32[]{:S(2)}) copy-start(bf16[768,1024]{1,0:T(8,128)(2,1)} %all-gather.18.cloned.1.call-done) | copy-start | bytes 4718596
  221.1 1.1 copy-start.30
  221.1 32.2 %copy-start.29 = (bf16[1024,768]{1,0:T(8,128)(2,1)}, bf16[1024,768]{1,0:T(8,128)(2,1)S(1)}, u32[]{:S(2)}) copy-start(bf16[1024,768]{1,0:T(8,128)(2,1)S(1)} %get-tuple-element.78) | copy-start | bytes 4718596
  260.4 28.7 %copy-start.7 = (f32[256,1024]{1,0:T(8,128)S(1)}, f32[256,1024]{1,0:T(8,128)}, u32[]{:S(2)}) copy-start(f32[256,1024]{1,0:T(8,128)} %scatter_sum_4.1) | copy-start | bytes 3145732
  260.4 28.7 %copy-start.9 = (bf16[1,256,1024]{2,1,0:T(8,128)(2,1)S(1)}, bf16[1,256,1024]{2,1,0:T(8,128)(2,1)}, u32[]{:S(2)}) copy-start(bf16[1,256,1024]{2,1,0:T(8,128)(2,1)} %param.29) | copy-start | bytes 1572868
  287.5 1.6 copy-start.2
  290.9 26.8 %copy-start.11 = (bf16[512,4,256]{0,2,1:T(8,128)(2,1)S(1)}, bf16[512,4,256]{0,2,1:T(8,128)(2,1)}, u32[]{:S(2)}) copy-start(bf16[512,4,256]{0,2,1:T(8,128)(2,1)} %copy.66) | copy-start | bytes 3145732
  346.9 1.5 copy-start.16
  346.9 1.6 copy-start.15
  346.9 3.0 copy-start.6
  348.6 1.4 copy-start.14
  354.0 77.4 %reduce-scatter.9.cloned.1.call-start = ((), (), s32[]{:S(2)}) async-start(), calls=%async_computation.12 | async-start | bytes 3538944 | tf_op jit(solution)/shard_map/reduce_scatter | solution.py:397
  361.7 146.7 %reduce-scatter.7.cloned.1.call-start = ((), (), s32[]{:S(2)}) async-start(), calls=%async_computation.11 | async-start | bytes 1179648 | tf_op jit(solution)/shard_map/reduce_scatter | solution.py:397
  381.1 141.3 %reduce-scatter.11.cloned.1.call-start = ((), (), s32[]{:S(2)}) async-start(), calls=%async_computation.13 | async-start | bytes 1769472 | tf_op jit(solution)/shard_map/reduce_scatter | solution.py:397
  386.3 151.1 %all-gather.20.cloned.1.call-start = ((), (), s32[]{:S(2)}) async-start(), calls=%async_computation.14 | async-start | bytes 1310720 | tf_op jit(solution)/shard_map/all_gather | solution.py:396
  390.2 175.5 %all-gather.22.cloned.1.call-start = ((), (), s32[]{:S(2)}) async-start(), calls=%async_computation.15 | async-start | bytes 1966080 | tf_op jit(solution)/shard_map/all_gather | solution.py:396
  437.3 26.5 %copy-start.20 = (f32[1,128]{1,0:T(1,128)S(1)}, f32[1,128]{1,0:T(1,128)}, u32[]{:S(2)}) copy-start(f32[1,128]{1,0:T(1,128)} %get-tuple-element.29) | copy-start | bytes 1540
  437.3 26.6 %copy-start.21 = (f32[1,128]{1,0:T(1,128)S(1)}, f32[1,128]{1,0:T(1,128)}, u32[]{:S(2)}) copy-start(f32[1,128]{1,0:T(1,128)} %get-tuple-element.30) | copy-start | bytes 1540
  437.4 70.0 %copy-start.8 = (f32[256,1024]{1,0:T(8,128)S(1)}, f32[256,1024]{1,0:T(8,128)}, u32[]{:S(2)}) copy-start(f32[256,1024]{1,0:T(8,128)} %get-tuple-element.75) | copy-start | bytes 3145732
  463.9 43.4 %copy-start.3 = (f32[256,1024]{1,0:T(8,128)S(1)}, f32[256,1024]{1,0:T(8,128)}, u32[]{:S(2)}) copy-start(f32[256,1024]{1,0:T(8,128)} %scatter_sum_7.1) | copy-start | bytes 3145732
  577.1 4.3 copy-start.1
Sparse Core Ops, SparseCore 0:
  10.2 25.2 all-gather.13
  37.7 28.8 all-gather.11
  68.8 38.5 all-gather.15
  109.4 23.4 all-gather.17
  354.1 36.0 reduce-scatter.4
  392.4 38.9 reduce-scatter.8
  433.6 32.0 reduce-scatter.6
  468.6 32.6 reduce-scatter.10
  503.2 29.4 all-gather.19
  534.4 31.3 all-gather.21

commit v2 on v1

v2 whole, which is shorter than its diff:
```python
import functools

import jax
import jax.numpy as jnp
from jax import lax
from jax.experimental import pallas as pl
from jax.experimental.pallas import tpu as pltpu
from jax.sharding import PartitionSpec as P

HQ = 16
KEY_VALUE_HEADS = 8
HEAD_SIZE = 128
GROUP = HQ // KEY_VALUE_HEADS

ROPE_BASE = 1000000.0
EPSILON = 1e-06
MASKED = -1e30
SCALE = HEAD_SIZE ** (-0.5)
MESH = pl.DeviceIdType.MESH
BF16 = jnp.bfloat16
F32 = jnp.float32


def matrix_product(left, right):
    return jnp.dot(left, right, preferred_element_type=F32)


def outer_sum(left, right):
    return lax.dot_general(left, right, (((0,), (0,)), ((), ())), preferred_element_type=F32)


def back_matmul(left, right):
    return lax.dot_general(left, right, (((1,), (1,)), ((), ())), preferred_element_type=F32)


def inverse_rms(values):
    return lax.rsqrt(jnp.mean(values * values, axis=-1, keepdims=True) + EPSILON)


def rms_backward(values, gain, grad):
    c = inverse_rms(values)
    scaled = grad * gain
    inner = jnp.mean(values * scaled, axis=-1, keepdims=True)
    return c * scaled - values * (c * c * c) * inner, grad * values * c


def greet(*axes):
    barrier = pltpu.get_barrier_semaphore()
    count = 0
    for axis in axes:
        n = lax.axis_size(axis)
        me = lax.axis_index(axis)
        for step in range(1, n):
            pl.semaphore_signal(
                barrier, inc=1, device_id={axis: lax.rem(me + step, n)}, device_id_type=MESH
            )
        count += n - 1
    pl.semaphore_wait(barrier, count)


def block_of(index, size):
    return pl.ds(pl.multiple_of(index * size, size), size)


def start_to_peers(axis, source, target, send_sem, recv_sem):
    n = lax.axis_size(axis)
    me = lax.axis_index(axis)
    copies = []
    for step in range(1, n):
        peer = lax.rem(me + step, n)
        copy = pltpu.make_async_remote_copy(
            src_ref=source(peer),
            dst_ref=target(step),
            send_sem=send_sem.at[step - 1],
            recv_sem=recv_sem.at[step - 1],
            device_id={axis: peer},
            device_id_type=MESH,
        )
        copy.start()
        copies.append(copy)
    return copies


def semaphores(*counts):
    return [pltpu.SemaphoreType.DMA((count,)) for count in counts]


VMEM_SPEC = pl.BlockSpec(memory_space=pltpu.VMEM)
ANY_SPEC = pl.BlockSpec(memory_space=pl.ANY)


def communicating(call_id, **more):
    return pltpu.CompilerParams(collective_id=call_id, has_side_effects=True, **more)


def gather_kernel(x_ref, o_ref, send_sem, recv_sem):
    greet("seq")
    mine = block_of(lax.axis_index("seq"), x_ref.shape[0])
    copies = start_to_peers(
        "seq", lambda peer: x_ref, lambda step: o_ref.at[mine], send_sem, recv_sem
    )
    o_ref[mine, :] = x_ref[...]
    for copy in copies:
        copy.wait()


def gather_rows(x, n, call_id):
    rows, width = x.shape
    return pl.pallas_call(
        gather_kernel,
        out_shape=jax.ShapeDtypeStruct((n * rows, width), x.dtype),
        in_specs=[VMEM_SPEC],
        out_specs=VMEM_SPEC,
        scratch_shapes=semaphores(n - 1, n - 1),
        compiler_params=communicating(call_id),
        name=f"gather_rows_{call_id}",
    )(x)


def gather_first_kernel(x_ref, gains_ref, o_ref, all_gains, send, recv, gain_send, gain_recv):
    greet("seq", "fsdp")
    place = lax.axis_index("fsdp")
    gain_copies = start_to_peers(
        "fsdp", lambda peer: gains_ref, lambda step: all_gains.at[place], gain_send, gain_recv
    )
    mine = block_of(lax.axis_index("seq"), x_ref.shape[0])
    copies = start_to_peers("seq", lambda peer: x_ref, lambda step: o_ref.at[mine], send, recv)
    o_ref[mine, :] = x_ref[...]
    all_gains[place] = gains_ref[...]
    for copy in gain_copies + copies:
        copy.wait()


def gather_first(x, gains, n, shards, call_id):
    rows, width = x.shape
    return pl.pallas_call(
        gather_first_kernel,
        out_shape=(
            jax.ShapeDtypeStruct((n * rows, width), x.dtype),
            jax.ShapeDtypeStruct((shards,) + gains.shape, gains.dtype),
        ),
        in_specs=[VMEM_SPEC, VMEM_SPEC],
        out_specs=(VMEM_SPEC, VMEM_SPEC),
        scratch_shapes=semaphores(n - 1, n - 1, shards - 1, shards - 1),
        compiler_params=communicating(call_id),
        name="gather_first",
    )(x, gains)


def scatter_kernel(p_ref, o_ref, landed, send_sem, recv_sem):
    greet("seq")
    rows = o_ref.shape[0]
    copies = start_to_peers(
        "seq",
        lambda peer: p_ref.at[block_of(peer, rows)],
        lambda step: landed.at[step - 1],
        send_sem,
        recv_sem,
    )
    o_ref[...] = p_ref[block_of(lax.axis_index("seq"), rows), :].astype(F32)
    for step, copy in enumerate(copies):
        copy.wait()
        o_ref[...] += landed[step].astype(F32)


def scatter_sum(partial, n, call_id):
    total, width = partial.shape
    rows = total // n
    return pl.pallas_call(
        scatter_kernel,
        out_shape=jax.ShapeDtypeStruct((rows, width), F32),
        in_specs=[VMEM_SPEC],
        out_specs=VMEM_SPEC,
        scratch_shapes=[pltpu.VMEM((n - 1, rows, width), partial.dtype)] + semaphores(n - 1, n - 1),
        compiler_params=communicating(call_id),
        name=f"scatter_sum_{call_id}",
    )(partial)


def scatter_last_kernel(
    p_ref, small_ref, o_ref, small_out, landed, part_landed, part_sum, row_landed,
    send, recv, part_send, part_recv, row_send, row_recv,
):
    greet("seq", "fsdp")
    rows = o_ref.shape[0]
    part_copies = start_to_peers(
        "fsdp",
        lambda peer: small_ref.at[peer],
        lambda step: part_landed.at[step - 1],
        part_send,
        part_recv,
    )
    copies = start_to_peers(
        "seq",
        lambda peer: p_ref.at[block_of(peer, rows)],
        lambda step: landed.at[step - 1],
        send,
        recv,
    )
    total = small_ref[lax.axis_index("fsdp")]
    for step, copy in enumerate(part_copies):
        copy.wait()
        total = total + part_landed[step]
    part_sum[...] = total
    o_ref[...] = p_ref[block_of(lax.axis_index("seq"), rows), :].astype(F32)
    row_copies = start_to_peers(
        "seq", lambda peer: part_sum, lambda step: row_landed.at[step - 1], row_send, row_recv
    )
    for step, copy in enumerate(copies):
        copy.wait()
        o_ref[...] += landed[step].astype(F32)
    for step, copy in enumerate(row_copies):
        copy.wait()
        total = total + row_landed[step]
    small_out[...] = total


def scatter_last(partial, small, n, shards, call_id):
    total, width = partial.shape
    rows = total // n
    piece = small.shape[1:]
    return pl.pallas_call(
        scatter_last_kernel,
        out_shape=(jax.ShapeDtypeStruct((rows, width), F32), jax.ShapeDtypeStruct(piece, F32)),
        in_specs=[VMEM_SPEC, VMEM_SPEC],
        out_specs=(VMEM_SPEC, VMEM_SPEC),
        scratch_shapes=[
            pltpu.VMEM((n - 1, rows, width), partial.dtype),
            pltpu.VMEM((shards - 1,) + piece, F32),
            pltpu.VMEM(piece, F32),
            pltpu.VMEM((n - 1,) + piece, F32),
        ]
        + semaphores(n - 1, n - 1, shards - 1, shards - 1, n - 1, n - 1),
        compiler_params=communicating(call_id),
        name="scatter_last",
    )(partial, small)


def rope(values, cosine, sine):
    return values * cosine + pltpu.roll(values, HEAD_SIZE // 2, 1) * sine


def rope_back(grad, cosine, sine):
    return grad * cosine - pltpu.roll(grad, HEAD_SIZE // 2, 1) * sine


def head_columns(index):
    return pl.ds(pl.multiple_of(index * HEAD_SIZE, HEAD_SIZE), HEAD_SIZE)


def turned_block(shift):
    def block(i):
        return lax.rem(lax.axis_index("seq") + shift + i, lax.axis_size("seq"))

    return block


def forward_kernel(
    q_pre, k_pre, v_ref, gain_q, gain_k, cos_q, sin_q, cos_k, sin_k, place_k, place_q, start_q, cot,
    out_ref, p_ref, q_ref, k_ref, cot_all,
    v_turned, outs, cot_send, cot_recv, cot_local, send, recv, local,
):
    i, head = pl.program_id(0), pl.program_id(1)
    n, heads = pl.num_programs(0), pl.num_programs(1)
    seq = lax.axis_size("seq")
    me = lax.axis_index("seq")
    kv = outs.shape[1] // GROUP
    rows = cot.shape[0]
    mine = block_of(me, rows)

    def cot_copies():
        return [
            pltpu.make_async_remote_copy(
                src_ref=cot,
                dst_ref=cot_all.at[mine],
                send_sem=cot_send.at[step - 1],
                recv_sem=cot_recv.at[step - 1],
                device_id={"seq": lax.rem(me + step, seq)},
                device_id_type=MESH,
            )
            for step in range(1, seq)
        ]

    cot_own = pltpu.make_async_copy(cot, cot_all.at[mine], cot_local)

    def out_copy(step, which):
        return pltpu.make_async_remote_copy(
            src_ref=outs.at[step, which],
            dst_ref=out_ref.at[:, head_columns(me * heads + which)],
            send_sem=send.at[step, which],
            recv_sem=recv.at[step, which],
            device_id={"seq": lax.rem(me + 1 + step, seq)},
            device_id_type=MESH,
        )

    def own_copy(which):
        return pltpu.make_async_copy(
            outs.at[seq - 1, which], out_ref.at[:, head_columns(me * heads + which)], local.at[which]
        )

    @pl.when((i == 0) & (head == 0))
    def _():
        greet("seq")
        for copy in cot_copies():
            copy.start()
        cot_own.start()
        for which in range(kv):
            own = pl.ds(which * HEAD_SIZE, HEAD_SIZE)
            pre = k_pre[:, own]
            k_ref[:, own] = rope(
                pre * inverse_rms(pre) * gain_k[...], cos_k[...], sin_k[...]
            ).astype(BF16)
            v_turned[which] = v_ref[:, own].astype(F32).T.astype(BF16)

    @pl.when((head > 0) & (i < n - 1))
    def _():
        out_copy(i, head - 1).start()

    @pl.when((head == 0) & (i > 0))
    def _():
        out_copy(i - 1, heads - 1).start()

    pre = q_pre[...]
    query = rope(pre * inverse_rms(pre) * gain_q[...], cos_q[...], sin_q[...]).astype(BF16)
    q_ref[...] = query
    pair = head // GROUP
    scores = back_matmul(k_ref[:, head_columns(pair)], query) * SCALE
    keys = place_k[...]
    allowed = (keys <= place_q[...]) & (keys >= start_q[...])
    scores = jnp.where(allowed, scores, MASKED)
    top = jnp.max(scores, axis=0, keepdims=True)
    weights = jnp.exp(scores - top)
    total = jnp.sum(weights, axis=0, keepdims=True)
    weights = (weights * (1.0 / total)).astype(BF16)
    p_ref[0] = weights
    outs[i, head] = matrix_product(v_turned[pair], weights).T.astype(BF16)

    @pl.when((i == n - 1) & (head == heads - 1))
    def _():
        for which in range(outs.shape[1]):
            own_copy(which).start()
        for copy in cot_copies():
            copy.wait()
        cot_own.wait()
        for step in range(seq - 1):
            for which in range(outs.shape[1]):
                out_copy(step, which).wait()
        for which in range(outs.shape[1]):
            own_copy(which).wait()


def attend_forward(
    q_pre, k_pre, value, gain_q, gain_k, cosine, sine, place, start, cotangent, n, call_id
):
    rows = q_pre.shape[0]
    heads = q_pre.shape[1] // HEAD_SIZE
    kv = heads // GROUP
    block = rows // n
    width = cotangent.shape[1]
    turn = turned_block(1)
    q_spec = pl.BlockSpec((block, HEAD_SIZE), lambda i, h: (turn(i), h))
    k_spec = pl.BlockSpec((rows, kv * HEAD_SIZE), lambda i, h: (0, 0))
    gain_spec = pl.BlockSpec((1, HEAD_SIZE), lambda i, h: (0, 0))
    trig_q = pl.BlockSpec((block, HEAD_SIZE), lambda i, h: (turn(i), 0))
    trig_k = pl.BlockSpec((rows, HEAD_SIZE), lambda i, h: (0, 0))
    column = pl.BlockSpec((rows, 1), lambda i, h: (0, 0))
    row = pl.BlockSpec((1, block), lambda i, h: (0, turn(i)))
    return pl.pallas_call(
        forward_kernel,
        grid=(n, heads),
        out_shape=(
            jax.ShapeDtypeStruct((block, n * heads * HEAD_SIZE), BF16),
            jax.ShapeDtypeStruct((heads, rows, rows), BF16),
            jax.ShapeDtypeStruct((rows, heads * HEAD_SIZE), BF16),
            jax.ShapeDtypeStruct((rows, kv * HEAD_SIZE), BF16),
            jax.ShapeDtypeStruct((rows, width), BF16),
        ),
        in_specs=[
            q_spec, k_spec, k_spec, gain_spec, gain_spec, trig_q, trig_q, trig_k, trig_k,
            column, row, row, ANY_SPEC,
        ],
        out_specs=(
            ANY_SPEC,
            pl.BlockSpec((1, rows, block), lambda i, h: (h, 0, turn(i))),
            q_spec,
            k_spec,
            ANY_SPEC,
        ),
        scratch_shapes=[
            pltpu.VMEM((kv, HEAD_SIZE, rows), BF16),
            pltpu.VMEM((n, heads, block, HEAD_SIZE), BF16),
            pltpu.SemaphoreType.DMA((n - 1,)),
            pltpu.SemaphoreType.DMA((n - 1,)),
            pltpu.SemaphoreType.DMA,
            pltpu.SemaphoreType.DMA((n - 1, heads)),
            pltpu.SemaphoreType.DMA((n - 1, heads)),
            pltpu.SemaphoreType.DMA((heads,)),
        ],
        compiler_params=communicating(call_id),
        name="attend_forward",
    )(
        q_pre, k_pre, value, gain_q, gain_k, cosine, sine, cosine, sine,
        place[:, None], place[None, :], start[None, :], cotangent,
    )


def backward_kernel(
    p_ref, q_ref, k_ref, v_ref, q_pre, k_pre, gain_q, gain_k, cos_q, sin_q, cos_k, sin_k,
    grad_own, bulk,
    dq_ref, dk_ref, dv_ref, dgain_q, dgain_k, bulk_landed,
    k_turned, dk_sum, dv_sum, grads, send, recv, local, bulk_send, bulk_recv,
):
    i, head = pl.program_id(0), pl.program_id(1)
    n, heads = pl.num_programs(0), pl.num_programs(1)
    seq = lax.axis_size("seq")
    me = lax.axis_index("seq")
    kv = k_turned.shape[0]
    rows = grads.shape[1]
    span = grads.shape[2]
    first = (i == 0) & (head == 0)
    last = (i == n - 1) & (head == heads - 1)

    def grad_copy(step):
        peer = lax.rem(me + step, seq)
        return pltpu.make_async_remote_copy(
            src_ref=grad_own.at[:, block_of(peer, span)],
            dst_ref=grads.at[step],
            send_sem=send.at[step - 1],
            recv_sem=recv.at[step - 1],
            device_id={"seq": peer},
            device_id_type=MESH,
        )

    def bulk_copy(step):
        peer = lax.rem(me + step, seq)
        return pltpu.make_async_remote_copy(
            src_ref=bulk.at[block_of(peer, rows)],
            dst_ref=bulk_landed.at[step - 1],
            send_sem=bulk_send.at[step - 1],
            recv_sem=bulk_recv.at[step - 1],
            device_id={"seq": peer},
            device_id_type=MESH,
        )

    own_copy = pltpu.make_async_copy(grad_own.at[:, block_of(me, span)], grads.at[0], local)

    @pl.when(first)
    def _():
        greet("seq")
        own_copy.start()
        for step in range(1, seq):
            grad_copy(step).start()
        for step in range(1, seq):
            bulk_copy(step).start()
        dgain_q[...] = jnp.zeros_like(dgain_q)
        dgain_k[...] = jnp.zeros_like(dgain_k)
        dk_sum[...] = jnp.zeros_like(dk_sum)
        dv_sum[...] = jnp.zeros_like(dv_sum)
        for which in range(kv):
            own = pl.ds(which * HEAD_SIZE, HEAD_SIZE)
            k_turned[which] = k_ref[:, own].astype(F32).T.astype(BF16)
        own_copy.wait()

    for step in range(1, seq):
        @pl.when((head == 0) & (i == seq - step))
        def _():
            grad_copy(step).wait_recv()

    slot = lax.rem(seq - i, seq)
    pair = head // GROUP
    rounded = p_ref[0]
    weights = rounded.astype(F32)
    grad = grads[slot, :, head_columns(head)]
    grad_weights = back_matmul(v_ref[:, head_columns(pair)], grad)
    delta = jnp.sum(weights * grad_weights, axis=0, keepdims=True)
    grad_scores = (weights * (grad_weights - delta)).astype(BF16)
    dk_sum[pair] += matrix_product(grad_scores, q_ref[...])
    dv_sum[pair] += matrix_product(rounded, grad)
    dq = (matrix_product(k_turned[pair], grad_scores).T * SCALE).astype(BF16).astype(F32)
    dq, gain_rows = rms_backward(q_pre[...], gain_q[...], rope_back(dq, cos_q[...], sin_q[...]))
    dq_ref[...] = dq.astype(BF16)
    dgain_q[...] += jnp.sum(gain_rows, axis=0, keepdims=True)

    @pl.when(last)
    def _():
        for which in range(kv):
            own = pl.ds(which * HEAD_SIZE, HEAD_SIZE)
            dk = (dk_sum[which] * SCALE).astype(BF16).astype(F32)
            dk, gain_rows = rms_backward(
                k_pre[:, own], gain_k[...], rope_back(dk, cos_k[...], sin_k[...])
            )
            dk_ref[:, own] = dk.astype(BF16)
            dgain_k[...] += jnp.sum(gain_rows, axis=0, keepdims=True)
            dv_ref[:, own] = dv_sum[which].astype(BF16)
        for step in range(1, seq):
            grad_copy(step).wait_send()
            bulk_copy(step).wait()


def attend_backward(
    weights, query, key, value, grad_own, bulk, q_pre, k_pre, gain_q, gain_k, cosine, sine, n, call_id
):
    rows = q_pre.shape[0]
    heads = q_pre.shape[1] // HEAD_SIZE
    kv = heads // GROUP
    block = rows // n
    turn = turned_block(0)
    q_spec = pl.BlockSpec((block, HEAD_SIZE), lambda i, h: (turn(i), h))
    k_spec = pl.BlockSpec((rows, kv * HEAD_SIZE), lambda i, h: (0, 0))
    gain_spec = pl.BlockSpec((1, HEAD_SIZE), lambda i, h: (0, 0))
    trig_q = pl.BlockSpec((block, HEAD_SIZE), lambda i, h: (turn(i), 0))
    trig_k = pl.BlockSpec((rows, HEAD_SIZE), lambda i, h: (0, 0))
    return pl.pallas_call(
        backward_kernel,
        grid=(n, heads),
        out_shape=(
            jax.ShapeDtypeStruct((rows, heads * HEAD_SIZE), BF16),
            jax.ShapeDtypeStruct((rows, kv * HEAD_SIZE), BF16),
            jax.ShapeDtypeStruct((rows, kv * HEAD_SIZE), BF16),
            jax.ShapeDtypeStruct((1, HEAD_SIZE), F32),
            jax.ShapeDtypeStruct((1, HEAD_SIZE), F32),
            jax.ShapeDtypeStruct((n - 1, block, bulk.shape[1]), BF16),
        ),
        in_specs=[
            pl.BlockSpec((1, rows, block), lambda i, h: (h, 0, turn(i))),
            q_spec, k_spec, k_spec, q_spec, k_spec, gain_spec, gain_spec,
            trig_q, trig_q, trig_k, trig_k, ANY_SPEC, ANY_SPEC,
        ],
        out_specs=(q_spec, k_spec, k_spec, gain_spec, gain_spec, ANY_SPEC),
        scratch_shapes=[
            pltpu.VMEM((kv, HEAD_SIZE, rows), BF16),
            pltpu.VMEM((kv, rows, HEAD_SIZE), F32),
            pltpu.VMEM((kv, rows, HEAD_SIZE), F32),
            pltpu.VMEM((n, block, heads * HEAD_SIZE), BF16),
            pltpu.SemaphoreType.DMA((n - 1,)),
            pltpu.SemaphoreType.DMA((n - 1,)),
            pltpu.SemaphoreType.DMA,
            pltpu.SemaphoreType.DMA((n - 1,)),
            pltpu.SemaphoreType.DMA((n - 1,)),
        ],
        compiler_params=communicating(call_id),
        name="attend_backward",
    )(
        weights, query, key, value, q_pre, k_pre, gain_q, gain_k, cosine, sine, cosine, sine,
        grad_own, bulk,
    )


def on_device(
    tokens, lengths, packing, norm_in, w_query, key_projection, value_projection, norm_query,
    norm_key, w_out, norm_post, w_gate, w_up, w_down, cotangent,
):
    n = lax.axis_size("seq")
    shards = lax.axis_size("fsdp")
    me = lax.axis_index("seq")
    resident = tokens.shape[1]
    width = tokens.shape[2]
    rows = resident * n
    heads = HQ // n
    kv = KEY_VALUE_HEADS // n
    hidden_piece = w_down.shape[0] // n

    def columns(weight, pieces):
        size = weight.shape[1] // pieces
        return lax.dynamic_slice_in_dim(weight, me * size, size, axis=1)

    def spread_columns(weight):
        pieces = weight.reshape(weight.shape[0], shards, n, hidden_piece)
        return lax.dynamic_index_in_dim(pieces, me, axis=2, keepdims=False).reshape(
            weight.shape[0], shards * hidden_piece
        )

    def tile_of(values):
        pad = 1024 - values.shape[-1]
        values = jnp.concatenate([values, jnp.zeros(values.shape[:-1] + (pad,), F32)], axis=-1)
        return values.reshape(values.shape[:-1] + (8, 128))

    part, small = norm_in.shape[0], norm_query.shape[0]
    whole, gains = gather_first(
        tokens[0],
        tile_of(jnp.concatenate([norm_in, norm_post, norm_query, norm_key]).astype(F32)),
        n, shards, 0,
    )
    gains = gains.reshape(shards, -1)
    gain_in = gains[:, :part].reshape(1, -1)
    gain_post = gains[:, part : 2 * part].reshape(1, -1)
    gain_query = gains[:, 2 * part : 2 * part + small].reshape(1, -1)
    gain_key = gains[:, 2 * part + small : 2 * part + 2 * small].reshape(1, -1)

    qkv_weight = lax.all_gather(
        jnp.concatenate(
            [columns(w_query, n), columns(key_projection, n), columns(value_projection, n)], axis=1
        ),
        "fsdp", axis=0, tiled=True,
    )
    out_weight = lax.all_gather(w_out, "fsdp", axis=0, tiled=True)
    gate_up_weight = lax.all_gather(
        jnp.concatenate([spread_columns(w_gate), spread_columns(w_up)], axis=1), "fsdp", axis=0, tiled=True
    )
    down_weight = lax.all_gather(
        lax.dynamic_slice_in_dim(w_down, me * hidden_piece, hidden_piece, axis=0),
        "fsdp", axis=0, tiled=True,
    )

    order = packing[0]
    places = jnp.arange(rows, dtype=jnp.int32)
    place = jnp.sum(jnp.where(order[None, :] == places[:, None], places[None, :], 0), axis=1)
    ends = jnp.cumsum(lengths[0])
    start = jnp.sum(jnp.where(place[:, None] >= ends[None, :], lengths[0][None, :], 0), axis=1)
    half = HEAD_SIZE // 2
    inv_freq = ROPE_BASE ** (-jnp.arange(half, dtype=F32) / half)
    angles = (place - start).astype(F32)[:, None] * inv_freq[None, :]
    cosine, sine = jnp.cos(angles), jnp.sin(angles)
    cosine = jnp.concatenate([cosine, cosine], axis=1)
    sine = jnp.concatenate([-sine, sine], axis=1)

    inputs = tokens[0].astype(F32)
    whole_f32 = whole.astype(F32)
    unit = whole_f32 * inverse_rms(whole_f32)
    normalized = (unit * gain_in).astype(BF16)
    qkv = matrix_product(normalized, qkv_weight)
    split = heads * HEAD_SIZE
    q_pre = qkv[:, :split]
    k_pre = qkv[:, split : split + kv * HEAD_SIZE]
    value = qkv[:, split + kv * HEAD_SIZE :].astype(BF16)
    attended, weights, query, key, grad_mlp = attend_forward(
        q_pre, k_pre, value, gain_query, gain_key, cosine, sine, place, start, cotangent[0], n, 1
    )
    middle = inputs + matrix_product(attended, out_weight)
    normed_post_mine = (middle * inverse_rms(middle) * gain_post).astype(BF16)
    normed_post = gather_rows(normed_post_mine, n, 2)

    gate_up = matrix_product(normed_post, gate_up_weight)
    units = shards * hidden_piece
    gate, up = gate_up[:, :units], gate_up[:, units:]
    logistic = 1.0 / (1.0 + jnp.exp(-gate))
    hidden = (gate / (1.0 + jnp.exp(-gate)) * up).astype(BF16)
    mlp_partial = matrix_product(hidden, down_weight).astype(BF16)

    grad_hidden = back_matmul(grad_mlp, down_weight)
    grad_down = outer_sum(hidden, grad_mlp).astype(BF16)
    grad_gate = (grad_hidden * up * (logistic + gate * logistic * (1.0 - logistic))).astype(BF16)
    grad_up = (grad_hidden * gate * logistic).astype(BF16)
    grad_gate_up = jnp.concatenate([grad_gate, grad_up], axis=1)
    grad_gate_up_weight = outer_sum(normed_post, grad_gate_up).astype(BF16)
    grad_partial, grad_down, grad_gate_up_weight = lax.optimization_barrier(
        (back_matmul(grad_gate_up, gate_up_weight).astype(BF16), grad_down, grad_gate_up_weight)
    )
    grad_normed_post = scatter_sum(grad_partial, n, 3)
    grad_middle, gain_rows = rms_backward(middle, gain_post, grad_normed_post)
    grad_middle = cotangent[0].astype(F32) + grad_middle
    grad_gain_post = jnp.sum(gain_rows, axis=0)
    grad_branch = grad_middle.astype(BF16)
    grad_out = outer_sum(attended, grad_branch).astype(BF16)
    grad_attended = back_matmul(grad_branch, out_weight).astype(BF16)
    grad_q, grad_k, grad_v, grad_gain_query, grad_gain_key, mlp_landed = attend_backward(
        weights, query, key, value, grad_attended, mlp_partial, q_pre, k_pre, gain_query, gain_key,
        cosine, sine, n, 4,
    )
    result = middle + lax.dynamic_slice_in_dim(mlp_partial, me * resident, resident).astype(F32)
    output = (result + jnp.sum(mlp_landed.astype(F32), axis=0)).astype(BF16)[None]
    grad_qkv = jnp.concatenate([grad_q, grad_k, grad_v], axis=1)
    grad_qkv_weight = outer_sum(normalized, grad_qkv).astype(BF16)
    partial = back_matmul(grad_qkv, qkv_weight)
    grad_gain_in = jnp.sum(partial * unit, axis=0)
    small_grads = [grad_gain_in, grad_gain_post, grad_gain_query, grad_gain_key]
    small_grads = tile_of(jnp.concatenate([g.reshape(shards, -1) for g in small_grads], axis=1))
    grad_normed, gain_shares = scatter_last(partial.astype(BF16), small_grads, n, shards, 5)
    gain_shares = gain_shares.reshape(-1)
    grad_inputs, _ = rms_backward(inputs, gain_in, grad_normed)
    input_grad = (grad_middle + grad_inputs).astype(BF16)[None]

    def shared(grad):
        return lax.all_gather(
            lax.psum_scatter(grad, "fsdp", scatter_dimension=0, tiled=True), "seq", axis=0
        ).astype(F32)

    def beside(pieces):
        return jnp.swapaxes(pieces, 0, 1).reshape(pieces.shape[1], -1)

    final_down = shared(grad_down).reshape(-1, width)
    gate_up_all = shared(grad_gate_up_weight)

    def spread_back(pieces):
        pieces = pieces.reshape(n, pieces.shape[1], shards, hidden_piece)
        return jnp.transpose(pieces, (1, 2, 0, 3)).reshape(pieces.shape[1], -1)

    final_gate = spread_back(gate_up_all[:, :, :units])
    final_up = spread_back(gate_up_all[:, :, units:])
    final_out = lax.psum(
        lax.psum_scatter(grad_out, "fsdp", scatter_dimension=0, tiled=True), "seq"
    ).astype(F32)
    qkv_all = shared(grad_qkv_weight)
    final_query = beside(qkv_all[:, :, :split])
    final_key = beside(qkv_all[:, :, split : split + kv * HEAD_SIZE])
    final_value = beside(qkv_all[:, :, split + kv * HEAD_SIZE :])

    return (
        output,
        input_grad,
        gain_shares[:part],
        final_query,
        final_key,
        final_value,
        gain_shares[2 * part : 2 * part + small],
        gain_shares[2 * part + small : 2 * part + 2 * small],
        final_out,
        gain_shares[part : 2 * part],
        final_gate,
        final_up,
        final_down,
    )


def solution(mesh):
    flat, wide = P("fsdp"), P("fsdp", None)
    whole = P("fsdp", "seq", None)
    in_specs = (
        whole, wide, wide, flat, wide, wide, wide, flat, flat, wide, flat, wide, wide, wide, whole,
    )
    out_specs = (whole, whole, flat, wide, wide, wide, flat, flat, wide, flat, wide, wide, wide)
    return jax.shard_map(
        on_device, mesh=mesh, in_specs=in_specs, out_specs=out_specs, check_vma=False
    )
```

time: 597 us -> 557 us (0.933)
  waiting for transfers between devices: 68.8 us -> 199 us
  blocking collectives: 102 us -> 10.5 us
  Pallas kernels: 274 us -> 202 us
    pallas_call x10 -> x6, Pallas kernels: 274 us -> 202 us  [the longest x1 41.1 us: attend_backward(): pl.pallas_call(backward_kernel, grid=(n, heads), out_shape=(jax.ShapeDtyp...]
    reduce_scatter x0 -> x1, waiting for transfers between devices: none -> 49.6 us  [on_device(): lax.psum_scatter(grad_out, 'fsdp', scatter_dimension=0, tiled=True)]
    psum x1 -> x0, blocking collectives: 40.7 us -> none  [on_device(): lax.psum(jnp.concatenate([grad_gain_in, grad_gain_post, grad_gain_query[0...]
    psum x0 -> x1, waiting for transfers between devices: none -> 32.6 us  [on_device(): lax.psum(lax.psum_scatter(grad_out, 'fsdp', scatter_dimension=0, tiled=Tr...]
    reduce_scatter x4 -> x3, waiting for transfers between devices: 44.7 us -> 69.5 us  [shared(): lax.psum_scatter(grad, 'fsdp', scatter_dimension=0, tiled=True)]
    unnamed x1 -> x0, blocking collectives: 19 us -> none
    all_to_all x1 -> x0, blocking collectives: 16.1 us -> none  [on_device(): lax.all_to_all(grad_out, 'seq', split_axis=1, concat_axis=0, tiled=True)]
    all_gather x2 -> x1, blocking collectives: 25.9 us -> 10.5 us  [shared(): lax.all_gather(lax.psum_scatter(grad, 'fsdp', scatter_dimension=0, tiled=...]
  transfers between devices with their start and end apart: 11 -> 11, of which waited for: 3 -> 7; matrix products, arithmetic and copies ran while one was open for 12% -> 14% of each run, Pallas kernels for 28% -> 24%
where the time goes in v2:
time: 557 us; the launch traced here: 550 us
  Pallas kernels  202 us (36%)
  waiting for transfers between devices  199 us (36%)
  matrix products  62.9 us (11%)
  local copies, waits for them, and re-layouts  36.9 us (7%)
  other arithmetic  22.9 us (4%)
  between operations  14.9 us (3%)
  blocking collectives  10.5 us (2%)
    reduce_scatter x3, waiting for transfers between devices, shared(): lax.psum_scatter(grad, 'fsdp', scatter_dimension=0, tiled=True)  69.5 us
    reduce_scatter x1, waiting for transfers between devices, on_device(): lax.psum_scatter(grad_out, 'fsdp', scatter_dimension=0, tiled=True)  49.6 us
    pallas_call x1, Pallas kernels, attend_backward(): pl.pallas_call(backward_kernel, grid=(n, heads), out_shape=(jax.ShapeDtyp...  41.1 us
    pallas_call x1, Pallas kernels, attend_forward(): pl.pallas_call(forward_kernel, grid=(n, heads), out_shape=(jax.ShapeDtype...  41.1 us
    all_gather x2, waiting for transfers between devices, shared(): lax.all_gather(lax.psum_scatter(grad, 'fsdp', scatter_dimension=0, tiled=...  35.1 us
    pallas_call x1, Pallas kernels, gather_first(): pl.pallas_call(gather_first_kernel, out_shape=(jax.ShapeDtypeStruct((n *...  32.7 us
    psum x1, waiting for transfers between devices, on_device(): lax.psum(lax.psum_scatter(grad_out, 'fsdp', scatter_dimension=0, tiled=Tr...  32.6 us
    pallas_call x1, Pallas kernels, scatter_last(): pl.pallas_call(scatter_last_kernel, out_shape=(jax.ShapeDtypeStruct((rows...  30.5 us
  transfers between devices with their start and end apart: 11, of which 7 were waited for; matrix products, arithmetic and copies ran while one was open for 14% of the time, Pallas kernels for 24%

profile of v2, /device:TPU:0, one launch (start us, length us, event | category | flops | bytes accessed | tf_op | source)
XLA Modules:
  0.0 549.7 jit_solution(13621943293447418153)
XLA Ops:
  14.0 32.7 %gather_first.1 = (bf16[1024,1024]{1,0:T(8,128)(2,1)}, f32[8,8,128]{2,1,0:T(8,128)}) custom-call(bf16[256,1024]{1,0:T(8,128)(2,1)} %bitcast.93, f32[8,128]{1,0:T(8,128)} %fusion.30.gains_ref), custom_call_target="tpu_custom_call" | custom-call | tf_op jit(solution)/shard_map/gather_first/pallas_call | solution.py:136
  47.5 2.1 fusion.4
  50.5 1.9 fusion.21
  52.4 1.3 pad_maximum_fusion.5
  55.9 4.0 fusion.15
  59.9 1.5 slice.82.q_pre
  61.4 1.1 slice.83.k_pre
  63.3 41.1 %attend_forward.1 = (bf16[256,2048]{1,0:T(8,128)(2,1)}, bf16[4,1024,1024]{2,1,0:T(8,128)(2,1)}, bf16[1024,512]{1,0:T(8,128)(2,1)}, bf16[1024,256]{1,0:T(8,128)(2,1)}, bf16[1024,1024]{1,0:T(8,128)(2,1)}) custom-call(f32[1024,512]{1,0:T(8,128)} %slice.82.q_pre, f32[1024,256]{1,0:T(8,128)} %slice.83.k_pre, bf16[1024,256]{1,0:T(8,128)(2,1)} %slice.108.v_ref, ...), custom_call_target="tpu_custom_call" | custom-call | tf_op jit(solution)/shard_map/attend_forward/pallas_call | solution.py:368
  104.4 3.9 multiply_reduce_fusion.2
  109.3 27.4 %gather_rows_2.1 = bf16[1024,1024]{1,0:T(8,128)(2,1)} custom-call(bf16[256,1024]{1,0:T(8,128)(2,1)} %multiply_convert_fusion.3.x_ref), custom_call_target="tpu_custom_call" | custom-call | tf_op jit(solution)/shard_map/gather_rows_2/pallas_call | solution.py:109
  136.7 8.9 %fusion.36 = f32[1024,1536]{1,0:T(8,128)} fusion(bf16[1024,1024]{1,0:T(8,128)(2,1)} %gather_rows_2.1, bf16[1024,1536]{0,1:T(8,128)(2,1)} %all-gather.14.cloned.1.call-done), kind=kOutput, calls=%fused_computation.96 | convolution fusion | flops 3221225472 | bytes 11534336 | tf_op jit(solution)/shard_map/dot_general | solution.py:25
  145.6 10.3 %all-gather.16.cloned.1.call-done = bf16[768,1024]{1,0:T(8,128)(2,1)} async-done(((bf16[96,1024]{1,0:T(8,128)(2,1)}), bf16[768,1024]{1,0:T(8,128)(2,1)}) %all-gather.16.cloned.1.call-update) | async-done | bytes 1572880 | tf_op jit(solution)/shard_map/all_gather | solution.py:600
  155.9 7.9 %multiply_convert_fusion.1 = (bf16[1024,768]{1,0:T(8,128)(2,1)S(1)}, bf16[1024,768]{1,0:T(8,128)(2,1)}, bf16[1024,768]{1,0:T(8,128)(2,1)S(1)}) fusion(f32[1024,1536]{1,0:T(8,128)} %fusion.36, bf16[1024,1024]{1,0:T(8,128)(2,1)} %get-tuple-element.37, bf16[768,1024]{1,0:T(8,128)(2,1)} %all-gather.16.cloned.1.call-done), kind=kOutput, calls=%fused_computation.14 | convolution fusion | flops 1623195648 | bytes 14680064 | tf_op jit(solution)/shard_map/dot_general | solution.py:33
  163.8 1.1 copy-done.27
  165.0 3.0 convolution_convert_fusion.5
  168.0 7.2 %convolution_convert_fusion.1 = bf16[1024,1536]{1,0:T(8,128)(2,1)} fusion(bf16[1024,1024]{1,0:T(8,128)(2,1)} %gather_rows_2.1, bf16[1024,768]{1,0:T(8,128)(2,1)} %get-tuple-element.80, bf16[1024,768]{1,0:T(8,128)(2,1)S(1)} %get-tuple-element.79), kind=kOutput, calls=%fused_computation.10 | convolution fusion | flops 3229089792 | bytes 8388608 | tf_op jit(solution)/shard_map/dot_general | solution.py:29
  175.1 7.4 %fusion.7.p_ref = bf16[1024,1024]{1,0:T(8,128)(2,1)} fusion(bf16[1024,1536]{0,1:T(8,128)(2,1)} %all-gather.14.cloned.1.call-done, bf16[1024,768]{1,0:T(8,128)(2,1)} %get-tuple-element.80, bf16[1024,768]{1,0:T(8,128)(2,1)S(1)} %get-tuple-element.79), kind=kOutput, calls=%fused_computation.21 | convolution fusion | flops 3228565504 | bytes 8388608 | tf_op jit(solution)/shard_map/dot_general | solution.py:33
  182.6 29.0 %scatter_sum_3.1 = f32[256,1024]{1,0:T(8,128)} custom-call(bf16[1024,1024]{1,0:T(8,128)(2,1)} %fusion.7.p_ref), custom_call_target="tpu_custom_call" | custom-call | tf_op jit(solution)/shard_map/scatter_sum_3/pallas_call | solution.py:169
  211.6 1.6 multiply_reduce_fusion
  215.1 3.2 convolution_convert_fusion.4.bulk
  218.3 2.3 convolution_convert_fusion.2.grad_own
  220.6 41.1 %attend_backward.1 = (bf16[1024,512]{1,0:T(8,128)(2,1)}, bf16[1024,256]{1,0:T(8,128)(2,1)}, bf16[1024,256]{1,0:T(8,128)(2,1)}, f32[1,128]{1,0:T(1,128)}, f32[1,1...) custom-call(bf16[4,1024,1024]{2,1,0:T(8,128)(2,1)} %get-tuple-element.34.p_ref, bf16[1024,512]{1,0:T(8,128)(2,1)} %get-tuple-element.35.q_ref, ...), custom_call_target="tpu_custom_call" | custom-call | tf_op jit(solution)/shard_map/attend_backward/pallas_call | solution.py:513
  261.7 1.5 constant_dynamic-update-slice_fusion.2
  263.4 1.4 copy-done.10
  264.7 4.1 convolution_convert_fusion.3
  270.3 33.2 %reduce-scatter.5.cloned.1.call-done = bf16[128,1024]{1,0:T(8,128)(2,1)} async-done(((bf16[1024,1024]{1,0:T(8,128)(2,1)}), bf16[128,1024]{1,0:T(8,128)(2,1)}) %reduce-scatter.5.cloned.1.call-update) | async-done | bytes 262160 | tf_op jit(solution)/shard_map/reduce_scatter | solution.py:675
  303.6 4.5 convolution_convert_fusion
  308.1 36.2 %reduce-scatter.9.cloned.1.call-done = bf16[128,1536]{1,0:T(8,128)(2,1)} async-done(((bf16[1024,1536]{1,0:T(8,128)(2,1)}), bf16[128,1536]{1,0:T(8,128)(2,1)}) %reduce-scatter.9.cloned.1.call-update) | async-done | bytes 393232 | tf_op jit(solution)/shard_map/reduce_scatter | solution.py:675
  344.7 6.7 %fusion.3 = (f32[1024]{0:T(1024)S(1)}, bf16[1024,1024]{1,0:T(8,128)(2,1)}) fusion(bf16[1024,1024]{1,0:T(8,128)(2,1)} %get-tuple-element.31, f32[1024]{0:T(1024)S(1)} %add_rsqrt_fusion, bf16[1024,1024]{1,0:T(8,128)(2,1)} %copy-done.10, bf16[1024,1024]{1,0:T(8,128)(2,1)} %all-gather.10.cloned.1.call-done), kind=kOutput, calls=%fused_computation.5 | convolution fusion | flops 2152725504 | bytes 8396800 | tf_op jit(solution)/shard_map/dot_general | solution.py:33
  354.1 30.5 %scatter_last.1 = (f32[256,1024]{1,0:T(8,128)}, f32[8,128]{1,0:T(8,128)}) custom-call(bf16[1024,1024]{1,0:T(8,128)(2,1)} %get-tuple-element.83.p_ref, f32[8,8,128]{2,1,0:T(8,128)} %bitcast.103), custom_call_target="tpu_custom_call" | custom-call | tf_op jit(solution)/shard_map/scatter_last/pallas_call | solution.py:222
  384.6 1.9 convert_reduce_fusion
  388.0 2.1 fusion.17
  390.1 1.1 fusion.18
  391.2 10.5 %all-gather.2 = bf16[384,1024]{1,0:T(8,128)(2,1)S(1)} all-gather(bf16[96,1024]{1,0:T(8,128)(2,1)} %reduce-scatter.11.cloned.1.call-done), channel_id=4, replica_groups=mesh['seq'=4,'fsdp'=8] {'seq'}, dimensions={0}, use_global_device_ids=true | all-gather | bytes 983040 | tf_op jit(solution)/shard_map/all_gather | solution.py:674
  401.7 1.3 reshape.221
  403.0 5.9 %all-gather.18.cloned.1.call-done = bf16[512,1024]{1,0:T(8,128)(2,1)} async-done(((bf16[128,1024]{1,0:T(8,128)(2,1)}), bf16[512,1024]{1,0:T(8,128)(2,1)}) %all-gather.18.cloned.1.call-update) | async-done | bytes 1048592 | tf_op jit(solution)/shard_map/all_gather | solution.py:674
  408.9 1.5 convert.8
  411.5 49.6 %reduce-scatter.7.cloned.1.call-done = bf16[256,1024]{1,0:T(8,128)(2,1)} async-done(((bf16[2048,1024]{1,0:T(8,128)(2,1)}), bf16[256,1024]{1,0:T(8,128)(2,1)}) %reduce-scatter.7.cloned.1.call-update) | async-done | bytes 524304 | tf_op jit(solution)/shard_map/reduce_scatter | solution.py:691
  463.0 29.2 %all-gather.20.cloned.1.call-done = bf16[512,1536]{1,0:T(8,128)(2,1)} async-done(((bf16[128,1536]{1,0:T(8,128)(2,1)}), bf16[512,1536]{1,0:T(8,128)(2,1)}) %all-gather.20.cloned.1.call-update) | async-done | bytes 1572880 | tf_op jit(solution)/shard_map/all_gather | solution.py:674
  492.2 3.3 fusion.33
  495.5 1.9 copy.64
  497.3 1.3 copy.58
  498.7 3.0 copy.61
  501.7 1.9 copy.65
  503.6 1.3 copy.60
  504.9 3.1 copy.62
  508.0 32.6 %all-reduce.3.cloned.1.call-done = bf16[256,1024]{1,0:T(8,128)(2,1)} async-done(((bf16[256,1024]{1,0:T(8,128)(2,1)}), bf16[256,1024]{1,0:T(8,128)(2,1)}) %all-reduce.3.cloned.1.call-update) | async-done | bytes 524304 | tf_op jit(solution)/shard_map/psum | solution.py:690
  540.6 2.1 convert_element_type.105
  (128 shorter events, 23.3 us)
Async XLA Ops:
  7.2 5.3 copy-start
  7.2 3.6 copy-start.8
  7.2 4.0 copy-start.9
  7.2 48.7 %all-gather.10.cloned.1.call-start = ((), (), s32[]{:S(2)}) async-start(), calls=%async_computation.4 | async-start | bytes 2359296 | tf_op jit(solution)/shard_map/all_gather | solution.py:590
  10.0 94.4 %all-gather.12.cloned.1.call-start = ((), (), s32[]{:S(2)}) async-start(), calls=%async_computation.5 | async-start | bytes 4718592 | tf_op jit(solution)/shard_map/all_gather | solution.py:596
  10.7 125.9 %all-gather.14.cloned.1.call-start = ((), (), s32[]{:S(2)}) async-start(), calls=%async_computation.6 | async-start | bytes 3538944 | tf_op jit(solution)/shard_map/all_gather | solution.py:597
  11.2 2.2 copy-start.16
  11.2 2.1 copy-start.17
  11.2 2.1 copy-start.18
  11.2 2.1 copy-start.19
  11.7 38.0 %copy-start.24 = (s32[1,1024]{1,0:T(1,128)S(1)}, s32[1,1024]{1,0:T(1,128)}, u32[]{:S(2)}) copy-start(s32[1,1024]{1,0:T(1,128)} %param.17) | copy-start | bytes 12292
  11.7 38.5 %copy-start.20 = (s32[1,8]{1,0:T(1,128)S(1)}, s32[1,8]{1,0:T(1,128)}, u32[]{:S(2)}) copy-start(s32[1,8]{1,0:T(1,128)} %param.16) | copy-start | bytes 100
  12.5 143.4 %all-gather.16.cloned.1.call-start = ((), (), s32[]{:S(2)}) async-start(), calls=%async_computation.7 | async-start | bytes 1769472 | tf_op jit(solution)/shard_map/all_gather | solution.py:600
  13.3 290.2 %reduce-scatter.5.cloned.1.call-start = ((), (), s32[]{:S(2)}) async-start(), calls=%async_computation.8 | async-start | bytes 2359296 | tf_op jit(solution)/shard_map/reduce_scatter | solution.py:675
  50.1 4.7 copy-start.13
  50.4 3.3 copy-start.14
  50.5 5.5 copy-start.5
  63.3 41.1 %copy-start.3 = (bf16[1,256,1024]{2,1,0:T(8,128)(2,1)S(1)}, bf16[1,256,1024]{2,1,0:T(8,128)(2,1)}, u32[]{:S(2)}) copy-start(bf16[1,256,1024]{2,1,0:T(8,128)(2,1)} %param.15) | copy-start | bytes 1572868
  155.9 9.1 %copy-start.22 = (bf16[1024,1024]{1,0:T(8,128)(2,1)S(1)}, bf16[1024,1024]{1,0:T(8,128)(2,1)}, u32[]{:S(2)}) copy-start(bf16[1024,1024]{1,0:T(8,128)(2,1)} %get-tuple-element.37) | copy-start | bytes 6291460
  163.8 1.1 copy-start.27
  182.5 30.7 %copy-start.7 = (bf16[1,256,1024]{2,1,0:T(8,128)(2,1)S(1)}, bf16[1,256,1024]{2,1,0:T(8,128)(2,1)}, u32[]{:S(2)}) copy-start(bf16[1,256,1024]{2,1,0:T(8,128)(2,1)} %param.29) | copy-start | bytes 1572868
  211.6 1.6 copy-start.2
  213.2 1.4 copy-start.23
  213.2 1.9 copy-start.28
  215.1 3.2 copy-start.21
  261.7 1.5 copy-start.12
  261.7 1.6 copy-start.11
  261.7 3.0 copy-start.6
  263.4 1.4 copy-start.10
  268.9 75.5 %reduce-scatter.9.cloned.1.call-start = ((), (), s32[]{:S(2)}) async-start(), calls=%async_computation.11 | async-start | bytes 3538944 | tf_op jit(solution)/shard_map/reduce_scatter | solution.py:675
  269.5 121.8 %reduce-scatter.11.cloned.1.call-start = ((), (), s32[]{:S(2)}) async-start(), calls=%async_computation.12 | async-start | bytes 1769472 | tf_op jit(solution)/shard_map/reduce_scatter | solution.py:675
  270.2 138.7 %all-gather.18.cloned.1.call-start = ((), (), s32[]{:S(2)}) async-start(), calls=%async_computation.13 | async-start | bytes 1310720 | tf_op jit(solution)/shard_map/all_gather | solution.py:674
  303.5 157.6 %reduce-scatter.7.cloned.1.call-start = ((), (), s32[]{:S(2)}) async-start(), calls=%async_computation.9 | async-start | bytes 4718592 | tf_op jit(solution)/shard_map/reduce_scatter | solution.py:691
  308.1 184.1 %all-gather.20.cloned.1.call-start = ((), (), s32[]{:S(2)}) async-start(), calls=%async_computation.14 | async-start | bytes 1966080 | tf_op jit(solution)/shard_map/all_gather | solution.py:674
  344.4 7.5 %copy-start.26 = (f32[1,128]{1,0:T(1,128)S(1)}, f32[1,128]{1,0:T(1,128)}, u32[]{:S(2)}) copy-start(f32[1,128]{1,0:T(1,128)} %get-tuple-element.43) | copy-start | bytes 1540
  344.4 8.2 %copy-start.25 = (f32[1,128]{1,0:T(1,128)S(1)}, f32[1,128]{1,0:T(1,128)}, u32[]{:S(2)}) copy-start(f32[1,128]{1,0:T(1,128)} %get-tuple-element.44) | copy-start | bytes 1540
  344.4 196.2 %all-reduce.3.cloned.1.call-start = ((), (), s32[]{:S(2)}) async-start(), calls=%async_computation.10 | async-start | bytes 1048576 | tf_op jit(solution)/shard_map/psum | solution.py:690
  384.6 1.9 copy-start.4
  384.6 2.3 copy-start.15
  504.9 37.8 %copy-start.1 = (bf16[384,1024]{1,0:T(8,128)(2,1)S(1)}, bf16[384,1024]{1,0:T(8,128)(2,1)}, u32[]{:S(2)}) copy-start(bf16[384,1024]{1,0:T(8,128)(2,1)} %param.28) | copy-start | bytes 2359300
Sparse Core Ops, SparseCore 0:
  10.2 32.1 all-gather.9
  44.0 46.1 all-gather.11
  92.3 37.9 all-gather.13
  132.4 23.4 all-gather.15
  269.0 34.4 reduce-scatter.4
  305.7 38.6 reduce-scatter.8
  347.2 33.8 reduce-scatter.10
  383.0 25.8 all-gather.17
  411.2 49.8 reduce-scatter.6
  462.8 29.3 all-gather.19
  495.2 45.3 all-reduce.2

commit v3 on v2

--- a/solution.py
+++ b/solution.py
@@ -6,6 +6,7 @@
 from jax.experimental import pallas as pl
 from jax.experimental.pallas import tpu as pltpu
 from jax.sharding import PartitionSpec as P
+
 
 HQ = 16
 KEY_VALUE_HEADS = 8
@@ -113,7 +114,6 @@
         out_specs=VMEM_SPEC,
         scratch_shapes=semaphores(n - 1, n - 1),
         compiler_params=communicating(call_id),
-        name=f"gather_rows_{call_id}",
     )(x)
 
 
@@ -173,15 +173,16 @@
         out_specs=VMEM_SPEC,
         scratch_shapes=[pltpu.VMEM((n - 1, rows, width), partial.dtype)] + semaphores(n - 1, n - 1),
         compiler_params=communicating(call_id),
-        name=f"scatter_sum_{call_id}",
     )(partial)
 
 
 def scatter_last_kernel(
-    p_ref, small_ref, o_ref, small_out, landed, part_landed, part_sum, row_landed,
-    send, recv, part_send, part_recv, row_send, row_recv,
+    p_ref, small_ref, down_ref, gate_up_ref, o_ref, small_out, down_all, gate_up_all,
+    landed, part_landed, part_sum, row_landed,
+    send, recv, part_send, part_recv, row_send, row_recv, down_send, down_recv, wide_send, wide_recv,
 ):
     greet("seq", "fsdp")
+    me = lax.axis_index("seq")
     rows = o_ref.shape[0]
     part_copies = start_to_peers(
         "fsdp",
@@ -202,10 +203,17 @@
         copy.wait()
         total = total + part_landed[step]
     part_sum[...] = total
-    o_ref[...] = p_ref[block_of(lax.axis_index("seq"), rows), :].astype(F32)
+    o_ref[...] = p_ref[block_of(me, rows), :].astype(F32)
     row_copies = start_to_peers(
         "seq", lambda peer: part_sum, lambda step: row_landed.at[step - 1], row_send, row_recv
     )
+    share_copies = start_to_peers(
+        "seq", lambda peer: down_ref, lambda step: down_all.at[me], down_send, down_recv
+    ) + start_to_peers(
+        "seq", lambda peer: gate_up_ref, lambda step: gate_up_all.at[me], wide_send, wide_recv
+    )
+    down_all[me] = down_ref[...]
+    gate_up_all[me] = gate_up_ref[...]
     for step, copy in enumerate(copies):
         copy.wait()
         o_ref[...] += landed[step].astype(F32)
@@ -213,27 +221,125 @@
         copy.wait()
         total = total + row_landed[step]
     small_out[...] = total
-
-
-def scatter_last(partial, small, n, shards, call_id):
+    for copy in share_copies:
+        copy.wait()
+
+
+def scatter_last(partial, small, down, gate_up, n, shards, call_id):
     total, width = partial.shape
     rows = total // n
     piece = small.shape[1:]
     return pl.pallas_call(
         scatter_last_kernel,
-        out_shape=(jax.ShapeDtypeStruct((rows, width), F32), jax.ShapeDtypeStruct(piece, F32)),
-        in_specs=[VMEM_SPEC, VMEM_SPEC],
-        out_specs=(VMEM_SPEC, VMEM_SPEC),
+        out_shape=(
+            jax.ShapeDtypeStruct((rows, width), F32),
+            jax.ShapeDtypeStruct(piece, F32),
+            jax.ShapeDtypeStruct((n,) + down.shape, BF16),
+            jax.ShapeDtypeStruct((n,) + gate_up.shape, BF16),
+        ),
+        in_specs=[VMEM_SPEC] * 4,
+        out_specs=(VMEM_SPEC,) * 4,
         scratch_shapes=[
             pltpu.VMEM((n - 1, rows, width), partial.dtype),
             pltpu.VMEM((shards - 1,) + piece, F32),
             pltpu.VMEM(piece, F32),
             pltpu.VMEM((n - 1,) + piece, F32),
         ]
-        + semaphores(n - 1, n - 1, shards - 1, shards - 1, n - 1, n - 1),
+        + semaphores(n - 1, n - 1, shards - 1, shards - 1, *([n - 1] * 6)),
         compiler_params=communicating(call_id),
         name="scatter_last",
-    )(partial, small)
+    )(partial, small, down, gate_up)
+
+
+def finish_kernel(
+    qkv_ref, out_ref, q_final, k_final, v_final, out_final,
+    qkv_landed, out_landed, out_mine, out_back,
+    qkv_send, qkv_recv, first_send, first_recv, second_send, second_recv,
+):
+    greet("seq")
+    n = lax.axis_size("seq")
+    me = lax.axis_index("seq")
+    piece = out_mine.shape[0]
+    split = q_final.shape[1] // n
+    narrow = k_final.shape[1] // n
+    first = start_to_peers(
+        "seq",
+        lambda peer: out_ref.at[block_of(peer, piece)],
+        lambda step: out_landed.at[step - 1],
+        first_send,
+        first_recv,
+    )
+    beside = start_to_peers(
+        "seq", lambda peer: qkv_ref, lambda step: qkv_landed.at[step - 1], qkv_send, qkv_recv
+    )
+
+    def place(values, owner):
+        values = values.astype(F32)
+        q_final[:, block_of(owner, split)] = values[:, :split]
+        k_final[:, block_of(owner, narrow)] = values[:, split : split + narrow]
+        v_final[:, block_of(owner, narrow)] = values[:, split + narrow :]
+
+    total = out_ref[block_of(me, piece), :].astype(F32)
+    for step, copy in enumerate(first):
+        copy.wait()
+        total = total + out_landed[step].astype(F32)
+    out_mine[...] = total.astype(BF16)
+    out_final[block_of(me, piece), :] = out_mine[...].astype(F32)
+    place(qkv_ref[...], me)
+    second = start_to_peers(
+        "seq", lambda peer: out_mine, lambda step: out_back.at[step - 1], second_send, second_recv
+    )
+    for step, copy in enumerate(beside):
+        copy.wait()
+        place(qkv_landed[step], lax.rem(me + n - 1 - step, n))
+    for step, copy in enumerate(second):
+        copy.wait()
+        owner = lax.rem(me + n - 1 - step, n)
+        out_final[block_of(owner, piece), :] = out_back[step].astype(F32)
+
+
+def finish(qkv, out, widths, n, call_id):
+    rows, width = out.shape
+    return pl.pallas_call(
+        finish_kernel,
+        out_shape=tuple(jax.ShapeDtypeStruct((qkv.shape[0], size), F32) for size in widths)
+        + (jax.ShapeDtypeStruct(out.shape, F32),),
+        in_specs=[VMEM_SPEC] * 2,
+        out_specs=(VMEM_SPEC,) * 4,
+        scratch_shapes=[
+            pltpu.VMEM((n - 1,) + qkv.shape, BF16),
+            pltpu.VMEM((n - 1, rows // n, width), BF16),
+            pltpu.VMEM((rows // n, width), BF16),
+            pltpu.VMEM((n - 1, rows // n, width), BF16),
+        ]
+        + semaphores(*([n - 1] * 6)),
+        compiler_params=communicating(call_id),
+        name="finish",
+    )(qkv, out)
+
+
+def spread_kernel(hidden_piece, pieces_ref, gate_ref, up_ref):
+    n, _, width = pieces_ref.shape
+    units = width // 2
+    span = n * hidden_piece
+    for target, base in ((gate_ref, 0), (up_ref, units)):
+        for shard in range(units // hidden_piece):
+            at = base + shard * hidden_piece
+            target[:, shard * span : (shard + 1) * span] = jnp.concatenate(
+                [pieces_ref[s, :, at : at + hidden_piece].astype(F32) for s in range(n)], axis=1
+            )
+
+
+def spread_back(pieces, hidden_piece):
+    n, rows, width = pieces.shape
+    shape = jax.ShapeDtypeStruct((rows, n * width // 2), F32)
+    return pl.pallas_call(
+        functools.partial(spread_kernel, hidden_piece),
+        out_shape=(shape, shape),
+        in_specs=[VMEM_SPEC],
+        out_specs=(VMEM_SPEC, VMEM_SPEC),
+        name="spread_back",
+    )(pieces)
 
 
 def rope(values, cosine, sine):
@@ -646,54 +752,41 @@
     grad_partial, grad_down, grad_gate_up_weight = lax.optimization_barrier(
         (back_matmul(grad_gate_up, gate_up_weight).astype(BF16), grad_down, grad_gate_up_weight)
     )
+    down_share = lax.psum_scatter(grad_down, "fsdp", scatter_dimension=0, tiled=True)
+    gate_up_share = lax.psum_scatter(grad_gate_up_weight, "fsdp", scatter_dimension=0, tiled=True)
     grad_normed_post = scatter_sum(grad_partial, n, 3)
     grad_middle, gain_rows = rms_backward(middle, gain_post, grad_normed_post)
     grad_middle = cotangent[0].astype(F32) + grad_middle
     grad_gain_post = jnp.sum(gain_rows, axis=0)
     grad_branch = grad_middle.astype(BF16)
     grad_out = outer_sum(attended, grad_branch).astype(BF16)
+    out_share = lax.psum_scatter(grad_out, "fsdp", scatter_dimension=0, tiled=True)
     grad_attended = back_matmul(grad_branch, out_weight).astype(BF16)
     grad_q, grad_k, grad_v, grad_gain_query, grad_gain_key, mlp_landed = attend_backward(
-        weights, query, key, value, grad_attended, mlp_partial, q_pre, k_pre, gain_query, gain_key,
-        cosine, sine, n, 4,
+        weights, query, key, value, grad_attended, mlp_partial, q_pre, k_pre, gain_query,
+        gain_key, cosine, sine, n, 4,
     )
     result = middle + lax.dynamic_slice_in_dim(mlp_partial, me * resident, resident).astype(F32)
     output = (result + jnp.sum(mlp_landed.astype(F32), axis=0)).astype(BF16)[None]
     grad_qkv = jnp.concatenate([grad_q, grad_k, grad_v], axis=1)
     grad_qkv_weight = outer_sum(normalized, grad_qkv).astype(BF16)
+    qkv_share = lax.psum_scatter(grad_qkv_weight, "fsdp", scatter_dimension=0, tiled=True)
     partial = back_matmul(grad_qkv, qkv_weight)
     grad_gain_in = jnp.sum(partial * unit, axis=0)
     small_grads = [grad_gain_in, grad_gain_post, grad_gain_query, grad_gain_key]
     small_grads = tile_of(jnp.concatenate([g.reshape(shards, -1) for g in small_grads], axis=1))
-    grad_normed, gain_shares = scatter_last(partial.astype(BF16), small_grads, n, shards, 5)
+    grad_normed, gain_shares, down_all, gate_up_all = scatter_last(
+        partial.astype(BF16), small_grads, down_share, gate_up_share, n, shards, 5
+    )
     gain_shares = gain_shares.reshape(-1)
     grad_inputs, _ = rms_backward(inputs, gain_in, grad_normed)
     input_grad = (grad_middle + grad_inputs).astype(BF16)[None]
 
-    def shared(grad):
-        return lax.all_gather(
-            lax.psum_scatter(grad, "fsdp", scatter_dimension=0, tiled=True), "seq", axis=0
-        ).astype(F32)
-
-    def beside(pieces):
-        return jnp.swapaxes(pieces, 0, 1).reshape(pieces.shape[1], -1)
-
-    final_down = shared(grad_down).reshape(-1, width)
-    gate_up_all = shared(grad_gate_up_weight)
-
-    def spread_back(pieces):
-        pieces = pieces.reshape(n, pieces.shape[1], shards, hidden_piece)
-        return jnp.transpose(pieces, (1, 2, 0, 3)).reshape(pieces.shape[1], -1)
-
-    final_gate = spread_back(gate_up_all[:, :, :units])
-    final_up = spread_back(gate_up_all[:, :, units:])
-    final_out = lax.psum(
-        lax.psum_scatter(grad_out, "fsdp", scatter_dimension=0, tiled=True), "seq"
-    ).astype(F32)
-    qkv_all = shared(grad_qkv_weight)
-    final_query = beside(qkv_all[:, :, :split])
-    final_key = beside(qkv_all[:, :, split : split + kv * HEAD_SIZE])
-    final_value = beside(qkv_all[:, :, split + kv * HEAD_SIZE :])
+    final_down = down_all.astype(F32).reshape(-1, width)
+    final_gate, final_up = spread_back(gate_up_all, hidden_piece)
+    final_query, final_key, final_value, final_out = finish(
+        qkv_share, out_share, (HQ * HEAD_SIZE,) + (KEY_VALUE_HEADS * HEAD_SIZE,) * 2, n, 6
+    )
 
     return (
         output,
@@ -719,6 +812,7 @@
         whole, wide, wide, flat, wide, wide, wide, flat, flat, wide, flat, wide, wide, wide, whole,
     )
     out_specs = (whole, whole, flat, wide, wide, wide, flat, flat, wide, flat, wide, wide, wide)
+
     return jax.shard_map(
         on_device, mesh=mesh, in_specs=in_specs, out_specs=out_specs, check_vma=False
     )

time: 557 us -> 401 us (0.72)
  waiting for transfers between devices: 199 us -> 16.3 us
  Pallas kernels: 202 us -> 257 us
  local copies, waits for them, and re-layouts: 36.9 us -> 22.6 us
  blocking collectives: 10.5 us -> 0 us
    reduce_scatter x3, waiting for transfers between devices: 69.5 us -> 0.01 us  [the longest x1 0.01 us: on_device(): lax.psum_scatter(grad_down, 'fsdp', scatter_dimension=0, tiled=True)]
    reduce_scatter x1, waiting for transfers between devices: 49.6 us -> 4.94 us  [on_device(): lax.psum_scatter(grad_out, 'fsdp', scatter_dimension=0, tiled=True)]
    all_gather x2 -> x0, waiting for transfers between devices: 35.1 us -> none  [shared(): lax.all_gather(lax.psum_scatter(grad, 'fsdp', scatter_dimension=0, tiled=...]
    psum x1 -> x0, waiting for transfers between devices: 32.6 us -> none  [on_device(): lax.psum(lax.psum_scatter(grad_out, 'fsdp', scatter_dimension=0, tiled=Tr...]
    pallas_call x0 -> x2, Pallas kernels: none -> 30.5 us  [the longest x1 27 us: finish(): pl.pallas_call(finish_kernel, out_shape=tuple((jax.ShapeDtypeStruct((qkv....]
    pallas_call x1, Pallas kernels: 30.5 us -> 55.2 us  [scatter_last(): pl.pallas_call(scatter_last_kernel, out_shape=(jax.ShapeDtypeStruct((rows...]
    all_gather x1 -> x0, blocking collectives: 10.5 us -> none  [shared(): lax.all_gather(lax.psum_scatter(grad, 'fsdp', scatter_dimension=0, tiled=...]
    unnamed x70 -> x76, local copies, waits for them, and re-layouts: 17.9 us -> 12.2 us
  transfers between devices with their start and end apart: 11 -> 8, of which waited for: 7 -> 2; matrix products, arithmetic and copies ran while one was open for 14% -> 17% of each run, Pallas kernels for 24% -> 58%
where the time goes in v3:
time: 401 us; the launch traced here: 394 us
  Pallas kernels  257 us (64%)
  matrix products  62.9 us (16%)
  local copies, waits for them, and re-layouts  22.6 us (6%)
  other arithmetic  19.3 us (5%)
  waiting for transfers between devices  16.3 us (4%)
  between operations  14.9 us (4%)
    pallas_call x1, Pallas kernels, scatter_last(): pl.pallas_call(scatter_last_kernel, out_shape=(jax.ShapeDtypeStruct((rows...  55.2 us
    pallas_call x1, Pallas kernels, attend_forward(): pl.pallas_call(forward_kernel, grid=(n, heads), out_shape=(jax.ShapeDtype...  41.3 us
    pallas_call x1, Pallas kernels, attend_backward(): pl.pallas_call(backward_kernel, grid=(n, heads), out_shape=(jax.ShapeDtyp...  41.1 us
    pallas_call x1, Pallas kernels, gather_first(): pl.pallas_call(gather_first_kernel, out_shape=(jax.ShapeDtypeStruct((n *...  32.7 us
    pallas_call x1, Pallas kernels, scatter_sum(): pl.pallas_call(scatter_kernel, out_shape=jax.ShapeDtypeStruct((rows, widt...  29 us
    pallas_call x1, Pallas kernels, gather_rows(): pl.pallas_call(gather_kernel, out_shape=jax.ShapeDtypeStruct((n * rows, w...  27.4 us
    pallas_call x1, Pallas kernels, finish(): pl.pallas_call(finish_kernel, out_shape=tuple((jax.ShapeDtypeStruct((qkv....  27 us
    dot_general x4, matrix products, back_matmul(): lax.dot_general(left, right, (((1,), (1,)), ((), ())), preferred_element_...  24.2 us
  transfers between devices with their start and end apart: 8, of which 2 were waited for; matrix products, arithmetic and copies ran while one was open for 17% of the time, Pallas kernels for 58%

profile of v3, /device:TPU:0, one launch (start us, length us, event | category | flops | bytes accessed | tf_op | source)
XLA Modules:
  0.0 393.7 jit_solution(113797565799503384)
XLA Ops:
  7.3 1.1 constant_dynamic-slice_fusion.5
  8.3 0.9 constant_dynamic-slice_fusion.3
  9.2 0.7 pad_maximum_fusion.8
  11.7 0.8 pad_maximum_fusion.7
  14.0 32.7 %gather_first.1 = (bf16[1024,1024]{1,0:T(8,128)(2,1)}, f32[8,8,128]{2,1,0:T(8,128)}) custom-call(bf16[256,1024]{1,0:T(8,128)(2,1)} %bitcast.67, f32[8,128]{1,0:T(8,128)} %fusion.30.gains_ref), custom_call_target="tpu_custom_call" | custom-call | tf_op jit(solution)/shard_map/gather_first/pallas_call | solution.py:136
  46.7 0.8 copy.46
  47.5 2.1 fusion.4
  50.5 1.9 fusion.21
  52.4 1.3 pad_maximum_fusion.5
  54.9 1.0 copy.35.place_k
  55.9 4.0 %fusion.15 = f32[1024,1024]{1,0:T(8,128)S(1)} fusion(bf16[1024,1024]{1,0:T(8,128)(2,1)} %all-gather.5.cloned.1.call-done, bf16[1024,1024]{1,0:T(8,128)(2,1)S(1)} %copy-done.5, f32[1024]{0:T(1024)S(1)} %get-tuple-element.75, f32[1024]{0:T(1024)S(1)} %add_rsqrt_fusion), kind=kOutput, calls=%fused_computation.44 | convolution fusion | flops 2151677952 | bytes 8396800 | tf_op jit(solution)/shard_map/dot_general | solution.py:26
  59.9 1.5 slice.62.q_pre
  61.4 1.1 slice.63.k_pre
  62.5 0.9 slice.80.v_ref
  63.4 41.3 %attend_forward.1 = (bf16[256,2048]{1,0:T(8,128)(2,1)}, bf16[4,1024,1024]{2,1,0:T(8,128)(2,1)}, bf16[1024,512]{1,0:T(8,128)(2,1)}, bf16[1024,256]{1,0:T(8,128)(2,1)}, bf16[1024,1024]{1,0:T(8,128)(2,1)}) custom-call(f32[1024,512]{1,0:T(8,128)} %slice.62.q_pre, f32[1024,256]{1,0:T(8,128)} %slice.63.k_pre, bf16[1024,256]{1,0:T(8,128)(2,1)} %slice.80.v_ref, ...), custom_call_target="tpu_custom_call" | custom-call | tf_op jit(solution)/shard_map/attend_forward/pallas_call | solution.py:474
  104.7 3.9 multiply_reduce_fusion.2
  108.6 1.0 multiply_convert_fusion.3.x_ref
  109.5 27.4 %shard_map.246 = bf16[1024,1024]{1,0:T(8,128)(2,1)} custom-call(bf16[256,1024]{1,0:T(8,128)(2,1)} %multiply_convert_fusion.3.x_ref), custom_call_target="tpu_custom_call" | custom-call | tf_op jit(solution)/shard_map/pallas_call | solution.py:110
  137.0 8.9 %fusion.35 = f32[1024,1536]{1,0:T(8,128)} fusion(bf16[1024,1024]{1,0:T(8,128)(2,1)} %shard_map.246, bf16[1024,1536]{0,1:T(8,128)(2,1)} %all-gather.9.cloned.1.call-done), kind=kOutput, calls=%fused_computation.93 | convolution fusion | flops 3221225472 | bytes 11534336 | tf_op jit(solution)/shard_map/dot_general | solution.py:26
  145.9 10.0 %all-gather.11.cloned.1.call-done = bf16[768,1024]{1,0:T(8,128)(2,1)} async-done(((bf16[96,1024]{1,0:T(8,128)(2,1)}), bf16[768,1024]{1,0:T(8,128)(2,1)}) %all-gather.11.cloned.1.call-update) | async-done | bytes 1572880 | tf_op jit(solution)/shard_map/all_gather | solution.py:706
  155.9 7.9 %multiply_convert_fusion.1 = (bf16[1024,768]{1,0:T(8,128)(2,1)S(1)}, bf16[1024,768]{1,0:T(8,128)(2,1)}, bf16[1024,768]{1,0:T(8,128)(2,1)S(1)}) fusion(f32[1024,1536]{1,0:T(8,128)} %fusion.35, bf16[1024,1024]{1,0:T(8,128)(2,1)} %get-tuple-element.45, bf16[768,1024]{1,0:T(8,128)(2,1)} %all-gather.11.cloned.1.call-done), kind=kOutput, calls=%fused_computation.14 | convolution fusion | flops 1623195648 | bytes 14680064 | tf_op jit(solution)/shard_map/dot_general | solution.py:34
  163.8 1.1 copy-done.31
  165.0 3.0 convolution_convert_fusion.5
  168.0 7.2 %convolution_convert_fusion.1 = bf16[1024,1536]{1,0:T(8,128)(2,1)} fusion(bf16[1024,1024]{1,0:T(8,128)(2,1)} %shard_map.246, bf16[1024,768]{1,0:T(8,128)(2,1)} %get-tuple-element.70, bf16[1024,768]{1,0:T(8,128)(2,1)S(1)} %get-tuple-element.69), kind=kOutput, calls=%fused_computation.10 | convolution fusion | flops 3229089792 | bytes 8388608 | tf_op jit(solution)/shard_map/dot_general | solution.py:30
  175.2 7.4 %fusion.7.p_ref = bf16[1024,1024]{1,0:T(8,128)(2,1)} fusion(bf16[1024,1536]{0,1:T(8,128)(2,1)} %all-gather.9.cloned.1.call-done, bf16[1024,768]{1,0:T(8,128)(2,1)} %get-tuple-element.70, bf16[1024,768]{1,0:T(8,128)(2,1)S(1)} %get-tuple-element.69), kind=kOutput, calls=%fused_computation.21 | convolution fusion | flops 3228565504 | bytes 8388608 | tf_op jit(solution)/shard_map/dot_general | solution.py:34
  183.2 29.0 %shard_map.247 = f32[256,1024]{1,0:T(8,128)} custom-call(bf16[1024,1024]{1,0:T(8,128)(2,1)} %fusion.7.p_ref), custom_call_target="tpu_custom_call" | custom-call | tf_op jit(solution)/shard_map/pallas_call | solution.py:169
  212.3 1.7 multiply_reduce_fusion
  214.3 0.8 copy-done.25
  215.1 2.3 convolution_convert_fusion.2.grad_own
  217.4 3.2 convolution_convert_fusion.4.bulk
  220.6 41.1 %attend_backward.1 = (bf16[1024,512]{1,0:T(8,128)(2,1)}, bf16[1024,256]{1,0:T(8,128)(2,1)}, bf16[1024,256]{1,0:T(8,128)(2,1)}, f32[1,128]{1,0:T(1,128)}, f32[1,1...) custom-call(bf16[4,1024,1024]{2,1,0:T(8,128)(2,1)} %get-tuple-element.42.p_ref, bf16[1024,512]{1,0:T(8,128)(2,1)} %get-tuple-element.43.q_ref, ...), custom_call_target="tpu_custom_call" | custom-call | tf_op jit(solution)/shard_map/attend_backward/pallas_call | solution.py:619
  261.7 1.5 constant_dynamic-update-slice_fusion.2
  263.4 1.3 copy-done.12
  264.7 4.1 %convolution_convert_fusion.3 = bf16[1024,1024]{1,0:T(8,128)(2,1)} fusion(bf16[1024,1024]{1,0:T(8,128)(2,1)S(1)} %constant_dynamic-update-slice_fusion, bf16[1024,1024]{1,0:T(8,128)(2,1)S(1)} %copy-done.6, f32[1024]{0:T(1024)S(1)} %get-tuple-element.75, f32[1024]{0:T(1024)S(1)} %add_rsqrt_fusion), kind=kOutput, calls=%fused_computation.20 | convolution fusion | flops 2152726528 | bytes 6299648 | tf_op jit(solution)/shard_map/dot_general | solution.py:30
  269.1 4.5 %convolution_convert_fusion = bf16[2048,1024]{1,0:T(8,128)(2,1)} fusion(bf16[256,2048]{1,0:T(8,128)(2,1)} %get-tuple-element.41, f32[256,1024]{1,0:T(8,128)S(1)} %subtract_add_fusion), kind=kOutput, calls=%fused_computation.9 | convolution fusion | flops 1076101120 | bytes 6291456 | tf_op jit(solution)/shard_map/dot_general | solution.py:30
  275.7 6.6 %fusion.3 = (f32[1024]{0:T(1024)S(1)}, bf16[1024,1024]{1,0:T(8,128)(2,1)}) fusion(bf16[1024,1024]{1,0:T(8,128)(2,1)} %get-tuple-element.39, f32[1024]{0:T(1024)S(1)} %add_rsqrt_fusion, bf16[1024,1024]{1,0:T(8,128)(2,1)} %copy-done.12, bf16[1024,1024]{1,0:T(8,128)(2,1)} %all-gather.5.cloned.1.call-done), kind=kOutput, calls=%fused_computation.5 | convolution fusion | flops 2152725504 | bytes 8396800 | tf_op jit(solution)/shard_map/dot_general | solution.py:34
  283.1 1.9 convert_reduce_fusion
  284.9 2.1 fusion.17
  287.0 55.2 %scatter_last.1 = (f32[256,1024]{1,0:T(8,128)}, f32[8,128]{1,0:T(8,128)}, bf16[4,96,1024]{2,1,0:T(8,128)(2,1)}, bf16[4,128,1536]{2,1,0:T(8,128)(2,1)}) custom-call(bf16[1024,1024]{1,0:T(8,128)(2,1)} %get-tuple-element.73.p_ref, f32[8,8,128]{2,1,0:T(8,128)} %bitcast.73, bf16[96,1024]{1,0:T(8,128)(2,1)} %reduce-scatter.5.cloned.1.call-done.down_ref, ...), custom_call_target="tpu_custom_call" | custom-call | tf_op jit(solution)/shard_map/scatter_last/pallas_call | solution.py:232
  342.2 3.6 spread_back.1
  347.2 1.4 bitcast_convert_fusion
  348.6 1.1 fusion.18
  349.7 4.9 %reduce-scatter.11.cloned.1.call-done.out_ref = bf16[256,1024]{1,0:T(8,128)(2,1)} async-done(((bf16[2048,1024]{1,0:T(8,128)(2,1)}), bf16[256,1024]{1,0:T(8,128)(2,1)}) %reduce-scatter.11.cloned.1.call-update) | async-done | bytes 524304 | tf_op jit(solution)/shard_map/reduce_scatter | solution.py:763
  354.6 27.0 %finish.1 = (f32[128,2048]{1,0:T(8,128)}, f32[128,1024]{1,0:T(8,128)}, f32[128,1024]{1,0:T(8,128)}, f32[256,1024]{1,0:T(8,128)}) custom-call(bf16[128,1024]{1,0:T(8,128)(2,1)} %reduce-scatter.9.cloned.1.call-done.qkv_ref, bf16[256,1024]{1,0:T(8,128)(2,1)} %reduce-scatter.11.cloned.1.call-done.out_ref), custom_call_target="tpu_custom_call" | custom-call | tf_op jit(solution)/shard_map/finish/pallas_call | solution.py:303
  381.7 2.4 copy.53
  384.1 0.8 copy.54
  384.9 0.8 copy.55
  385.7 1.0 copy.56
  (118 shorter events, 10.9 us)
Async XLA Ops:
  7.2 5.3 %copy-start = (bf16[384,1024]{1,0:T(8,128)(2,1)S(1)}, bf16[384,1024]{1,0:T(8,128)(2,1)}, u32[]{:S(2)}) copy-start(bf16[384,1024]{1,0:T(8,128)(2,1)} %param.28) | copy-start | bytes 2359300
  7.2 3.6 copy-start.9
  7.2 4.0 %copy-start.10 = (bf16[128,3072]{1,0:T(8,128)(2,1)S(1)}, bf16[128,3072]{1,0:T(8,128)(2,1)}, u32[]{:S(2)}) copy-start(bf16[128,3072]{1,0:T(8,128)(2,1)} %param.26) | copy-start | bytes 2359300
  7.2 48.7 %all-gather.5.cloned.1.call-start = ((), (), s32[]{:S(2)}) async-start(), calls=%async_computation.4 | async-start | bytes 2359296 | tf_op jit(solution)/shard_map/all_gather | solution.py:696
  10.0 94.7 %all-gather.7.cloned.1.call-start = ((), (), s32[]{:S(2)}) async-start(), calls=%async_computation.5 | async-start | bytes 4718592 | tf_op jit(solution)/shard_map/all_gather | solution.py:702
  10.7 126.2 %all-gather.9.cloned.1.call-start = ((), (), s32[]{:S(2)}) async-start(), calls=%async_computation.6 | async-start | bytes 3538944 | tf_op jit(solution)/shard_map/all_gather | solution.py:703
  11.2 2.2 copy-start.20
  11.2 2.1 copy-start.21
  11.2 2.1 copy-start.22
  11.2 2.1 copy-start.23
  11.7 38.0 %copy-start.28 = (s32[1,1024]{1,0:T(1,128)S(1)}, s32[1,1024]{1,0:T(1,128)}, u32[]{:S(2)}) copy-start(s32[1,1024]{1,0:T(1,128)} %param.17) | copy-start | bytes 12292
  11.7 38.5 %copy-start.24 = (s32[1,8]{1,0:T(1,128)S(1)}, s32[1,8]{1,0:T(1,128)}, u32[]{:S(2)}) copy-start(s32[1,8]{1,0:T(1,128)} %param.16) | copy-start | bytes 100
  12.5 143.4 %all-gather.11.cloned.1.call-start = ((), (), s32[]{:S(2)}) async-start(), calls=%async_computation.7 | async-start | bytes 1769472 | tf_op jit(solution)/shard_map/all_gather | solution.py:706
  13.3 273.8 %reduce-scatter.5.cloned.1.call-start = ((), (), s32[]{:S(2)}) async-start(), calls=%async_computation.8 | async-start | bytes 1769472 | tf_op jit(solution)/shard_map/reduce_scatter | solution.py:755
  50.1 4.7 %copy-start.17 = (s32[1024]{0:T(1024)}, s32[1024]{0:T(1024)S(1)}, u32[]{:S(2)}) copy-start(s32[1024]{0:T(1024)S(1)} %select_reduce_fusion) | copy-start | bytes 12292
  50.4 3.3 copy-start.18
  50.5 5.5 %copy-start.5 = (bf16[1024,1024]{1,0:T(8,128)(2,1)S(1)}, bf16[1024,1024]{1,0:T(8,128)(2,1)}, u32[]{:S(2)}) copy-start(bf16[1024,1024]{1,0:T(8,128)(2,1)} %get-tuple-element.39) | copy-start | bytes 6291460
  63.4 41.4 %copy-start.3 = (bf16[1,256,1024]{2,1,0:T(8,128)(2,1)S(1)}, bf16[1,256,1024]{2,1,0:T(8,128)(2,1)}, u32[]{:S(2)}) copy-start(bf16[1,256,1024]{2,1,0:T(8,128)(2,1)} %param.15) | copy-start | bytes 1572868
  155.9 9.1 %copy-start.26 = (bf16[1024,1024]{1,0:T(8,128)(2,1)S(1)}, bf16[1024,1024]{1,0:T(8,128)(2,1)}, u32[]{:S(2)}) copy-start(bf16[1024,1024]{1,0:T(8,128)(2,1)} %get-tuple-element.45) | copy-start | bytes 6291460
  163.8 1.1 copy-start.31
  182.6 104.5 %reduce-scatter.7.cloned.1.call-start = ((), (), s32[]{:S(2)}) async-start(), calls=%async_computation.9 | async-start | bytes 3538944 | tf_op jit(solution)/shard_map/reduce_scatter | solution.py:756
  183.1 30.8 %copy-start.7 = (bf16[1,256,1024]{2,1,0:T(8,128)(2,1)S(1)}, bf16[1,256,1024]{2,1,0:T(8,128)(2,1)}, u32[]{:S(2)}) copy-start(bf16[1,256,1024]{2,1,0:T(8,128)(2,1)} %param.29) | copy-start | bytes 1572868
  183.2 166.5 %reduce-scatter.9.cloned.1.call-start = ((), (), s32[]{:S(2)}) async-start(), calls=%async_computation.10 | async-start | bytes 2359296 | tf_op jit(solution)/shard_map/reduce_scatter | solution.py:773
  212.3 1.7 copy-start.2
  212.3 2.8 copy-start.25
  215.1 2.3 copy-start.27
  215.1 2.3 copy-start.32
  261.7 1.5 copy-start.14
  261.7 1.6 copy-start.13
  261.7 3.0 copy-start.6
  263.4 1.3 copy-start.12
  268.8 85.8 %reduce-scatter.11.cloned.1.call-start = ((), (), s32[]{:S(2)}) async-start(), calls=%async_computation.11 | async-start | bytes 4718592 | tf_op jit(solution)/shard_map/reduce_scatter | solution.py:763
  273.6 0.6 copy-start.30
  273.6 1.4 copy-start.29
  342.2 3.6 copy-start.4
  342.2 3.9 copy-start.19
  345.8 1.4 copy-start.11
  381.6 2.5 copy-start.16
  381.6 3.3 copy-start.15
  381.6 4.1 %copy-start.8 = (f32[256,1024]{1,0:T(8,128)S(1)}, f32[256,1024]{1,0:T(8,128)}, u32[]{:S(2)}) copy-start(f32[256,1024]{1,0:T(8,128)} %get-tuple-element.119) | copy-start | bytes 3145732
  381.7 5.0 %copy-start.1 = (bf16[384,1024]{1,0:T(8,128)(2,1)S(1)}, bf16[384,1024]{1,0:T(8,128)(2,1)}, u32[]{:S(2)}) copy-start(bf16[384,1024]{1,0:T(8,128)(2,1)} %param.28) | copy-start | bytes 2359300
Sparse Core Ops, SparseCore 0:
  10.2 32.1 all-gather.4
  44.0 46.1 all-gather.6
  92.3 37.9 all-gather.8
  132.4 23.4 all-gather.10
  182.7 33.5 reduce-scatter.4
  218.4 38.4 reduce-scatter.6
  269.0 34.8 reduce-scatter.8
  306.2 48.4 reduce-scatter.10

commit v4 on v3

--- a/solution.py
+++ b/solution.py
@@ -94,15 +94,215 @@
     return pltpu.CompilerParams(collective_id=call_id, has_side_effects=True, **more)
 
 
-def gather_kernel(x_ref, o_ref, send_sem, recv_sem):
+def remote(source, target, send_sem, recv_sem, peer):
+    return pltpu.make_async_remote_copy(
+        src_ref=source,
+        dst_ref=target,
+        send_sem=send_sem,
+        recv_sem=recv_sem,
+        device_id={"seq": peer},
+        device_id_type=MESH,
+    )
+
+
+class Plane:
+    def __init__(self):
+        self.n = lax.axis_size("seq")
+        self.ny = self.n // 2
+        self.me = lax.axis_index("seq")
+        self.x = lax.rem(self.me, 2)
+        self.y = self.me // 2
+
+    def at(self, j, across):
+        row = lax.rem(self.y + j + self.ny, self.ny)
+        return row * 2 + ((1 - self.x) if across else self.x)
+
+
+class RelayGather(Plane):
+    def __init__(self, source, target, sems):
+        super().__init__()
+        self.source, self.target = source, target
+        self.sx, self.rx, self.sy, self.ry, self.sy2, self.ry2, self.sx2, self.rx2 = sems
+
+    @staticmethod
+    def semaphores(n):
+        ny = n // 2
+        dma = pltpu.SemaphoreType.DMA
+        return [dma((2,))] * 2 + [dma((ny - 1, 2))] * 2 + [dma((ny - 1,))] * 4
+
+    def x1(self, half):
+        return remote(
+            self.source(half), self.target(self.me, half), self.sx.at[half], self.rx.at[half],
+            self.at(0, True),
+        )
+
+    def y1(self, j, half):
+        return remote(
+            self.source(half), self.target(self.me, half), self.sy.at[j - 1, half],
+            self.ry.at[j - 1, half], self.at(j, False),
+        )
+
+    def y2(self, j):
+        block = self.target(self.at(0, True), 0)
+        return remote(block, block, self.sy2.at[j - 1], self.ry2.at[j - 1], self.at(j, False))
+
+    def x2(self, j):
+        block = self.target(self.at(-j, False), 1)
+        return remote(block, block, self.sx2.at[j - 1], self.rx2.at[j - 1], self.at(0, True))
+
+    def start(self):
+        others = range(1, self.ny)
+        self.x1(0).start()
+        for j in others:
+            self.y1(j, 1).start()
+        self.x1(1).start()
+        for j in others:
+            self.y1(j, 0).start()
+
+    def forward(self):
+        others = range(1, self.ny)
+        self.x1(0).wait_recv()
+        for j in others:
+            self.y2(j).start()
+        for j in others:
+            self.y1(j, 1).wait_recv()
+            self.x2(j).start()
+
+    def finish(self):
+        self.x1(0).wait_send()
+        self.x1(1).wait()
+        for j in range(1, self.ny):
+            self.y1(j, 1).wait_send()
+            self.y1(j, 0).wait()
+            self.y2(j).wait()
+            self.x2(j).wait()
+
+
+def row_halves(ref, rows, owner, half):
+    size = rows // 2
+    return ref.at[pl.ds(pl.multiple_of(owner * rows + half * size, size), size)]
+
+
+def column_halves(ref, half):
+    size = ref.shape[-1] // 2
+    return ref.at[:, half * size : (half + 1) * size]
+
+
+def gather_by_rows(x_ref, o_ref, sems):
+    rows = x_ref.shape[0]
+    return RelayGather(
+        lambda half: row_halves(x_ref, rows, 0, half),
+        lambda owner, half: row_halves(o_ref, rows, owner, half),
+        sems,
+    )
+
+
+def gather_by_columns(x_ref, o_ref, sems):
+    return RelayGather(
+        lambda half: column_halves(x_ref, half),
+        lambda owner, half: column_halves(o_ref.at[owner], half),
+        sems,
+    )
+
+
+class RelayScatter(Plane):
+    def __init__(self, partial, buffers, sems):
+        super().__init__()
+        self.partial = partial
+        self.rows = partial.shape[0] // self.n
+        self.from_x, self.from_y, self.sent_y, self.late_y, self.sent_x, self.late_x = buffers
+        self.sx, self.rx, self.sy, self.ry, self.sy2, self.ry2, self.sx2, self.rx2 = sems
+
+    @staticmethod
+    def scratch(n, rows, width):
+        ny, half = n // 2, rows // 2
+        dma = pltpu.SemaphoreType.DMA
+        return [
+            pltpu.VMEM((ny, half, width), BF16),
+            pltpu.VMEM((ny - 1, 2, half, width), BF16),
+            pltpu.VMEM((ny - 1, half, width), BF16),
+            pltpu.VMEM((ny - 1, half, width), BF16),
+            pltpu.VMEM((half, width), BF16),
+            pltpu.VMEM((half, width), BF16),
+        ] + [dma((ny,))] * 2 + [dma((ny - 1, 2))] * 2 + [dma((ny - 1,))] * 2 + [dma((1,))] * 2
+
+    def piece(self, owner, half):
+        return row_halves(self.partial, self.rows, owner, half)
+
+    def x1(self, j):
+        return remote(
+            self.piece(self.at(j, True), 0), self.from_x.at[j], self.sx.at[j], self.rx.at[j],
+            self.at(0, True),
+        )
+
+    def y1(self, j, final):
+        return remote(
+            self.piece(self.at(j, not final), 1), self.from_y.at[j - 1, int(final)],
+            self.sy.at[j - 1, int(final)], self.ry.at[j - 1, int(final)], self.at(j, False),
+        )
+
+    def y2(self, j):
+        return remote(
+            self.sent_y.at[j - 1], self.late_y.at[j - 1], self.sy2.at[j - 1], self.ry2.at[j - 1],
+            self.at(j, False),
+        )
+
+    def x2(self):
+        return remote(self.sent_x, self.late_x, self.sx2.at[0], self.rx2.at[0], self.at(0, True))
+
+    def start(self):
+        others = range(1, self.ny)
+        for j in others:
+            self.x1(j).start()
+            self.y1(j, False).start()
+        self.x1(0).start()
+        for j in others:
+            self.y1(j, True).start()
+
+    def forward(self, o_ref):
+        others = range(1, self.ny)
+        half = self.rows // 2
+        for j in others:
+            self.x1(j).wait_recv()
+            own = self.piece(self.at(j, False), 0)[...].astype(F32)
+            self.sent_y[j - 1] = (own + self.from_x[j].astype(F32)).astype(BF16)
+        total = self.piece(self.at(0, True), 1)[...].astype(F32)
+        for j in others:
+            self.y1(j, False).wait_recv()
+            total = total + self.from_y[j - 1, 0].astype(F32)
+        self.sent_x[...] = total.astype(BF16)
+        for j in others:
+            self.y2(j).start()
+        o_ref[:half, :] = self.piece(self.me, 0)[...].astype(F32)
+        self.x2().start()
+        o_ref[half:, :] = self.piece(self.me, 1)[...].astype(F32)
+
+    def finish(self, o_ref):
+        others = range(1, self.ny)
+        half = self.rows // 2
+        self.x1(0).wait()
+        first = o_ref[:half, :] + self.from_x[0].astype(F32)
+        second = o_ref[half:, :]
+        for j in others:
+            self.x1(j).wait_send()
+            self.y1(j, False).wait_send()
+            self.y1(j, True).wait()
+            second = second + self.from_y[j - 1, 1].astype(F32)
+        for j in others:
+            self.y2(j).wait()
+            first = first + self.late_y[j - 1].astype(F32)
+        o_ref[:half, :] = first
+        self.x2().wait()
+        o_ref[half:, :] = second + self.late_x[...].astype(F32)
+
+
+def gather_kernel(x_ref, o_ref, *sems):
     greet("seq")
-    mine = block_of(lax.axis_index("seq"), x_ref.shape[0])
-    copies = start_to_peers(
-        "seq", lambda peer: x_ref, lambda step: o_ref.at[mine], send_sem, recv_sem
-    )
-    o_ref[mine, :] = x_ref[...]
-    for copy in copies:
-        copy.wait()
+    relay = gather_by_rows(x_ref, o_ref, sems)
+    relay.start()
+    o_ref[block_of(lax.axis_index("seq"), x_ref.shape[0]), :] = x_ref[...]
+    relay.forward()
+    relay.finish()
 
 
 def gather_rows(x, n, call_id):
@@ -112,22 +312,24 @@
         out_shape=jax.ShapeDtypeStruct((n * rows, width), x.dtype),
         in_specs=[VMEM_SPEC],
         out_specs=VMEM_SPEC,
-        scratch_shapes=semaphores(n - 1, n - 1),
+        scratch_shapes=RelayGather.semaphores(n),
         compiler_params=communicating(call_id),
     )(x)
 
 
-def gather_first_kernel(x_ref, gains_ref, o_ref, all_gains, send, recv, gain_send, gain_recv):
+def gather_first_kernel(x_ref, gains_ref, o_ref, all_gains, gain_send, gain_recv, *sems):
     greet("seq", "fsdp")
     place = lax.axis_index("fsdp")
     gain_copies = start_to_peers(
         "fsdp", lambda peer: gains_ref, lambda step: all_gains.at[place], gain_send, gain_recv
     )
-    mine = block_of(lax.axis_index("seq"), x_ref.shape[0])
-    copies = start_to_peers("seq", lambda peer: x_ref, lambda step: o_ref.at[mine], send, recv)
-    o_ref[mine, :] = x_ref[...]
+    relay = gather_by_rows(x_ref, o_ref, sems)
+    relay.start()
+    o_ref[block_of(lax.axis_index("seq"), x_ref.shape[0]), :] = x_ref[...]
     all_gains[place] = gains_ref[...]
-    for copy in gain_copies + copies:
+    relay.forward()
+    relay.finish()
+    for copy in gain_copies:
         copy.wait()
 
 
@@ -141,26 +343,18 @@
         ),
         in_specs=[VMEM_SPEC, VMEM_SPEC],
         out_specs=(VMEM_SPEC, VMEM_SPEC),
-        scratch_shapes=semaphores(n - 1, n - 1, shards - 1, shards - 1),
+        scratch_shapes=semaphores(shards - 1, shards - 1) + RelayGather.semaphores(n),
         compiler_params=communicating(call_id),
         name="gather_first",
     )(x, gains)
 
 
-def scatter_kernel(p_ref, o_ref, landed, send_sem, recv_sem):
+def scatter_kernel(p_ref, o_ref, *scratch):
     greet("seq")
-    rows = o_ref.shape[0]
-    copies = start_to_peers(
-        "seq",
-        lambda peer: p_ref.at[block_of(peer, rows)],
-        lambda step: landed.at[step - 1],
-        send_sem,
-        recv_sem,
-    )
-    o_ref[...] = p_ref[block_of(lax.axis_index("seq"), rows), :].astype(F32)
-    for step, copy in enumerate(copies):
-        copy.wait()
-        o_ref[...] += landed[step].astype(F32)
+    relay = RelayScatter(p_ref, scratch[:6], scratch[6:])
+    relay.start()
+    relay.forward(o_ref)
+    relay.finish(o_ref)
 
 
 def scatter_sum(partial, n, call_id):
@@ -171,19 +365,17 @@
         out_shape=jax.ShapeDtypeStruct((rows, width), F32),
         in_specs=[VMEM_SPEC],
         out_specs=VMEM_SPEC,
-        scratch_shapes=[pltpu.VMEM((n - 1, rows, width), partial.dtype)] + semaphores(n - 1, n - 1),
+        scratch_shapes=RelayScatter.scratch(n, rows, width),
         compiler_params=communicating(call_id),
     )(partial)
 
 
 def scatter_last_kernel(
     p_ref, small_ref, down_ref, gate_up_ref, o_ref, small_out, down_all, gate_up_all,
-    landed, part_landed, part_sum, row_landed,
-    send, recv, part_send, part_recv, row_send, row_recv, down_send, down_recv, wide_send, wide_recv,
+    part_landed, part_sum, row_landed, part_send, part_recv, row_send, row_recv, *scratch,
 ):
     greet("seq", "fsdp")
     me = lax.axis_index("seq")
-    rows = o_ref.shape[0]
     part_copies = start_to_peers(
         "fsdp",
         lambda peer: small_ref.at[peer],
@@ -191,38 +383,32 @@
         part_send,
         part_recv,
     )
-    copies = start_to_peers(
-        "seq",
-        lambda peer: p_ref.at[block_of(peer, rows)],
-        lambda step: landed.at[step - 1],
-        send,
-        recv,
-    )
+    relay = RelayScatter(p_ref, scratch[:6], scratch[6:14])
+    down = gather_by_columns(down_ref, down_all, scratch[14:22])
+    gate_up = gather_by_columns(gate_up_ref, gate_up_all, scratch[22:30])
+    relay.start()
+    down.start()
+    gate_up.start()
     total = small_ref[lax.axis_index("fsdp")]
     for step, copy in enumerate(part_copies):
         copy.wait()
         total = total + part_landed[step]
     part_sum[...] = total
-    o_ref[...] = p_ref[block_of(me, rows), :].astype(F32)
+    down_all[me] = down_ref[...]
+    gate_up_all[me] = gate_up_ref[...]
     row_copies = start_to_peers(
         "seq", lambda peer: part_sum, lambda step: row_landed.at[step - 1], row_send, row_recv
     )
-    share_copies = start_to_peers(
-        "seq", lambda peer: down_ref, lambda step: down_all.at[me], down_send, down_recv
-    ) + start_to_peers(
-        "seq", lambda peer: gate_up_ref, lambda step: gate_up_all.at[me], wide_send, wide_recv
-    )
-    down_all[me] = down_ref[...]
-    gate_up_all[me] = gate_up_ref[...]
-    for step, copy in enumerate(copies):
-        copy.wait()
-        o_ref[...] += landed[step].astype(F32)
+    relay.forward(o_ref)
+    down.forward()
+    gate_up.forward()
+    relay.finish(o_ref)
     for step, copy in enumerate(row_copies):
         copy.wait()
         total = total + row_landed[step]
     small_out[...] = total
-    for copy in share_copies:
-        copy.wait()
+    down.finish()
+    gate_up.finish()
 
 
 def scatter_last(partial, small, down, gate_up, n, shards, call_id):
@@ -240,12 +426,13 @@
         in_specs=[VMEM_SPEC] * 4,
         out_specs=(VMEM_SPEC,) * 4,
         scratch_shapes=[
-            pltpu.VMEM((n - 1, rows, width), partial.dtype),
             pltpu.VMEM((shards - 1,) + piece, F32),
             pltpu.VMEM(piece, F32),
             pltpu.VMEM((n - 1,) + piece, F32),
         ]
-        + semaphores(n - 1, n - 1, shards - 1, shards - 1, *([n - 1] * 6)),
+        + semaphores(shards - 1, shards - 1, n - 1, n - 1)
+        + RelayScatter.scratch(n, rows, width)
+        + RelayGather.semaphores(n) * 2,
         compiler_params=communicating(call_id),
         name="scatter_last",
     )(partial, small, down, gate_up)
@@ -254,7 +441,7 @@
 def finish_kernel(
     qkv_ref, out_ref, q_final, k_final, v_final, out_final,
     qkv_landed, out_landed, out_mine, out_back,
-    qkv_send, qkv_recv, first_send, first_recv, second_send, second_recv,
+    first_send, first_recv, second_send, second_recv, *sems,
 ):
     greet("seq")
     n = lax.axis_size("seq")
@@ -269,9 +456,8 @@
         first_send,
         first_recv,
     )
-    beside = start_to_peers(
-        "seq", lambda peer: qkv_ref, lambda step: qkv_landed.at[step - 1], qkv_send, qkv_recv
-    )
+    relay = gather_by_columns(qkv_ref, qkv_landed, sems)
+    relay.start()
 
     def place(values, owner):
         values = values.astype(F32)
@@ -286,12 +472,14 @@
     out_mine[...] = total.astype(BF16)
     out_final[block_of(me, piece), :] = out_mine[...].astype(F32)
     place(qkv_ref[...], me)
+    relay.forward()
     second = start_to_peers(
         "seq", lambda peer: out_mine, lambda step: out_back.at[step - 1], second_send, second_recv
     )
-    for step, copy in enumerate(beside):
-        copy.wait()
-        place(qkv_landed[step], lax.rem(me + n - 1 - step, n))
+    relay.finish()
+    for step in range(n - 1):
+        owner = lax.rem(me + n - 1 - step, n)
+        place(qkv_landed[owner], owner)
     for step, copy in enumerate(second):
         copy.wait()
         owner = lax.rem(me + n - 1 - step, n)
@@ -307,12 +495,13 @@
         in_specs=[VMEM_SPEC] * 2,
         out_specs=(VMEM_SPEC,) * 4,
         scratch_shapes=[
-            pltpu.VMEM((n - 1,) + qkv.shape, BF16),
+            pltpu.VMEM((n,) + qkv.shape, BF16),
             pltpu.VMEM((n - 1, rows // n, width), BF16),
             pltpu.VMEM((rows // n, width), BF16),
             pltpu.VMEM((n - 1, rows // n, width), BF16),
         ]
-        + semaphores(*([n - 1] * 6)),
+        + semaphores(*([n - 1] * 4))
+        + RelayGather.semaphores(n),
         compiler_params=communicating(call_id),
         name="finish",
     )(qkv, out)
@@ -364,7 +553,7 @@
 def forward_kernel(
     q_pre, k_pre, v_ref, gain_q, gain_k, cos_q, sin_q, cos_k, sin_k, place_k, place_q, start_q, cot,
     out_ref, p_ref, q_ref, k_ref, cot_all,
-    v_turned, outs, cot_send, cot_recv, cot_local, send, recv, local,
+    v_turned, outs, cot_local, send, recv, local, *cot_sems,
 ):
     i, head = pl.program_id(0), pl.program_id(1)
     n, heads = pl.num_programs(0), pl.num_programs(1)
@@ -374,19 +563,7 @@
     rows = cot.shape[0]
     mine = block_of(me, rows)
 
-    def cot_copies():
-        return [
-            pltpu.make_async_remote_copy(
-                src_ref=cot,
-                dst_ref=cot_all.at[mine],
-                send_sem=cot_send.at[step - 1],
-                recv_sem=cot_recv.at[step - 1],
-                device_id={"seq": lax.rem(me + step, seq)},
-                device_id_type=MESH,
-            )
-            for step in range(1, seq)
-        ]
-
+    cot_relay = gather_by_rows(cot, cot_all, cot_sems)
     cot_own = pltpu.make_async_copy(cot, cot_all.at[mine], cot_local)
 
     def out_copy(step, which):
@@ -407,8 +584,7 @@
     @pl.when((i == 0) & (head == 0))
     def _():
         greet("seq")
-        for copy in cot_copies():
-            copy.start()
+        cot_relay.start()
         cot_own.start()
         for which in range(kv):
             own = pl.ds(which * HEAD_SIZE, HEAD_SIZE)
@@ -417,6 +593,10 @@
                 pre * inverse_rms(pre) * gain_k[...], cos_k[...], sin_k[...]
             ).astype(BF16)
             v_turned[which] = v_ref[:, own].astype(F32).T.astype(BF16)
+
+    @pl.when((i == n // 2) & (head == 0))
+    def _():
+        cot_relay.forward()
 
     @pl.when((head > 0) & (i < n - 1))
     def _():
@@ -445,8 +625,7 @@
     def _():
         for which in range(outs.shape[1]):
             own_copy(which).start()
-        for copy in cot_copies():
-            copy.wait()
+        cot_relay.finish()
         cot_own.wait()
         for step in range(seq - 1):
             for which in range(outs.shape[1]):
@@ -495,13 +674,12 @@
         scratch_shapes=[
             pltpu.VMEM((kv, HEAD_SIZE, rows), BF16),
             pltpu.VMEM((n, heads, block, HEAD_SIZE), BF16),
-            pltpu.SemaphoreType.DMA((n - 1,)),
-            pltpu.SemaphoreType.DMA((n - 1,)),
             pltpu.SemaphoreType.DMA,
             pltpu.SemaphoreType.DMA((n - 1, heads)),
             pltpu.SemaphoreType.DMA((n - 1, heads)),
             pltpu.SemaphoreType.DMA((heads,)),
-        ],
+        ]
+        + RelayGather.semaphores(n),
         compiler_params=communicating(call_id),
         name="attend_forward",
     )(
@@ -513,15 +691,14 @@
 def backward_kernel(
     p_ref, q_ref, k_ref, v_ref, q_pre, k_pre, gain_q, gain_k, cos_q, sin_q, cos_k, sin_k,
     grad_own, bulk,
-    dq_ref, dk_ref, dv_ref, dgain_q, dgain_k, bulk_landed,
-    k_turned, dk_sum, dv_sum, grads, send, recv, local, bulk_send, bulk_recv,
+    dq_ref, dk_ref, dv_ref, dgain_q, dgain_k, bulk_sum,
+    k_turned, dk_sum, dv_sum, grads, send, recv, local, *scratch,
 ):
     i, head = pl.program_id(0), pl.program_id(1)
     n, heads = pl.num_programs(0), pl.num_programs(1)
     seq = lax.axis_size("seq")
     me = lax.axis_index("seq")
     kv = k_turned.shape[0]
-    rows = grads.shape[1]
     span = grads.shape[2]
     first = (i == 0) & (head == 0)
     last = (i == n - 1) & (head == heads - 1)
@@ -537,17 +714,7 @@
             device_id_type=MESH,
         )
 
-    def bulk_copy(step):
-        peer = lax.rem(me + step, seq)
-        return pltpu.make_async_remote_copy(
-            src_ref=bulk.at[block_of(peer, rows)],
-            dst_ref=bulk_landed.at[step - 1],
-            send_sem=bulk_send.at[step - 1],
-            recv_sem=bulk_recv.at[step - 1],
-            device_id={"seq": peer},
-            device_id_type=MESH,
-        )
-
+    bulk_relay = RelayScatter(bulk, scratch[:6], scratch[6:])
     own_copy = pltpu.make_async_copy(grad_own.at[:, block_of(me, span)], grads.at[0], local)
 
     @pl.when(first)
@@ -556,8 +723,7 @@
         own_copy.start()
         for step in range(1, seq):
             grad_copy(step).start()
-        for step in range(1, seq):
-            bulk_copy(step).start()
+        bulk_relay.start()
         dgain_q[...] = jnp.zeros_like(dgain_q)
         dgain_k[...] = jnp.zeros_like(dgain_k)
         dk_sum[...] = jnp.zeros_like(dk_sum)
@@ -571,6 +737,10 @@
         @pl.when((head == 0) & (i == seq - step))
         def _():
             grad_copy(step).wait_recv()
+
+    @pl.when((i == n - 1) & (head == 0))
+    def _():
+        bulk_relay.forward(bulk_sum)
 
     slot = lax.rem(seq - i, seq)
     pair = head // GROUP
@@ -600,7 +770,7 @@
             dv_ref[:, own] = dv_sum[which].astype(BF16)
         for step in range(1, seq):
             grad_copy(step).wait_send()
-            bulk_copy(step).wait()
+        bulk_relay.finish(bulk_sum)
 
 
 def attend_backward(
@@ -625,14 +795,18 @@
             jax.ShapeDtypeStruct((rows, kv * HEAD_SIZE), BF16),
             jax.ShapeDtypeStruct((1, HEAD_SIZE), F32),
             jax.ShapeDtypeStruct((1, HEAD_SIZE), F32),
-            jax.ShapeDtypeStruct((n - 1, block, bulk.shape[1]), BF16),
+            jax.ShapeDtypeStruct((block, bulk.shape[1]), F32),
         ),
         in_specs=[
             pl.BlockSpec((1, rows, block), lambda i, h: (h, 0, turn(i))),
             q_spec, k_spec, k_spec, q_spec, k_spec, gain_spec, gain_spec,
-            trig_q, trig_q, trig_k, trig_k, ANY_SPEC, ANY_SPEC,
+            trig_q, trig_q, trig_k, trig_k, ANY_SPEC,
+            pl.BlockSpec(bulk.shape, lambda i, h: (0, 0)),
         ],
-        out_specs=(q_spec, k_spec, k_spec, gain_spec, gain_spec, ANY_SPEC),
+        out_specs=(
+            q_spec, k_spec, k_spec, gain_spec, gain_spec,
+            pl.BlockSpec((block, bulk.shape[1]), lambda i, h: (0, 0)),
+        ),
         scratch_shapes=[
             pltpu.VMEM((kv, HEAD_SIZE, rows), BF16),
             pltpu.VMEM((kv, rows, HEAD_SIZE), F32),
@@ -641,9 +815,8 @@
             pltpu.SemaphoreType.DMA((n - 1,)),
             pltpu.SemaphoreType.DMA((n - 1,)),
             pltpu.SemaphoreType.DMA,
-            pltpu.SemaphoreType.DMA((n - 1,)),
-            pltpu.SemaphoreType.DMA((n - 1,)),
-        ],
+        ]
+        + RelayScatter.scratch(n, block, bulk.shape[1]),
         compiler_params=communicating(call_id),
         name="attend_backward",
     )(
@@ -762,12 +935,11 @@
     grad_out = outer_sum(attended, grad_branch).astype(BF16)
     out_share = lax.psum_scatter(grad_out, "fsdp", scatter_dimension=0, tiled=True)
     grad_attended = back_matmul(grad_branch, out_weight).astype(BF16)
-    grad_q, grad_k, grad_v, grad_gain_query, grad_gain_key, mlp_landed = attend_backward(
+    grad_q, grad_k, grad_v, grad_gain_query, grad_gain_key, mlp_sum = attend_backward(
         weights, query, key, value, grad_attended, mlp_partial, q_pre, k_pre, gain_query,
         gain_key, cosine, sine, n, 4,
     )
-    result = middle + lax.dynamic_slice_in_dim(mlp_partial, me * resident, resident).astype(F32)
-    output = (result + jnp.sum(mlp_landed.astype(F32), axis=0)).astype(BF16)[None]
+    output = (middle + mlp_sum).astype(BF16)[None]
     grad_qkv = jnp.concatenate([grad_q, grad_k, grad_v], axis=1)
     grad_qkv_weight = outer_sum(normalized, grad_qkv).astype(BF16)
     qkv_share = lax.psum_scatter(grad_qkv_weight, "fsdp", scatter_dimension=0, tiled=True)

time: 401 us -> 391 us (0.975)
  Pallas kernels: 257 us -> 219 us
  waiting for transfers between devices: 16.3 us -> 46.4 us
    reduce_scatter x1, waiting for transfers between devices: 4.94 us -> 17.7 us  [on_device(): lax.psum_scatter(grad_out, 'fsdp', scatter_dimension=0, tiled=True)]
    pallas_call x1, Pallas kernels: 55.2 us -> 44 us  [scatter_last(): pl.pallas_call(scatter_last_kernel, out_shape=(jax.ShapeDtypeStruct((rows...]
    all_gather x1, waiting for transfers between devices: 0.02 us -> 10.4 us  [on_device(): lax.all_gather(jnp.concatenate([spread_columns(w_gate), spread_columns(w_...]
    all_gather x1, waiting for transfers between devices: 10 us -> 16.9 us  [on_device(): lax.all_gather(lax.dynamic_slice_in_dim(w_down, me * hidden_piece, hidden...]
    pallas_call x1, Pallas kernels: 27.4 us -> 21.6 us  [gather_rows(): pl.pallas_call(gather_kernel, out_shape=jax.ShapeDtypeStruct((n * rows, w...]
    pallas_call x1, Pallas kernels: 41.3 us -> 35.6 us  [attend_forward(): pl.pallas_call(forward_kernel, grid=(n, heads), out_shape=(jax.ShapeDtype...]
    pallas_call x1, Pallas kernels: 29 us -> 23.4 us  [scatter_sum(): pl.pallas_call(scatter_kernel, out_shape=jax.ShapeDtypeStruct((rows, widt...]
    pallas_call x1, Pallas kernels: 32.7 us -> 27.1 us  [gather_first(): pl.pallas_call(gather_first_kernel, out_shape=(jax.ShapeDtypeStruct((n *...]
  transfers between devices with their start and end apart: 8 -> 8, of which waited for: 2 -> 3; matrix products, arithmetic and copies ran while one was open for 17% -> 17% of each run, Pallas kernels for 58% -> 51%
where the time goes in v4:
time: 391 us; the launch traced here: 384 us
  Pallas kernels  219 us (56%)
  matrix products  63.3 us (16%)
  waiting for transfers between devices  46.4 us (12%)
  local copies, waits for them, and re-layouts  22.6 us (6%)
  other arithmetic  17.5 us (4%)
  between operations  14.9 us (4%)
    pallas_call x1, Pallas kernels, scatter_last(): pl.pallas_call(scatter_last_kernel, out_shape=(jax.ShapeDtypeStruct((rows...  44 us
    pallas_call x1, Pallas kernels, attend_backward(): pl.pallas_call(backward_kernel, grid=(n, heads), out_shape=(jax.ShapeDtyp...  39 us
    pallas_call x1, Pallas kernels, attend_forward(): pl.pallas_call(forward_kernel, grid=(n, heads), out_shape=(jax.ShapeDtype...  35.6 us
    pallas_call x1, Pallas kernels, gather_first(): pl.pallas_call(gather_first_kernel, out_shape=(jax.ShapeDtypeStruct((n *...  27.1 us
    dot_general x4, matrix products, back_matmul(): lax.dot_general(left, right, (((1,), (1,)), ((), ())), preferred_element_...  24.7 us
    pallas_call x1, Pallas kernels, finish(): pl.pallas_call(finish_kernel, out_shape=tuple((jax.ShapeDtypeStruct((qkv....  24.2 us
    pallas_call x1, Pallas kernels, scatter_sum(): pl.pallas_call(scatter_kernel, out_shape=jax.ShapeDtypeStruct((rows, widt...  23.4 us
    pallas_call x1, Pallas kernels, gather_rows(): pl.pallas_call(gather_kernel, out_shape=jax.ShapeDtypeStruct((n * rows, w...  21.6 us
  transfers between devices with their start and end apart: 8, of which 3 were waited for; matrix products, arithmetic and copies ran while one was open for 17% of the time, Pallas kernels for 51%

profile of v4, /device:TPU:0, one launch (start us, length us, event | category | flops | bytes accessed | tf_op | source)
XLA Modules:
  0.0 383.8 jit_solution(4912089205497884071)
XLA Ops:
  7.3 1.1 constant_dynamic-slice_fusion.5
  8.3 0.9 constant_dynamic-slice_fusion.3
  9.2 0.7 pad_maximum_fusion.8
  11.7 0.8 pad_maximum_fusion.7
  14.0 27.1 %gather_first.1 = (bf16[1024,1024]{1,0:T(8,128)(2,1)}, f32[8,8,128]{2,1,0:T(8,128)}) custom-call(bf16[256,1024]{1,0:T(8,128)(2,1)} %bitcast.67, f32[8,128]{1,0:T(8,128)} %fusion.30.gains_ref), custom_call_target="tpu_custom_call" | custom-call | tf_op jit(solution)/shard_map/gather_first/pallas_call | solution.py:338
  41.2 0.8 copy.46
  41.9 2.1 fusion.4
  44.9 1.9 fusion.21
  46.8 1.3 pad_maximum_fusion.5
  49.3 1.0 copy.35.place_k
  50.4 4.1 %fusion.15 = f32[1024,1024]{1,0:T(8,128)S(1)} fusion(bf16[1024,1024]{1,0:T(8,128)(2,1)} %all-gather.5.cloned.1.call-done, bf16[1024,1024]{1,0:T(8,128)(2,1)S(1)} %copy-done.5, f32[1024]{0:T(1024)S(1)} %get-tuple-element.75, f32[1024]{0:T(1024)S(1)} %add_rsqrt_fusion), kind=kOutput, calls=%fused_computation.43 | convolution fusion | flops 2151677952 | bytes 8396800 | tf_op jit(solution)/shard_map/dot_general | solution.py:26
  54.4 1.5 slice.62.q_pre
  55.9 1.1 slice.63.k_pre
  57.0 0.9 slice.80.v_ref
  57.9 35.6 %attend_forward.1 = (bf16[256,2048]{1,0:T(8,128)(2,1)}, bf16[4,1024,1024]{2,1,0:T(8,128)(2,1)}, bf16[1024,512]{1,0:T(8,128)(2,1)}, bf16[1024,256]{1,0:T(8,128)(2,1)}, bf16[1024,1024]{1,0:T(8,128)(2,1)}) custom-call(f32[1024,512]{1,0:T(8,128)} %slice.62.q_pre, f32[1024,256]{1,0:T(8,128)} %slice.63.k_pre, bf16[1024,256]{1,0:T(8,128)(2,1)} %slice.80.v_ref, ...), custom_call_target="tpu_custom_call" | custom-call | tf_op jit(solution)/shard_map/attend_forward/pallas_call | solution.py:653
  93.5 3.9 %multiply_reduce_fusion.2 = (f32[256]{0:T(256)S(1)}, f32[256,1024]{1,0:T(8,128)S(1)}) fusion(bf16[256,2048]{1,0:T(8,128)(2,1)} %get-tuple-element.41, bf16[2048,1024]{1,0:T(8,128)(2,1)} %all-gather.7.cloned.1.call-done, bf16[1,256,1024]{2,1,0:T(8,128)(2,1)S(1)} %copy-done.3), kind=kOutput, calls=%fused_computation.39 | convolution fusion | flops 1074790144 | bytes 6816768 | tf_op jit(solution)/shard_map/dot_general | solution.py:26
  97.4 1.0 multiply_convert_fusion.3.x_ref
  98.4 21.6 %shard_map.246 = bf16[1024,1024]{1,0:T(8,128)(2,1)} custom-call(bf16[256,1024]{1,0:T(8,128)(2,1)} %multiply_convert_fusion.3.x_ref), custom_call_target="tpu_custom_call" | custom-call | tf_op jit(solution)/shard_map/pallas_call | solution.py:310
  120.0 10.4 %all-gather.11.cloned.1.call-done = bf16[1024,1536]{0,1:T(8,128)(2,1)} async-done(((bf16[128,1536]{0,1:T(8,128)(2,1)}), bf16[1024,1536]{0,1:T(8,128)(2,1)}) %all-gather.11.cloned.1.call-update) | async-done | bytes 3145744 | tf_op jit(solution)/shard_map/all_gather | solution.py:876
  130.3 8.7 %fusion.35 = f32[1024,1536]{0,1:T(8,128)} fusion(bf16[1024,1024]{1,0:T(8,128)(2,1)} %shard_map.246, bf16[1024,1536]{0,1:T(8,128)(2,1)} %all-gather.11.cloned.1.call-done), kind=kOutput, calls=%fused_computation.92 | convolution fusion | flops 3221225472 | bytes 11534336 | tf_op jit(solution)/shard_map/dot_general | solution.py:26
  139.0 16.9 %all-gather.9.cloned.1.call-done = bf16[768,1024]{1,0:T(8,128)(2,1)} async-done(((bf16[96,1024]{1,0:T(8,128)(2,1)}), bf16[768,1024]{1,0:T(8,128)(2,1)}) %all-gather.9.cloned.1.call-update) | async-done | bytes 1572880 | tf_op jit(solution)/shard_map/all_gather | solution.py:879
  155.9 8.0 %multiply_convert_fusion.2 = (bf16[1024,768]{0,1:T(8,128)(2,1)S(1)}, bf16[1024,768]{0,1:T(8,128)(2,1)}, bf16[1024,768]{0,1:T(8,128)(2,1)S(1)}) fusion(f32[1024,1536]{0,1:T(8,128)} %fusion.35, bf16[1024,1024]{1,0:T(8,128)(2,1)} %get-tuple-element.45, bf16[768,1024]{1,0:T(8,128)(2,1)} %all-gather.9.cloned.1.call-done), kind=kOutput, calls=%fused_computation.14 | convolution fusion | flops 1623195648 | bytes 14680064 | tf_op jit(solution)/shard_map/dot_general | solution.py:34
  164.0 1.1 copy-done.31
  165.1 2.9 convolution_convert_fusion.5
  168.1 7.2 %convolution_convert_fusion.1 = bf16[1024,1536]{1,0:T(8,128)(2,1)} fusion(bf16[1024,1024]{1,0:T(8,128)(2,1)} %shard_map.246, bf16[1024,768]{0,1:T(8,128)(2,1)} %get-tuple-element.70, bf16[1024,768]{0,1:T(8,128)(2,1)S(1)} %get-tuple-element.69), kind=kOutput, calls=%fused_computation.10 | convolution fusion | flops 3229089792 | bytes 8388608 | tf_op jit(solution)/shard_map/dot_general | solution.py:30
  175.2 7.8 %fusion.7.p_ref = bf16[1024,1024]{1,0:T(8,128)(2,1)} fusion(bf16[1024,1536]{0,1:T(8,128)(2,1)} %all-gather.11.cloned.1.call-done, bf16[1024,768]{0,1:T(8,128)(2,1)} %get-tuple-element.70, bf16[1024,768]{0,1:T(8,128)(2,1)S(1)} %get-tuple-element.69), kind=kOutput, calls=%fused_computation.20 | convolution fusion | flops 3228565504 | bytes 8388608 | tf_op jit(solution)/shard_map/dot_general | solution.py:34
  183.7 23.4 %shard_map.247 = f32[256,1024]{1,0:T(8,128)} custom-call(bf16[1024,1024]{1,0:T(8,128)(2,1)} %fusion.7.p_ref), custom_call_target="tpu_custom_call" | custom-call | tf_op jit(solution)/shard_map/pallas_call | solution.py:363
  207.1 1.7 multiply_reduce_fusion
  209.2 0.9 copy-done.25
  210.0 2.3 convolution_convert_fusion.2.grad_own
  212.3 3.3 convolution_convert_fusion.4.bulk
  215.5 39.0 %attend_backward.1 = (bf16[1024,512]{1,0:T(8,128)(2,1)}, bf16[1024,256]{1,0:T(8,128)(2,1)}, bf16[1024,256]{1,0:T(8,128)(2,1)}, f32[1,128]{1,0:T(1,128)}, f32[1,128]{1,0:T(1,128)}, /*index=5*/f32[256,1024]{1,0:T(8,128)}) custom-call(bf16[4,1024,1024]{2,1,0:T(8,128)(2,1)} %get-tuple-element.42.p_ref, bf16[1024,512]{1,0:T(8,128)(2,1)} %get-tuple-element.43.q_ref, ...), custom_call_target="tpu_custom_call" | custom-call | tf_op jit(solution)/shard_map/attend_backward/pallas_call | solution.py:789
  254.6 1.5 constant_dynamic-update-slice_fusion.2
  256.3 1.4 copy-done.12
  257.7 4.1 %convolution_convert_fusion.3 = bf16[1024,1024]{1,0:T(8,128)(2,1)} fusion(bf16[1024,1024]{1,0:T(8,128)(2,1)S(1)} %constant_dynamic-update-slice_fusion, bf16[1024,1024]{1,0:T(8,128)(2,1)S(1)} %copy-done.6, f32[1024]{0:T(1024)S(1)} %get-tuple-element.75, f32[1024]{0:T(1024)S(1)} %add_rsqrt_fusion), kind=kOutput, calls=%fused_computation.19 | convolution fusion | flops 2152726528 | bytes 6299648 | tf_op jit(solution)/shard_map/dot_general | solution.py:30
  262.1 4.5 %convolution_convert_fusion = bf16[2048,1024]{1,0:T(8,128)(2,1)} fusion(bf16[256,2048]{1,0:T(8,128)(2,1)} %get-tuple-element.41, f32[256,1024]{1,0:T(8,128)S(1)} %subtract_add_fusion), kind=kOutput, calls=%fused_computation.9 | convolution fusion | flops 1076101120 | bytes 6291456 | tf_op jit(solution)/shard_map/dot_general | solution.py:30
  268.6 6.7 %fusion.3 = (f32[1024]{0:T(1024)S(1)}, bf16[1024,1024]{1,0:T(8,128)(2,1)}) fusion(bf16[1024,1024]{1,0:T(8,128)(2,1)} %get-tuple-element.39, f32[1024]{0:T(1024)S(1)} %add_rsqrt_fusion, bf16[1024,1024]{1,0:T(8,128)(2,1)} %copy-done.12, bf16[1024,1024]{1,0:T(8,128)(2,1)} %all-gather.5.cloned.1.call-done), kind=kOutput, calls=%fused_computation.5 | convolution fusion | flops 2152725504 | bytes 8396800 | tf_op jit(solution)/shard_map/dot_general | solution.py:34
  276.0 2.2 fusion.17
  278.2 44.0 %scatter_last.1 = (f32[256,1024]{1,0:T(8,128)}, f32[8,128]{1,0:T(8,128)}, bf16[4,96,1024]{2,1,0:T(8,128)(2,1)}, bf16[4,128,1536]{2,1,0:T(8,128)(2,1)}) custom-call(bf16[1024,1024]{1,0:T(8,128)(2,1)} %get-tuple-element.73.p_ref, f32[8,8,128]{2,1,0:T(8,128)} %bitcast.73, bf16[96,1024]{1,0:T(8,128)(2,1)} %reduce-scatter.5.cloned.1.call-done.down_ref, ...), custom_call_target="tpu_custom_call" | custom-call | tf_op jit(solution)/shard_map/scatter_last/pallas_call | solution.py:418
  322.2 3.5 spread_back.1
  327.2 1.4 bitcast_convert_fusion
  328.6 1.1 fusion.18
  329.7 17.7 %reduce-scatter.11.cloned.1.call-done.out_ref = bf16[256,1024]{1,0:T(8,128)(2,1)} async-done(((bf16[2048,1024]{1,0:T(8,128)(2,1)}), bf16[256,1024]{1,0:T(8,128)(2,1)}) %reduce-scatter.11.cloned.1.call-update) | async-done | bytes 524304 | tf_op jit(solution)/shard_map/reduce_scatter | solution.py:936
  347.4 24.2 %finish.1 = (f32[128,2048]{1,0:T(8,128)}, f32[128,1024]{1,0:T(8,128)}, f32[128,1024]{1,0:T(8,128)}, f32[256,1024]{1,0:T(8,128)}) custom-call(bf16[128,1024]{1,0:T(8,128)(2,1)} %reduce-scatter.9.cloned.1.call-done.qkv_ref, bf16[256,1024]{1,0:T(8,128)(2,1)} %reduce-scatter.11.cloned.1.call-done.out_ref), custom_call_target="tpu_custom_call" | custom-call | tf_op jit(solution)/shard_map/finish/pallas_call | solution.py:491
  371.7 2.4 copy.53
  374.1 0.8 copy.54
  374.9 0.8 copy.55
  375.7 1.0 copy.56
  (117 shorter events, 10.8 us)
Async XLA Ops:
  7.2 5.3 %copy-start = (bf16[384,1024]{1,0:T(8,128)(2,1)S(1)}, bf16[384,1024]{1,0:T(8,128)(2,1)}, u32[]{:S(2)}) copy-start(bf16[384,1024]{1,0:T(8,128)(2,1)} %param.28) | copy-start | bytes 2359300
  7.2 3.6 copy-start.9
  7.2 4.0 %copy-start.10 = (bf16[128,3072]{1,0:T(8,128)(2,1)S(1)}, bf16[128,3072]{1,0:T(8,128)(2,1)}, u32[]{:S(2)}) copy-start(bf16[128,3072]{1,0:T(8,128)(2,1)} %param.27) | copy-start | bytes 2359300
  7.2 43.1 %all-gather.5.cloned.1.call-start = ((), (), s32[]{:S(2)}) async-start(), calls=%async_computation.4 | async-start | bytes 2359296 | tf_op jit(solution)/shard_map/all_gather | solution.py:869
  10.0 83.5 %all-gather.7.cloned.1.call-start = ((), (), s32[]{:S(2)}) async-start(), calls=%async_computation.5 | async-start | bytes 4718592 | tf_op jit(solution)/shard_map/all_gather | solution.py:875
  10.7 119.6 %all-gather.11.cloned.1.call-start = ((), (), s32[]{:S(2)}) async-start(), calls=%async_computation.7 | async-start | bytes 3538944 | tf_op jit(solution)/shard_map/all_gather | solution.py:876
  11.2 2.2 copy-start.20
  11.2 2.1 copy-start.21
  11.2 2.1 copy-start.22
  11.2 2.1 copy-start.23
  11.7 32.4 %copy-start.28 = (s32[1,1024]{1,0:T(1,128)S(1)}, s32[1,1024]{1,0:T(1,128)}, u32[]{:S(2)}) copy-start(s32[1,1024]{1,0:T(1,128)} %param.17) | copy-start | bytes 12292
  11.7 32.9 %copy-start.24 = (s32[1,8]{1,0:T(1,128)S(1)}, s32[1,8]{1,0:T(1,128)}, u32[]{:S(2)}) copy-start(s32[1,8]{1,0:T(1,128)} %param.16) | copy-start | bytes 100
  12.5 143.5 %all-gather.9.cloned.1.call-start = ((), (), s32[]{:S(2)}) async-start(), calls=%async_computation.6 | async-start | bytes 1769472 | tf_op jit(solution)/shard_map/all_gather | solution.py:879
  13.3 264.9 %reduce-scatter.5.cloned.1.call-start = ((), (), s32[]{:S(2)}) async-start(), calls=%async_computation.8 | async-start | bytes 1769472 | tf_op jit(solution)/shard_map/reduce_scatter | solution.py:928
  44.6 4.7 %copy-start.17 = (s32[1024]{0:T(1024)}, s32[1024]{0:T(1024)S(1)}, u32[]{:S(2)}) copy-start(s32[1024]{0:T(1024)S(1)} %select_reduce_fusion) | copy-start | bytes 12292
  44.9 3.3 copy-start.18
  44.9 5.5 %copy-start.5 = (bf16[1024,1024]{1,0:T(8,128)(2,1)S(1)}, bf16[1024,1024]{1,0:T(8,128)(2,1)}, u32[]{:S(2)}) copy-start(bf16[1024,1024]{1,0:T(8,128)(2,1)} %get-tuple-element.39) | copy-start | bytes 6291460
  57.9 35.7 %copy-start.3 = (bf16[1,256,1024]{2,1,0:T(8,128)(2,1)S(1)}, bf16[1,256,1024]{2,1,0:T(8,128)(2,1)}, u32[]{:S(2)}) copy-start(bf16[1,256,1024]{2,1,0:T(8,128)(2,1)} %param.15) | copy-start | bytes 1572868
  155.9 9.2 %copy-start.26 = (bf16[1024,1024]{1,0:T(8,128)(2,1)S(1)}, bf16[1024,1024]{1,0:T(8,128)(2,1)}, u32[]{:S(2)}) copy-start(bf16[1024,1024]{1,0:T(8,128)(2,1)} %get-tuple-element.45) | copy-start | bytes 6291460
  164.0 1.1 copy-start.31
  183.0 95.1 %reduce-scatter.7.cloned.1.call-start = ((), (), s32[]{:S(2)}) async-start(), calls=%async_computation.9 | async-start | bytes 3538944 | tf_op jit(solution)/shard_map/reduce_scatter | solution.py:929
  183.6 25.2 %copy-start.7 = (bf16[1,256,1024]{2,1,0:T(8,128)(2,1)S(1)}, bf16[1,256,1024]{2,1,0:T(8,128)(2,1)}, u32[]{:S(2)}) copy-start(bf16[1,256,1024]{2,1,0:T(8,128)(2,1)} %param.29) | copy-start | bytes 1572868
  183.6 146.0 %reduce-scatter.9.cloned.1.call-start = ((), (), s32[]{:S(2)}) async-start(), calls=%async_computation.10 | async-start | bytes 2359296 | tf_op jit(solution)/shard_map/reduce_scatter | solution.py:945
  207.1 1.7 copy-start.2
  207.1 2.9 copy-start.25
  210.0 2.3 copy-start.27
  210.0 2.3 copy-start.32
  254.6 1.6 copy-start.14
  254.6 1.6 copy-start.13
  254.6 3.1 copy-start.6
  256.3 1.4 copy-start.12
  261.8 85.6 %reduce-scatter.11.cloned.1.call-start = ((), (), s32[]{:S(2)}) async-start(), calls=%async_computation.11 | async-start | bytes 4718592 | tf_op jit(solution)/shard_map/reduce_scatter | solution.py:936
  266.6 0.6 copy-start.30
  266.6 1.3 copy-start.29
  322.2 3.6 copy-start.4
  322.2 3.9 %copy-start.19 = (f32[8,128]{1,0:T(8,128)S(1)}, f32[8,128]{1,0:T(8,128)}, u32[]{:S(2)}) copy-start(f32[8,128]{1,0:T(8,128)} %get-tuple-element.56) | copy-start | bytes 12292
  325.8 1.4 copy-start.11
  371.7 2.5 copy-start.16
  371.7 3.3 copy-start.15
  371.7 4.1 %copy-start.8 = (f32[256,1024]{1,0:T(8,128)S(1)}, f32[256,1024]{1,0:T(8,128)}, u32[]{:S(2)}) copy-start(f32[256,1024]{1,0:T(8,128)} %get-tuple-element.119) | copy-start | bytes 3145732
  371.7 5.0 %copy-start.1 = (bf16[384,1024]{1,0:T(8,128)(2,1)S(1)}, bf16[384,1024]{1,0:T(8,128)(2,1)}, u32[]{:S(2)}) copy-start(bf16[384,1024]{1,0:T(8,128)(2,1)} %param.28) | copy-start | bytes 2359300
Sparse Core Ops, SparseCore 0:
  10.2 32.1 all-gather.4
  44.0 46.1 all-gather.6
  92.3 37.9 all-gather.10
  132.4 23.4 all-gather.8
  183.2 33.4 reduce-scatter.4
  218.8 38.5 reduce-scatter.6
  262.0 34.3 reduce-scatter.8
  298.6 48.7 reduce-scatter.10

commit v5 on v4

--- a/solution.py
+++ b/solution.py
@@ -371,8 +371,11 @@
 
 
 def scatter_last_kernel(
-    p_ref, small_ref, down_ref, gate_up_ref, o_ref, small_out, down_all, gate_up_all,
-    part_landed, part_sum, row_landed, part_send, part_recv, row_send, row_recv, *scratch,
+    p_ref, small_ref, down_ref, gate_up_ref, out_ref,
+    o_ref, small_out, down_all, gate_up_all, out_final,
+    part_landed, part_sum, row_landed, out_landed, out_mine, out_back,
+    part_send, part_recv, row_send, row_recv, first_send, first_recv, second_send, second_recv,
+    *scratch,
 ):
     greet("seq", "fsdp")
     me = lax.axis_index("seq")
@@ -387,6 +390,14 @@
     down = gather_by_columns(down_ref, down_all, scratch[14:22])
     gate_up = gather_by_columns(gate_up_ref, gate_up_all, scratch[22:30])
     relay.start()
+    piece = out_mine.shape[0]
+    first = start_to_peers(
+        "seq",
+        lambda peer: out_ref.at[block_of(peer, piece)],
+        lambda step: out_landed.at[step - 1],
+        first_send,
+        first_recv,
+    )
     down.start()
     gate_up.start()
     total = small_ref[lax.axis_index("fsdp")]
@@ -400,7 +411,16 @@
         "seq", lambda peer: part_sum, lambda step: row_landed.at[step - 1], row_send, row_recv
     )
     relay.forward(o_ref)
+    out_total = out_ref[block_of(me, piece), :].astype(F32)
+    for step, copy in enumerate(first):
+        copy.wait()
+        out_total = out_total + out_landed[step].astype(F32)
+    out_mine[...] = out_total.astype(BF16)
     down.forward()
+    out_final[block_of(me, piece), :] = out_mine[...].astype(F32)
+    second = start_to_peers(
+        "seq", lambda peer: out_mine, lambda step: out_back.at[step - 1], second_send, second_recv
+    )
     gate_up.forward()
     relay.finish(o_ref)
     for step, copy in enumerate(row_copies):
@@ -408,10 +428,14 @@
         total = total + row_landed[step]
     small_out[...] = total
     down.finish()
+    n = lax.axis_size("seq")
+    for step, copy in enumerate(second):
+        copy.wait()
+        out_final[block_of(lax.rem(me + n - 1 - step, n), piece), :] = out_back[step].astype(F32)
     gate_up.finish()
 
 
-def scatter_last(partial, small, down, gate_up, n, shards, call_id):
+def scatter_last(partial, small, down, gate_up, out, n, shards, call_id):
     total, width = partial.shape
     rows = total // n
     piece = small.shape[1:]
@@ -422,42 +446,32 @@
             jax.ShapeDtypeStruct(piece, F32),
             jax.ShapeDtypeStruct((n,) + down.shape, BF16),
             jax.ShapeDtypeStruct((n,) + gate_up.shape, BF16),
+            jax.ShapeDtypeStruct(out.shape, F32),
         ),
-        in_specs=[VMEM_SPEC] * 4,
-        out_specs=(VMEM_SPEC,) * 4,
+        in_specs=[VMEM_SPEC] * 5,
+        out_specs=(VMEM_SPEC,) * 5,
         scratch_shapes=[
             pltpu.VMEM((shards - 1,) + piece, F32),
             pltpu.VMEM(piece, F32),
             pltpu.VMEM((n - 1,) + piece, F32),
+            pltpu.VMEM((n - 1, out.shape[0] // n, width), BF16),
+            pltpu.VMEM((out.shape[0] // n, width), BF16),
+            pltpu.VMEM((n - 1, out.shape[0] // n, width), BF16),
         ]
-        + semaphores(shards - 1, shards - 1, n - 1, n - 1)
+        + semaphores(shards - 1, shards - 1, *([n - 1] * 6))
         + RelayScatter.scratch(n, rows, width)
         + RelayGather.semaphores(n) * 2,
         compiler_params=communicating(call_id),
         name="scatter_last",
-    )(partial, small, down, gate_up)
-
-
-def finish_kernel(
-    qkv_ref, out_ref, q_final, k_final, v_final, out_final,
-    qkv_landed, out_landed, out_mine, out_back,
-    first_send, first_recv, second_send, second_recv, *sems,
-):
+    )(partial, small, down, gate_up, out)
+
+
+def finish_kernel(qkv_ref, q_final, k_final, v_final, qkv_landed, *sems):
     greet("seq")
     n = lax.axis_size("seq")
     me = lax.axis_index("seq")
-    piece = out_mine.shape[0]
     split = q_final.shape[1] // n
     narrow = k_final.shape[1] // n
-    first = start_to_peers(
-        "seq",
-        lambda peer: out_ref.at[block_of(peer, piece)],
-        lambda step: out_landed.at[step - 1],
-        first_send,
-        first_recv,
-    )
-    relay = gather_by_columns(qkv_ref, qkv_landed, sems)
-    relay.start()
 
     def place(values, owner):
         values = values.astype(F32)
@@ -465,46 +479,26 @@
         k_final[:, block_of(owner, narrow)] = values[:, split : split + narrow]
         v_final[:, block_of(owner, narrow)] = values[:, split + narrow :]
 
-    total = out_ref[block_of(me, piece), :].astype(F32)
-    for step, copy in enumerate(first):
-        copy.wait()
-        total = total + out_landed[step].astype(F32)
-    out_mine[...] = total.astype(BF16)
-    out_final[block_of(me, piece), :] = out_mine[...].astype(F32)
+    relay = gather_by_columns(qkv_ref, qkv_landed, sems)
+    relay.start()
     place(qkv_ref[...], me)
     relay.forward()
-    second = start_to_peers(
-        "seq", lambda peer: out_mine, lambda step: out_back.at[step - 1], second_send, second_recv
-    )
     relay.finish()
-    for step in range(n - 1):
-        owner = lax.rem(me + n - 1 - step, n)
+    for step in range(1, n):
+        owner = lax.rem(me + step, n)
         place(qkv_landed[owner], owner)
-    for step, copy in enumerate(second):
-        copy.wait()
-        owner = lax.rem(me + n - 1 - step, n)
-        out_final[block_of(owner, piece), :] = out_back[step].astype(F32)
-
-
-def finish(qkv, out, widths, n, call_id):
-    rows, width = out.shape
+
+
+def finish(qkv, widths, n, call_id):
     return pl.pallas_call(
         finish_kernel,
-        out_shape=tuple(jax.ShapeDtypeStruct((qkv.shape[0], size), F32) for size in widths)
-        + (jax.ShapeDtypeStruct(out.shape, F32),),
-        in_specs=[VMEM_SPEC] * 2,
-        out_specs=(VMEM_SPEC,) * 4,
-        scratch_shapes=[
-            pltpu.VMEM((n,) + qkv.shape, BF16),
-            pltpu.VMEM((n - 1, rows // n, width), BF16),
-            pltpu.VMEM((rows // n, width), BF16),
-            pltpu.VMEM((n - 1, rows // n, width), BF16),
-        ]
-        + semaphores(*([n - 1] * 4))
-        + RelayGather.semaphores(n),
+        out_shape=tuple(jax.ShapeDtypeStruct((qkv.shape[0], size), F32) for size in widths),
+        in_specs=[VMEM_SPEC],
+        out_specs=(VMEM_SPEC,) * 3,
+        scratch_shapes=[pltpu.VMEM((n,) + qkv.shape, BF16)] + RelayGather.semaphores(n),
         compiler_params=communicating(call_id),
         name="finish",
-    )(qkv, out)
+    )(qkv)
 
 
 def spread_kernel(hidden_piece, pieces_ref, gate_ref, up_ref):
@@ -866,19 +860,26 @@
     gain_query = gains[:, 2 * part : 2 * part + small].reshape(1, -1)
     gain_key = gains[:, 2 * part + small : 2 * part + 2 * small].reshape(1, -1)
 
-    qkv_weight = lax.all_gather(
+    def gathered(*weights):
+        sizes = [weight.shape[0] for weight in weights]
+        if len({weight.shape[1] for weight in weights}) > 1:
+            return [lax.all_gather(weight, "fsdp", axis=0, tiled=True) for weight in weights]
+        joined = lax.all_gather(jnp.concatenate(weights, axis=0), "fsdp", axis=0)
+        starts = [sum(sizes[:i]) for i in range(len(sizes))]
+        return [
+            joined[:, start : start + size].reshape(-1, joined.shape[2])
+            for start, size in zip(starts, sizes)
+        ]
+
+    qkv_weight, down_weight = gathered(
         jnp.concatenate(
             [columns(w_query, n), columns(key_projection, n), columns(value_projection, n)], axis=1
         ),
-        "fsdp", axis=0, tiled=True,
+        lax.dynamic_slice_in_dim(w_down, me * hidden_piece, hidden_piece, axis=0),
     )
     out_weight = lax.all_gather(w_out, "fsdp", axis=0, tiled=True)
     gate_up_weight = lax.all_gather(
         jnp.concatenate([spread_columns(w_gate), spread_columns(w_up)], axis=1), "fsdp", axis=0, tiled=True
-    )
-    down_weight = lax.all_gather(
-        lax.dynamic_slice_in_dim(w_down, me * hidden_piece, hidden_piece, axis=0),
-        "fsdp", axis=0, tiled=True,
     )
 
     order = packing[0]
@@ -909,6 +910,7 @@
     normed_post_mine = (middle * inverse_rms(middle) * gain_post).astype(BF16)
     normed_post = gather_rows(normed_post_mine, n, 2)
 
+    grad_hidden = lax.optimization_barrier(back_matmul(grad_mlp, down_weight))
     gate_up = matrix_product(normed_post, gate_up_weight)
     units = shards * hidden_piece
     gate, up = gate_up[:, :units], gate_up[:, units:]
@@ -916,7 +918,6 @@
     hidden = (gate / (1.0 + jnp.exp(-gate)) * up).astype(BF16)
     mlp_partial = matrix_product(hidden, down_weight).astype(BF16)
 
-    grad_hidden = back_matmul(grad_mlp, down_weight)
     grad_down = outer_sum(hidden, grad_mlp).astype(BF16)
     grad_gate = (grad_hidden * up * (logistic + gate * logistic * (1.0 - logistic))).astype(BF16)
     grad_up = (grad_hidden * gate * logistic).astype(BF16)
@@ -925,7 +926,6 @@
     grad_partial, grad_down, grad_gate_up_weight = lax.optimization_barrier(
         (back_matmul(grad_gate_up, gate_up_weight).astype(BF16), grad_down, grad_gate_up_weight)
     )
-    down_share = lax.psum_scatter(grad_down, "fsdp", scatter_dimension=0, tiled=True)
     gate_up_share = lax.psum_scatter(grad_gate_up_weight, "fsdp", scatter_dimension=0, tiled=True)
     grad_normed_post = scatter_sum(grad_partial, n, 3)
     grad_middle, gain_rows = rms_backward(middle, gain_post, grad_normed_post)
@@ -933,7 +933,13 @@
     grad_gain_post = jnp.sum(gain_rows, axis=0)
     grad_branch = grad_middle.astype(BF16)
     grad_out = outer_sum(attended, grad_branch).astype(BF16)
-    out_share = lax.psum_scatter(grad_out, "fsdp", scatter_dimension=0, tiled=True)
+    out_down_share = lax.psum_scatter(
+        jnp.concatenate(
+            [grad_out.reshape(shards, -1, width), grad_down.reshape(shards, -1, width)], axis=1
+        ).reshape(-1, width),
+        "fsdp", scatter_dimension=0, tiled=True,
+    )
+    out_share, down_share = out_down_share[: w_out.shape[0]], out_down_share[w_out.shape[0] :]
     grad_attended = back_matmul(grad_branch, out_weight).astype(BF16)
     grad_q, grad_k, grad_v, grad_gain_query, grad_gain_key, mlp_sum = attend_backward(
         weights, query, key, value, grad_attended, mlp_partial, q_pre, k_pre, gain_query,
@@ -947,8 +953,8 @@
     grad_gain_in = jnp.sum(partial * unit, axis=0)
     small_grads = [grad_gain_in, grad_gain_post, grad_gain_query, grad_gain_key]
     small_grads = tile_of(jnp.concatenate([g.reshape(shards, -1) for g in small_grads], axis=1))
-    grad_normed, gain_shares, down_all, gate_up_all = scatter_last(
-        partial.astype(BF16), small_grads, down_share, gate_up_share, n, shards, 5
+    grad_normed, gain_shares, down_all, gate_up_all, final_out = scatter_last(
+        partial.astype(BF16), small_grads, down_share, gate_up_share, out_share, n, shards, 5
     )
     gain_shares = gain_shares.reshape(-1)
     grad_inputs, _ = rms_backward(inputs, gain_in, grad_normed)
@@ -956,8 +962,8 @@
 
     final_down = down_all.astype(F32).reshape(-1, width)
     final_gate, final_up = spread_back(gate_up_all, hidden_piece)
-    final_query, final_key, final_value, final_out = finish(
-        qkv_share, out_share, (HQ * HEAD_SIZE,) + (KEY_VALUE_HEADS * HEAD_SIZE,) * 2, n, 6
+    final_query, final_key, final_value = finish(
+        qkv_share, (HQ * HEAD_SIZE,) + (KEY_VALUE_HEADS * HEAD_SIZE,) * 2, n, 6
     )
 
     return (

time: 391 us -> 473 us (1.21)
  waiting for transfers between devices: 46.4 us -> 125 us
  matrix products: 63.3 us -> 52.1 us
  other arithmetic: 17.5 us -> 24.7 us
  local copies, waits for them, and re-layouts: 22.6 us -> 29 us
    reduce_scatter x1, waiting for transfers between devices: 0.01 us -> 37.5 us  [on_device(): lax.psum_scatter(grad_gate_up_weight, 'fsdp', scatter_dimension=0, tiled=...]
    reduce_scatter x2 -> x1, waiting for transfers between devices: 17.7 us -> 52.4 us  [on_device(): lax.psum_scatter(jnp.concatenate([grad_out.reshape(shards, -1, width), gr...]
    reduce_scatter x1, waiting for transfers between devices: 0.01 us -> 16.4 us  [on_device(): lax.psum_scatter(grad_qkv_weight, 'fsdp', scatter_dimension=0, tiled=True)]
    pallas_call x1, Pallas kernels: 44 us -> 55.9 us  [scatter_last(): pl.pallas_call(scatter_last_kernel, out_shape=(jax.ShapeDtypeStruct((rows...]
    pallas_call x1, Pallas kernels: 24.2 us -> 13.1 us  [finish(): pl.pallas_call(finish_kernel, out_shape=tuple((jax.ShapeDtypeStruct((qkv....]
    all_gather x2 -> x1, waiting for transfers between devices: 16.9 us -> 7.41 us  [gathered(): joined = lax.all_gather(jnp.concatenate(weights, axis=0), 'fsdp', axis=0)]
    slice x0 -> x4, local copies, waits for them, and re-layouts: none -> 6.9 us  [the longest x2 3.42 us: gathered(): joined[:, start:start + size].reshape(-1, joined.shape[2])]
    unnamed x76 -> x82, local copies, waits for them, and re-layouts: 12.3 us -> 11 us
  transfers between devices with their start and end apart: 8 -> 6, of which waited for: 3 -> 5; matrix products, arithmetic and copies ran while one was open for 17% -> 11% of each run, Pallas kernels for 51% -> 21%
where the time goes in v5:
time: 473 us; the launch traced here: 466 us
  Pallas kernels  220 us (47%)
  waiting for transfers between devices  125 us (26%)
  matrix products  52.1 us (11%)
  local copies, waits for them, and re-layouts  29 us (6%)
  other arithmetic  24.7 us (5%)
  between operations  14.9 us (3%)
    pallas_call x1, Pallas kernels, scatter_last(): pl.pallas_call(scatter_last_kernel, out_shape=(jax.ShapeDtypeStruct((rows...  55.9 us
    reduce_scatter x1, waiting for transfers between devices, on_device(): lax.psum_scatter(jnp.concatenate([grad_out.reshape(shards, -1, width), gr...  52.4 us
    pallas_call x1, Pallas kernels, attend_backward(): pl.pallas_call(backward_kernel, grid=(n, heads), out_shape=(jax.ShapeDtyp...  39 us
    reduce_scatter x1, waiting for transfers between devices, on_device(): lax.psum_scatter(grad_gate_up_weight, 'fsdp', scatter_dimension=0, tiled=...  37.5 us
    pallas_call x1, Pallas kernels, attend_forward(): pl.pallas_call(forward_kernel, grid=(n, heads), out_shape=(jax.ShapeDtype...  36.3 us
    pallas_call x1, Pallas kernels, gather_first(): pl.pallas_call(gather_first_kernel, out_shape=(jax.ShapeDtypeStruct((n *...  27 us
    pallas_call x1, Pallas kernels, scatter_sum(): pl.pallas_call(scatter_kernel, out_shape=jax.ShapeDtypeStruct((rows, widt...  23.5 us
    pallas_call x1, Pallas kernels, gather_rows(): pl.pallas_call(gather_kernel, out_shape=jax.ShapeDtypeStruct((n * rows, w...  22.2 us
  transfers between devices with their start and end apart: 6, of which 5 were waited for; matrix products, arithmetic and copies ran while one was open for 11% of the time, Pallas kernels for 21%

profile of v5, /device:TPU:0, one launch (start us, length us, event | category | flops | bytes accessed | tf_op | source)
XLA Modules:
  0.0 466.3 jit_solution(5203705458245379678)
XLA Ops:
  7.3 1.1 copy-done
  14.2 27.0 %gather_first.1 = (bf16[1024,1024]{1,0:T(8,128)(2,1)}, f32[8,8,128]{2,1,0:T(8,128)}) custom-call(bf16[256,1024]{1,0:T(8,128)(2,1)} %bitcast.75, f32[8,128]{1,0:T(8,128)} %fusion.30.gains_ref), custom_call_target="tpu_custom_call" | custom-call | tf_op jit(solution)/shard_map/gather_first/pallas_call | solution.py:338
  44.1 1.0 copy.31.place_k
  45.3 1.9 fusion.21
  47.2 1.3 pad_maximum_fusion.6
  49.0 7.4 %all-gather.9.cloned.1.call-done = bf16[1792,1024]{1,0:T(8,128)(2,1)} async-done(((bf16[224,1024]{1,0:T(8,128)(2,1)}), bf16[1792,1024]{1,0:T(8,128)(2,1)}) %all-gather.9.cloned.1.call-update) | async-done | bytes 3670032 | tf_op jit(solution)/shard_map/all_gather | solution.py:867
  56.4 1.8 slice.78
  58.2 2.4 fusion.15
  60.6 1.6 slice.79.q_pre
  62.2 1.1 slice.80.k_pre
  64.1 1.7 slice.84
  65.8 36.3 %attend_forward.1 = (bf16[256,2048]{1,0:T(8,128)(2,1)}, bf16[4,1024,1024]{2,1,0:T(8,128)(2,1)}, bf16[1024,512]{1,0:T(8,128)(2,1)}, bf16[1024,256]{1,0:T(8,128)(2,1)}, bf16[1024,1024]{1,0:T(8,128)(2,1)}) custom-call(f32[1024,512]{1,0:T(8,128)} %slice.79.q_pre, f32[1024,256]{1,0:T(8,128)} %slice.80.k_pre, bf16[1024,256]{1,0:T(8,128)(2,1)} %slice.100.v_ref, ...), custom_call_target="tpu_custom_call" | custom-call | tf_op jit(solution)/shard_map/attend_forward/pallas_call | solution.py:647
  102.2 5.2 %fusion.35 = f32[1024,768]{1,0:T(8,128)} fusion(bf16[1024,1024]{1,0:T(8,128)(2,1)} %get-tuple-element.45, bf16[768,1024]{1,0:T(8,128)(2,1)S(1)} %bitcast.81), kind=kOutput, calls=%fused_computation.93 | convolution fusion | flops 1610612736 | bytes 6815744 | tf_op jit(solution)/shard_map/dot_general | solution.py:34
  107.4 3.5 multiply_reduce_fusion.2
  111.9 22.2 %shard_map.246 = bf16[1024,1024]{1,0:T(8,128)(2,1)} custom-call(bf16[256,1024]{1,0:T(8,128)(2,1)} %multiply_convert_fusion.3.x_ref), custom_call_target="tpu_custom_call" | custom-call | tf_op jit(solution)/shard_map/pallas_call | solution.py:310
  134.1 9.8 %all-gather.7.cloned.1.call-done = bf16[1024,1536]{0,1:T(8,128)(2,1)} async-done(((bf16[128,1536]{0,1:T(8,128)(2,1)}), bf16[1024,1536]{0,1:T(8,128)(2,1)}) %all-gather.7.cloned.1.call-update) | async-done | bytes 3145744 | tf_op jit(solution)/shard_map/all_gather | solution.py:881
  143.9 6.1 %fusion.36 = f32[1024,1536]{1,0:T(8,128)S(1)} fusion(bf16[1024,1024]{1,0:T(8,128)(2,1)} %shard_map.246, bf16[1024,1536]{0,1:T(8,128)(2,1)} %all-gather.7.cloned.1.call-done), kind=kOutput, calls=%fused_computation.94 | convolution fusion | flops 3221225472 | bytes 11534336 | tf_op jit(solution)/shard_map/dot_general | solution.py:26
  150.1 2.0 multiply_convert_fusion.2
  152.1 3.0 convolution_convert_fusion.5
  155.1 3.2 convolution_convert_fusion.4.bulk
  158.3 5.4 %convolution_convert_fusion.1 = bf16[1024,1536]{1,0:T(8,128)(2,1)} fusion(bf16[1024,1024]{1,0:T(8,128)(2,1)S(1)} %copy-done.6, bf16[1024,768]{1,0:T(8,128)(2,1)S(1)} %get-tuple-element.70, bf16[1024,768]{1,0:T(8,128)(2,1)S(1)} %get-tuple-element.69), kind=kOutput, calls=%fused_computation.11 | convolution fusion | flops 3229089792 | bytes 8388608 | tf_op jit(solution)/shard_map/dot_general | solution.py:30
  163.7 7.6 %fusion.7.p_ref = bf16[1024,1024]{1,0:T(8,128)(2,1)} fusion(bf16[1024,1536]{0,1:T(8,128)(2,1)} %all-gather.7.cloned.1.call-done, bf16[1024,768]{1,0:T(8,128)(2,1)} %copy-done.12, bf16[1024,768]{1,0:T(8,128)(2,1)} %copy-done.11), kind=kOutput, calls=%fused_computation.21 | convolution fusion | flops 3228565504 | bytes 8388608 | tf_op jit(solution)/shard_map/dot_general | solution.py:34
  171.3 23.5 %shard_map.247 = f32[256,1024]{1,0:T(8,128)} custom-call(bf16[1024,1024]{1,0:T(8,128)(2,1)} %fusion.7.p_ref), custom_call_target="tpu_custom_call" | custom-call | tf_op jit(solution)/shard_map/pallas_call | solution.py:363
  194.8 1.7 multiply_reduce_fusion
  196.5 1.5 subtract_add_fusion
  198.1 2.3 convolution_convert_fusion.2.grad_own
  200.3 39.0 %attend_backward.1 = (bf16[1024,512]{1,0:T(8,128)(2,1)}, bf16[1024,256]{1,0:T(8,128)(2,1)}, bf16[1024,256]{1,0:T(8,128)(2,1)}, f32[1,128]{1,0:T(1,128)}, f32[1,128]{1,0:T(1,128)}, /*index=5*/f32[256,1024]{1,0:T(8,128)}) custom-call(bf16[4,1024,1024]{2,1,0:T(8,128)(2,1)} %get-tuple-element.42.p_ref, bf16[1024,512]{1,0:T(8,128)(2,1)} %get-tuple-element.43.q_ref, ...), custom_call_target="tpu_custom_call" | custom-call | tf_op jit(solution)/shard_map/attend_backward/pallas_call | solution.py:783
  239.3 1.5 constant_dynamic-update-slice_fusion.2
  240.8 1.1 constant_dynamic-update-slice_fusion.1
  242.0 1.4 copy-done.20
  243.4 4.1 convolution_convert_fusion.3
  247.6 2.6 convolution_convert_fusion
  250.2 3.1 pad_maximum_fusion
  256.0 6.6 %fusion.3 = (f32[1024]{0:T(1024)S(1)}, bf16[1024,1024]{1,0:T(8,128)(2,1)}) fusion(bf16[1024,1024]{1,0:T(8,128)(2,1)} %get-tuple-element.39, f32[1024]{0:T(1024)S(1)} %add_rsqrt_fusion, bf16[1024,1024]{1,0:T(8,128)(2,1)} %copy-done.20, bf16[1024,1024]{1,0:T(8,128)(2,1)} %bitcast.79), kind=kOutput, calls=%fused_computation.6 | convolution fusion | flops 2152725504 | bytes 8396800 | tf_op jit(solution)/shard_map/dot_general | solution.py:34
  263.3 2.1 fusion.17
  265.5 16.4 %reduce-scatter.8.cloned.1.call-done.qkv_ref = bf16[128,1024]{1,0:T(8,128)(2,1)} async-done(((bf16[1024,1024]{1,0:T(8,128)(2,1)}), bf16[128,1024]{1,0:T(8,128)(2,1)}) %reduce-scatter.8.cloned.1.call-update) | async-done | bytes 262160 | tf_op jit(solution)/shard_map/reduce_scatter | solution.py:951
  281.9 13.1 %finish.1 = (f32[128,2048]{1,0:T(8,128)}, f32[128,1024]{1,0:T(8,128)}, f32[128,1024]{1,0:T(8,128)}) custom-call(bf16[128,1024]{1,0:T(8,128)(2,1)} %reduce-scatter.8.cloned.1.call-done.qkv_ref), custom_call_target="tpu_custom_call" | custom-call | tf_op jit(solution)/shard_map/finish/pallas_call | solution.py:493
  295.0 52.4 %reduce-scatter.4.cloned.1.call-done = bf16[352,1024]{1,0:T(8,128)(2,1)} async-done(((bf16[2816,1024]{1,0:T(8,128)(2,1)}), bf16[352,1024]{1,0:T(8,128)(2,1)}) %reduce-scatter.4.cloned.1.call-update) | async-done | bytes 720912 | tf_op jit(solution)/shard_map/reduce_scatter | solution.py:936
  347.4 1.6 slice.88.down_ref
  349.1 1.9 slice.89.out_ref
  350.9 37.5 %reduce-scatter.6.cloned.1.call-done.gate_up_ref = bf16[128,1536]{1,0:T(8,128)(2,1)} async-done(((bf16[1024,1536]{1,0:T(8,128)(2,1)}), bf16[128,1536]{1,0:T(8,128)(2,1)}) %reduce-scatter.6.cloned.1.call-update) | async-done | bytes 393232 | tf_op jit(solution)/shard_map/reduce_scatter | solution.py:929
  388.5 55.9 %scatter_last.1 = (f32[256,1024]{1,0:T(8,128)}, f32[8,128]{1,0:T(8,128)}, bf16[4,96,1024]{2,1,0:T(8,128)(2,1)}, bf16[4,128,1536]{2,1,0:T(8,128)(2,1)}, f32[256,1024]{1,0:T(8,128)}) custom-call(bf16[1024,1024]{1,0:T(8,128)(2,1)} %get-tuple-element.73.p_ref, f32[8,8,128]{2,1,0:T(8,128)} %bitcast.88, bf16[96,1024]{1,0:T(8,128)(2,1)} %slice.88.down_ref, ...), custom_call_target="tpu_custom_call" | custom-call | tf_op jit(solution)/shard_map/scatter_last/pallas_call | solution.py:442
  444.4 1.6 fusion.8
  446.0 1.3 slice_bitcast_fusion.2
  447.3 1.3 fusion.34
  448.6 3.5 spread_back.1
  452.1 2.5 bitcast_convert_fusion
  454.6 1.1 fusion.18
  (123 shorter events, 18.1 us)
Async XLA Ops:
  7.2 1.1 copy-start
  7.2 4.6 copy-start.18
  7.2 5.0 %copy-start.19 = (bf16[128,3072]{1,0:T(8,128)(2,1)S(1)}, bf16[128,3072]{1,0:T(8,128)(2,1)}, u32[]{:S(2)}) copy-start(bf16[128,3072]{1,0:T(8,128)(2,1)} %param.27) | copy-start | bytes 2359300
  7.2 49.2 %all-gather.9.cloned.1.call-start = ((), (), s32[]{:S(2)}) async-start(), calls=%async_computation.8 | async-start | bytes 4128768 | tf_op jit(solution)/shard_map/all_gather | solution.py:867
  11.0 2.5 copy-start.26
  11.0 2.5 copy-start.27
  11.0 2.5 copy-start.28
  11.0 2.5 copy-start.29
  11.0 32.4 %copy-start.30 = (s32[1,8]{1,0:T(1,128)S(1)}, s32[1,8]{1,0:T(1,128)}, u32[]{:S(2)}) copy-start(s32[1,8]{1,0:T(1,128)} %param.16) | copy-start | bytes 100
  11.0 32.6 %copy-start.33 = (s32[1,1024]{1,0:T(1,128)S(1)}, s32[1,1024]{1,0:T(1,128)}, u32[]{:S(2)}) copy-start(s32[1,1024]{1,0:T(1,128)} %param.17) | copy-start | bytes 12292
  11.0 96.4 %all-gather.5.cloned.1.call-start = ((), (), s32[]{:S(2)}) async-start(), calls=%async_computation.3 | async-start | bytes 4718592 | tf_op jit(solution)/shard_map/all_gather | solution.py:880
  11.8 132.1 %all-gather.7.cloned.1.call-start = ((), (), s32[]{:S(2)}) async-start(), calls=%async_computation.4 | async-start | bytes 3538944 | tf_op jit(solution)/shard_map/all_gather | solution.py:881
  13.4 268.4 %reduce-scatter.8.cloned.1.call-start = ((), (), s32[]{:S(2)}) async-start(), calls=%async_computation.7 | async-start | bytes 2359296 | tf_op jit(solution)/shard_map/reduce_scatter | solution.py:951
  41.2 7.2 %copy-start.7 = (bf16[1024,1024]{1,0:T(8,128)(2,1)S(1)}, bf16[1024,1024]{1,0:T(8,128)(2,1)}, u32[]{:S(2)}) copy-start(bf16[1024,1024]{1,0:T(8,128)(2,1)} %get-tuple-element.39) | copy-start | bytes 6291460
  44.1 4.9 %copy-start.24 = (s32[1024]{0:T(1024)}, s32[1024]{0:T(1024)S(1)}, u32[]{:S(2)}) copy-start(s32[1024]{0:T(1024)S(1)} %select_reduce_fusion) | copy-start | bytes 12292
  45.2 3.7 copy-start.25
  58.2 2.4 copy-start.9
  65.8 36.4 %copy-start.13 = (bf16[8,96,1024]{2,1,0:T(8,128)(2,1)}, bf16[8,96,1024]{2,1,0:T(8,128)(2,1)S(1)}, u32[]{:S(2)}) copy-start(bf16[8,96,1024]{2,1,0:T(8,128)(2,1)S(1)} %slice.84) | copy-start | bytes 4718596
  102.2 5.2 %copy-start.2 = (bf16[1,256,1024]{2,1,0:T(8,128)(2,1)S(1)}, bf16[1,256,1024]{2,1,0:T(8,128)(2,1)}, u32[]{:S(2)}) copy-start(bf16[1,256,1024]{2,1,0:T(8,128)(2,1)} %param.15) | copy-start | bytes 1572868
  102.2 5.2 %copy-start.5 = (bf16[256,2048]{1,0:T(8,128)(2,1)S(1)}, bf16[256,2048]{1,0:T(8,128)(2,1)}, u32[]{:S(2)}) copy-start(bf16[256,2048]{1,0:T(8,128)(2,1)} %get-tuple-element.41) | copy-start | bytes 3145732
  143.9 6.1 %copy-start.4 = (f32[1024,768]{1,0:T(8,128)S(1)}, f32[1024,768]{1,0:T(8,128)}, u32[]{:S(2)}) copy-start(f32[1024,768]{1,0:T(8,128)} %fusion.35) | copy-start | bytes 9437188
  150.1 2.0 copy-start.32
  152.1 6.2 %copy-start.11 = (bf16[1024,768]{1,0:T(8,128)(2,1)}, bf16[1024,768]{1,0:T(8,128)(2,1)S(1)}, u32[]{:S(2)}) copy-start(bf16[1024,768]{1,0:T(8,128)(2,1)S(1)} %get-tuple-element.69) | copy-start | bytes 4718596
  152.1 6.2 %copy-start.12 = (bf16[1024,768]{1,0:T(8,128)(2,1)}, bf16[1024,768]{1,0:T(8,128)(2,1)S(1)}, u32[]{:S(2)}) copy-start(bf16[1024,768]{1,0:T(8,128)(2,1)S(1)} %get-tuple-element.70) | copy-start | bytes 4718596
  152.1 3.0 copy-start.14
  155.1 3.2 copy-start.6
  171.3 25.2 %copy-start.10 = (bf16[1,256,1024]{2,1,0:T(8,128)(2,1)S(1)}, bf16[1,256,1024]{2,1,0:T(8,128)(2,1)}, u32[]{:S(2)}) copy-start(bf16[1,256,1024]{2,1,0:T(8,128)(2,1)} %param.29) | copy-start | bytes 1572868
  194.8 3.2 copy-start.31
  239.3 2.6 copy-start.23
  239.3 4.1 copy-start.8
  242.0 1.4 copy-start.20
  247.5 99.9 %reduce-scatter.4.cloned.1.call-start = ((), (), s32[]{:S(2)}) async-start(), calls=%async_computation.5 | async-start | bytes 6488064 | tf_op jit(solution)/shard_map/reduce_scatter | solution.py:936
  247.6 2.6 copy-start.15
  253.4 1.1 copy-start.35
  253.4 1.9 copy-start.34
  253.4 135.1 %reduce-scatter.6.cloned.1.call-start = ((), (), s32[]{:S(2)}) async-start(), calls=%async_computation.6 | async-start | bytes 3538944 | tf_op jit(solution)/shard_map/reduce_scatter | solution.py:929
  444.4 10.3 %copy-start.3 = (f32[256,1024]{1,0:T(8,128)S(1)}, f32[256,1024]{1,0:T(8,128)}, u32[]{:S(2)}) copy-start(f32[256,1024]{1,0:T(8,128)} %get-tuple-element.55) | copy-start | bytes 3145732
  452.1 3.7 copy-start.16
  454.6 2.1 copy-start.22
  454.6 2.9 copy-start.21
  454.6 3.7 copy-start.17
  455.7 3.5 copy-start.1
Sparse Core Ops, SparseCore 0:
  11.1 45.2 all-gather.8
  58.0 45.6 all-gather.4
  105.9 37.9 all-gather.6
  247.6 34.1 reduce-scatter.7
  284.0 63.3 reduce-scatter.3
  349.6 38.8 reduce-scatter.5

commit v6 on v5

--- a/solution.py
+++ b/solution.py
@@ -371,14 +371,10 @@
 
 
 def scatter_last_kernel(
-    p_ref, small_ref, down_ref, gate_up_ref, out_ref,
-    o_ref, small_out, down_all, gate_up_all, out_final,
-    part_landed, part_sum, row_landed, out_landed, out_mine, out_back,
-    part_send, part_recv, row_send, row_recv, first_send, first_recv, second_send, second_recv,
-    *scratch,
+    p_ref, small_ref, o_ref, small_out, part_landed, part_sum, row_landed,
+    part_send, part_recv, row_send, row_recv, *scratch,
 ):
     greet("seq", "fsdp")
-    me = lax.axis_index("seq")
     part_copies = start_to_peers(
         "fsdp",
         lambda peer: small_ref.at[peer],
@@ -386,10 +382,52 @@
         part_send,
         part_recv,
     )
-    relay = RelayScatter(p_ref, scratch[:6], scratch[6:14])
-    down = gather_by_columns(down_ref, down_all, scratch[14:22])
-    gate_up = gather_by_columns(gate_up_ref, gate_up_all, scratch[22:30])
+    relay = RelayScatter(p_ref, scratch[:6], scratch[6:])
     relay.start()
+    total = small_ref[lax.axis_index("fsdp")]
+    for step, copy in enumerate(part_copies):
+        copy.wait()
+        total = total + part_landed[step]
+    part_sum[...] = total
+    relay.forward(o_ref)
+    row_copies = start_to_peers(
+        "seq", lambda peer: part_sum, lambda step: row_landed.at[step - 1], row_send, row_recv
+    )
+    relay.finish(o_ref)
+    for step, copy in enumerate(row_copies):
+        copy.wait()
+        total = total + row_landed[step]
+    small_out[...] = total
+
+
+def scatter_last(partial, small, n, shards, call_id):
+    total, width = partial.shape
+    rows = total // n
+    piece = small.shape[1:]
+    return pl.pallas_call(
+        scatter_last_kernel,
+        out_shape=(jax.ShapeDtypeStruct((rows, width), F32), jax.ShapeDtypeStruct(piece, F32)),
+        in_specs=[VMEM_SPEC] * 2,
+        out_specs=(VMEM_SPEC,) * 2,
+        scratch_shapes=[
+            pltpu.VMEM((shards - 1,) + piece, F32),
+            pltpu.VMEM(piece, F32),
+            pltpu.VMEM((n - 1,) + piece, F32),
+        ]
+        + semaphores(shards - 1, shards - 1, n - 1, n - 1)
+        + RelayScatter.scratch(n, rows, width),
+        compiler_params=communicating(call_id),
+        name="scatter_last",
+    )(partial, small)
+
+
+def share_kernel(
+    down_ref, out_ref, down_all, out_final, out_landed, out_mine, out_back,
+    first_send, first_recv, second_send, second_recv, *sems,
+):
+    greet("seq")
+    n = lax.axis_size("seq")
+    me = lax.axis_index("seq")
     piece = out_mine.shape[0]
     first = start_to_peers(
         "seq",
@@ -398,72 +436,45 @@
         first_send,
         first_recv,
     )
+    down = gather_by_columns(down_ref, down_all, sems)
     down.start()
-    gate_up.start()
-    total = small_ref[lax.axis_index("fsdp")]
-    for step, copy in enumerate(part_copies):
-        copy.wait()
-        total = total + part_landed[step]
-    part_sum[...] = total
     down_all[me] = down_ref[...]
-    gate_up_all[me] = gate_up_ref[...]
-    row_copies = start_to_peers(
-        "seq", lambda peer: part_sum, lambda step: row_landed.at[step - 1], row_send, row_recv
-    )
-    relay.forward(o_ref)
-    out_total = out_ref[block_of(me, piece), :].astype(F32)
+    total = out_ref[block_of(me, piece), :].astype(F32)
     for step, copy in enumerate(first):
         copy.wait()
-        out_total = out_total + out_landed[step].astype(F32)
-    out_mine[...] = out_total.astype(BF16)
+        total = total + out_landed[step].astype(F32)
+    out_mine[...] = total.astype(BF16)
     down.forward()
     out_final[block_of(me, piece), :] = out_mine[...].astype(F32)
     second = start_to_peers(
         "seq", lambda peer: out_mine, lambda step: out_back.at[step - 1], second_send, second_recv
     )
-    gate_up.forward()
-    relay.finish(o_ref)
-    for step, copy in enumerate(row_copies):
-        copy.wait()
-        total = total + row_landed[step]
-    small_out[...] = total
-    down.finish()
-    n = lax.axis_size("seq")
     for step, copy in enumerate(second):
         copy.wait()
         out_final[block_of(lax.rem(me + n - 1 - step, n), piece), :] = out_back[step].astype(F32)
-    gate_up.finish()
-
-
-def scatter_last(partial, small, down, gate_up, out, n, shards, call_id):
-    total, width = partial.shape
-    rows = total // n
-    piece = small.shape[1:]
+    down.finish()
+
+
+def share(down, out, n, call_id):
+    rows, width = out.shape
     return pl.pallas_call(
-        scatter_last_kernel,
+        share_kernel,
         out_shape=(
-            jax.ShapeDtypeStruct((rows, width), F32),
-            jax.ShapeDtypeStruct(piece, F32),
             jax.ShapeDtypeStruct((n,) + down.shape, BF16),
-            jax.ShapeDtypeStruct((n,) + gate_up.shape, BF16),
             jax.ShapeDtypeStruct(out.shape, F32),
         ),
-        in_specs=[VMEM_SPEC] * 5,
-        out_specs=(VMEM_SPEC,) * 5,
+        in_specs=[VMEM_SPEC] * 2,
+        out_specs=(VMEM_SPEC,) * 2,
         scratch_shapes=[
-            pltpu.VMEM((shards - 1,) + piece, F32),
-            pltpu.VMEM(piece, F32),
-            pltpu.VMEM((n - 1,) + piece, F32),
-            pltpu.VMEM((n - 1, out.shape[0] // n, width), BF16),
-            pltpu.VMEM((out.shape[0] // n, width), BF16),
-            pltpu.VMEM((n - 1, out.shape[0] // n, width), BF16),
+            pltpu.VMEM((n - 1, rows // n, width), BF16),
+            pltpu.VMEM((rows // n, width), BF16),
+            pltpu.VMEM((n - 1, rows // n, width), BF16),
         ]
-        + semaphores(shards - 1, shards - 1, *([n - 1] * 6))
-        + RelayScatter.scratch(n, rows, width)
-        + RelayGather.semaphores(n) * 2,
+        + semaphores(*([n - 1] * 4))
+        + RelayGather.semaphores(n),
         compiler_params=communicating(call_id),
-        name="scatter_last",
-    )(partial, small, down, gate_up, out)
+        name="share",
+    )(down, out)
 
 
 def finish_kernel(qkv_ref, q_final, k_final, v_final, qkv_landed, *sems):
@@ -916,15 +927,19 @@
     gate, up = gate_up[:, :units], gate_up[:, units:]
     logistic = 1.0 / (1.0 + jnp.exp(-gate))
     hidden = (gate / (1.0 + jnp.exp(-gate)) * up).astype(BF16)
-    mlp_partial = matrix_product(hidden, down_weight).astype(BF16)
-
-    grad_down = outer_sum(hidden, grad_mlp).astype(BF16)
     grad_gate = (grad_hidden * up * (logistic + gate * logistic * (1.0 - logistic))).astype(BF16)
     grad_up = (grad_hidden * gate * logistic).astype(BF16)
     grad_gate_up = jnp.concatenate([grad_gate, grad_up], axis=1)
     grad_gate_up_weight = outer_sum(normed_post, grad_gate_up).astype(BF16)
-    grad_partial, grad_down, grad_gate_up_weight = lax.optimization_barrier(
-        (back_matmul(grad_gate_up, gate_up_weight).astype(BF16), grad_down, grad_gate_up_weight)
+    grad_gate_up_weight, grad_gate_up, hidden = lax.optimization_barrier(
+        (grad_gate_up_weight, grad_gate_up, hidden)
+    )
+    mlp_partial = matrix_product(hidden, down_weight).astype(BF16)
+    grad_partial, grad_down = lax.optimization_barrier(
+        (
+            back_matmul(grad_gate_up, gate_up_weight).astype(BF16),
+            outer_sum(hidden, grad_mlp).astype(BF16),
+        )
     )
     gate_up_share = lax.psum_scatter(grad_gate_up_weight, "fsdp", scatter_dimension=0, tiled=True)
     grad_normed_post = scatter_sum(grad_partial, n, 3)
@@ -949,19 +964,35 @@
     grad_qkv = jnp.concatenate([grad_q, grad_k, grad_v], axis=1)
     grad_qkv_weight = outer_sum(normalized, grad_qkv).astype(BF16)
     qkv_share = lax.psum_scatter(grad_qkv_weight, "fsdp", scatter_dimension=0, tiled=True)
+    gate_up_share, _ = lax.optimization_barrier((gate_up_share, grad_qkv))
+    gate_up_all = [gate_up_share]
+    for step in range(1, n):
+        pairs = [(i, (i + step) % n) for i in range(n)]
+        gate_up_all.append(lax.ppermute(gate_up_share, "seq", pairs))
     partial = back_matmul(grad_qkv, qkv_weight)
     grad_gain_in = jnp.sum(partial * unit, axis=0)
     small_grads = [grad_gain_in, grad_gain_post, grad_gain_query, grad_gain_key]
     small_grads = tile_of(jnp.concatenate([g.reshape(shards, -1) for g in small_grads], axis=1))
-    grad_normed, gain_shares, down_all, gate_up_all, final_out = scatter_last(
-        partial.astype(BF16), small_grads, down_share, gate_up_share, out_share, n, shards, 5
-    )
+    grad_normed, gain_shares = scatter_last(
+        partial.astype(BF16), small_grads, n, shards, 5
+    )
+    late_down, late_out, _ = lax.optimization_barrier((down_share, out_share, gain_shares))
+    down_all, final_out = share(late_down, late_out, n, 7)
     gain_shares = gain_shares.reshape(-1)
     grad_inputs, _ = rms_backward(inputs, gain_in, grad_normed)
     input_grad = (grad_middle + grad_inputs).astype(BF16)[None]
 
     final_down = down_all.astype(F32).reshape(-1, width)
-    final_gate, final_up = spread_back(gate_up_all, hidden_piece)
+    by_step = jnp.stack(gate_up_all)
+    final_gate, final_up = spread_back(
+        jnp.stack(
+            [
+                lax.dynamic_index_in_dim(by_step, lax.rem(me + n - owner, n), keepdims=False)
+                for owner in range(n)
+            ]
+        ),
+        hidden_piece,
+    )
     final_query, final_key, final_value = finish(
         qkv_share, (HQ * HEAD_SIZE,) + (KEY_VALUE_HEADS * HEAD_SIZE,) * 2, n, 6
     )

time: 473 us -> 396 us (0.84)
  waiting for transfers between devices: 125 us -> 35.9 us
  other arithmetic: 24.7 us -> 30.4 us
    reduce_scatter x1, waiting for transfers between devices: 37.5 us -> 0.01 us  [on_device(): lax.psum_scatter(grad_gate_up_weight, 'fsdp', scatter_dimension=0, tiled=...]
    reduce_scatter x1, waiting for transfers between devices: 52.4 us -> 19.1 us  [on_device(): lax.psum_scatter(jnp.concatenate([grad_out.reshape(shards, -1, width), gr...]
    pallas_call x1, Pallas kernels: 55.9 us -> 23.7 us  [scatter_last(): pl.pallas_call(scatter_last_kernel, out_shape=(jax.ShapeDtypeStruct((rows...]
    pallas_call x0 -> x1, Pallas kernels: none -> 21.7 us  [share(): pl.pallas_call(share_kernel, out_shape=(jax.ShapeDtypeStruct((n,) + down....]
    reduce_scatter x1, waiting for transfers between devices: 16.4 us -> 0.01 us  [on_device(): lax.psum_scatter(grad_qkv_weight, 'fsdp', scatter_dimension=0, tiled=True)]
    pallas_call x1, Pallas kernels: 13.1 us -> 24.5 us  [finish(): pl.pallas_call(finish_kernel, out_shape=tuple((jax.ShapeDtypeStruct((qkv....]
    unnamed x82 -> x90, local copies, waits for them, and re-layouts: 11 us -> 13 us
  transfers between devices with their start and end apart: 6 -> 9, of which waited for: 5 -> 3; matrix products, arithmetic and copies ran while one was open for 11% -> 20% of each run, Pallas kernels for 21% -> 51%
where the time goes in v6:
time: 396 us; the launch traced here: 390 us
  Pallas kernels  221 us (56%)
  matrix products  51 us (13%)
  waiting for transfers between devices  35.9 us (9%)
  local copies, waits for them, and re-layouts  32.2 us (8%)
  other arithmetic  30.4 us (8%)
  between operations  15 us (4%)
  starting transfers between devices  4.07 us (1%)
    pallas_call x1, Pallas kernels, attend_backward(): pl.pallas_call(backward_kernel, grid=(n, heads), out_shape=(jax.ShapeDtyp...  38.8 us
    pallas_call x1, Pallas kernels, attend_forward(): pl.pallas_call(forward_kernel, grid=(n, heads), out_shape=(jax.ShapeDtype...  36.3 us
    pallas_call x1, Pallas kernels, gather_first(): pl.pallas_call(gather_first_kernel, out_shape=(jax.ShapeDtypeStruct((n *...  27 us
    pallas_call x1, Pallas kernels, finish(): pl.pallas_call(finish_kernel, out_shape=tuple((jax.ShapeDtypeStruct((qkv....  24.5 us
    pallas_call x1, Pallas kernels, scatter_last(): pl.pallas_call(scatter_last_kernel, out_shape=(jax.ShapeDtypeStruct((rows...  23.7 us
    pallas_call x1, Pallas kernels, scatter_sum(): pl.pallas_call(scatter_kernel, out_shape=jax.ShapeDtypeStruct((rows, widt...  23.5 us
    pallas_call x1, Pallas kernels, gather_rows(): pl.pallas_call(gather_kernel, out_shape=jax.ShapeDtypeStruct((n * rows, w...  22.2 us
    pallas_call x1, Pallas kernels, share(): pl.pallas_call(share_kernel, out_shape=(jax.ShapeDtypeStruct((n,) + down....  21.7 us
  transfers between devices with their start and end apart: 9, of which 3 were waited for; matrix products, arithmetic and copies ran while one was open for 20% of the time, Pallas kernels for 51%

profile of v6, /device:TPU:0, one launch (start us, length us, event | category | flops | bytes accessed | tf_op | source)
XLA Modules:
  0.0 389.8 jit_solution(12330537981114794366)
XLA Ops:
  14.3 27.0 %gather_first.1 = (bf16[1024,1024]{1,0:T(8,128)(2,1)}, f32[8,8,128]{2,1,0:T(8,128)}) custom-call(bf16[256,1024]{1,0:T(8,128)(2,1)} %bitcast.80, f32[8,128]{1,0:T(8,128)} %fusion.28.gains_ref), custom_call_target="tpu_custom_call" | custom-call | tf_op jit(solution)/shard_map/gather_first/pallas_call | solution.py:338
  45.2 1.9 fusion.19
  47.2 1.3 pad_maximum_fusion.4
  49.0 7.5 %all-gather.9.cloned.1.call-done = bf16[1792,1024]{1,0:T(8,128)(2,1)} async-done(((bf16[224,1024]{1,0:T(8,128)(2,1)}), bf16[1792,1024]{1,0:T(8,128)(2,1)}) %all-gather.9.cloned.1.call-update) | async-done | bytes 3670032 | tf_op jit(solution)/shard_map/all_gather | solution.py:878
  56.5 1.8 slice.78
  58.3 2.4 fusion.13
  60.7 1.5 slice.79.q_pre
  64.1 2.7 slice.85
  66.9 36.3 %attend_forward.1 = (bf16[256,2048]{1,0:T(8,128)(2,1)}, bf16[4,1024,1024]{2,1,0:T(8,128)(2,1)}, bf16[1024,512]{1,0:T(8,128)(2,1)}, bf16[1024,256]{1,0:T(8,128)(2,1)}, bf16[1024,1024]{1,0:T(8,128)(2,1)}) custom-call(f32[1024,512]{1,0:T(8,128)} %slice.79.q_pre, f32[1024,256]{1,0:T(8,128)} %slice.80.k_pre, bf16[1024,256]{1,0:T(8,128)(2,1)} %slice.100.v_ref, ...), custom_call_target="tpu_custom_call" | custom-call | tf_op jit(solution)/shard_map/attend_forward/pallas_call | solution.py:658
  103.2 5.6 %fusion.31 = f32[1024,768]{1,0:T(8,128)} fusion(bf16[1024,1024]{1,0:T(8,128)(2,1)} %get-tuple-element.49, bf16[768,1024]{1,0:T(8,128)(2,1)} %bitcast.86), kind=kOutput, calls=%fused_computation.96 | convolution fusion | flops 1610612736 | bytes 6815744 | tf_op jit(solution)/shard_map/dot_general | solution.py:34
  108.8 3.5 multiply_reduce_fusion.2
  113.3 22.2 %shard_map.246 = bf16[1024,1024]{1,0:T(8,128)(2,1)} custom-call(bf16[256,1024]{1,0:T(8,128)(2,1)} %multiply_convert_fusion.3.x_ref), custom_call_target="tpu_custom_call" | custom-call | tf_op jit(solution)/shard_map/pallas_call | solution.py:310
  135.5 8.5 %all-gather.7.cloned.1.call-done = bf16[1024,1536]{0,1:T(8,128)(2,1)} async-done(((bf16[128,1536]{0,1:T(8,128)(2,1)}), bf16[1024,1536]{0,1:T(8,128)(2,1)}) %all-gather.7.cloned.1.call-update) | async-done | bytes 3145744 | tf_op jit(solution)/shard_map/all_gather | solution.py:892
  144.0 6.1 %fusion.32 = f32[1024,1536]{1,0:T(8,128)S(1)} fusion(bf16[1024,1024]{1,0:T(8,128)(2,1)} %shard_map.246, bf16[1024,1536]{0,1:T(8,128)(2,1)} %all-gather.7.cloned.1.call-done), kind=kOutput, calls=%fused_computation.97 | convolution fusion | flops 3221225472 | bytes 11534336 | tf_op jit(solution)/shard_map/dot_general | solution.py:26
  150.1 2.9 multiply_convert_fusion.2
  153.1 1.1 copy-done.3
  154.2 5.2 %convolution_convert_fusion.1 = bf16[1024,1536]{1,0:T(8,128)(2,1)} fusion(bf16[1024,1024]{1,0:T(8,128)(2,1)S(1)} %copy-done.8, bf16[1024,768]{1,0:T(8,128)(2,1)S(1)} %get-tuple-element.78, bf16[1024,768]{1,0:T(8,128)(2,1)S(1)} %get-tuple-element.77), kind=kOutput, calls=%fused_computation.11 | convolution fusion | flops 3229089792 | bytes 8388608 | tf_op jit(solution)/shard_map/dot_general | solution.py:30
  159.4 3.3 pad_maximum_fusion.1
  163.0 1.2 copy-done.13
  164.2 4.7 %convolution_convert_fusion.6 = bf16[768,1024]{1,0:T(8,128)(2,1)} fusion(bf16[1024,768]{1,0:T(8,128)(2,1)S(1)} %copy-done.13, bf16[1024,1024]{1,0:T(8,128)(2,1)} %get-tuple-element.49), kind=kOutput, calls=%fused_computation.26 | convolution fusion | flops 1611399168 | bytes 5242880 | tf_op jit(solution)/shard_map/dot_general | solution.py:30
  168.9 4.7 %convolution_convert_fusion.4.p_ref = bf16[1024,1024]{1,0:T(8,128)(2,1)} fusion(bf16[1024,1536]{1,0:T(8,128)(2,1)S(1)} %copy-done.6, bf16[1024,1536]{0,1:T(8,128)(2,1)S(1)} %copy-done.36), kind=kOutput, calls=%fused_computation.20 | convolution fusion | flops 3222274048 | bytes 8388608 | tf_op jit(solution)/shard_map/dot_general | solution.py:34
  173.6 23.5 %shard_map.247 = f32[256,1024]{1,0:T(8,128)} custom-call(bf16[1024,1024]{1,0:T(8,128)(2,1)} %convolution_convert_fusion.4.p_ref), custom_call_target="tpu_custom_call" | custom-call | tf_op jit(solution)/shard_map/pallas_call | solution.py:363
  197.1 1.7 multiply_reduce_fusion
  200.0 2.3 convolution_convert_fusion.2.grad_own
  202.3 3.2 convolution_convert_fusion.5.bulk
  205.4 38.8 %attend_backward.1 = (bf16[1024,512]{1,0:T(8,128)(2,1)}, bf16[1024,256]{1,0:T(8,128)(2,1)}, bf16[1024,256]{1,0:T(8,128)(2,1)}, f32[1,128]{1,0:T(1,128)}, f32[1,128]{1,0:T(1,128)}, /*index=5*/f32[256,1024]{1,0:T(8,128)}) custom-call(bf16[4,1024,1024]{2,1,0:T(8,128)(2,1)} %get-tuple-element.46.p_ref, bf16[1024,512]{1,0:T(8,128)(2,1)} %get-tuple-element.47.q_ref, ...), custom_call_target="tpu_custom_call" | custom-call | tf_op jit(solution)/shard_map/attend_backward/pallas_call | solution.py:794
  244.3 1.5 constant_dynamic-update-slice_fusion.2
  246.0 1.3 copy-done.22
  247.3 4.0 %convolution_convert_fusion.3 = bf16[1024,1024]{1,0:T(8,128)(2,1)} fusion(bf16[1024,1024]{1,0:T(8,128)(2,1)S(1)} %constant_dynamic-update-slice_fusion, bf16[1024,1024]{1,0:T(8,128)(2,1)S(1)} %copy-done.10, f32[1024]{0:T(1024)S(1)} %get-tuple-element.87, f32[1024]{0:T(1024)S(1)} %add_rsqrt_fusion), kind=kOutput, calls=%fused_computation.19 | convolution fusion | flops 2152726528 | bytes 6299648 | tf_op jit(solution)/shard_map/dot_general | solution.py:30
  251.6 2.6 convolution_convert_fusion
  254.2 3.1 pad_maximum_fusion
  259.5 6.6 %fusion.3 = (f32[1024]{0:T(1024)S(1)}, bf16[1024,1024]{1,0:T(8,128)(2,1)}) fusion(bf16[1024,1024]{1,0:T(8,128)(2,1)} %get-tuple-element.43, f32[1024]{0:T(1024)S(1)} %add_rsqrt_fusion, bf16[1024,1024]{1,0:T(8,128)(2,1)} %copy-done.22, bf16[1024,1024]{1,0:T(8,128)(2,1)} %bitcast.84), kind=kOutput, calls=%fused_computation.6 | convolution fusion | flops 2152725504 | bytes 8396800 | tf_op jit(solution)/shard_map/dot_general | solution.py:34
  266.9 23.7 %scatter_last.1 = (f32[256,1024]{1,0:T(8,128)}, f32[8,128]{1,0:T(8,128)}) custom-call(bf16[1024,1024]{1,0:T(8,128)(2,1)} %get-tuple-element.81.p_ref, f32[8,8,128]{2,1,0:T(8,128)} %bitcast.96), custom_call_target="tpu_custom_call" | custom-call | tf_op jit(solution)/shard_map/scatter_last/pallas_call | solution.py:407
  290.6 1.6 fusion.6
  292.2 1.3 slice_bitcast_fusion.2
  293.5 1.3 fusion.30
  295.8 1.5 collective-permute-start.2
  297.8 1.4 collective-permute-start
  299.2 2.3 fusion.16
  301.5 24.5 %finish.1 = (f32[128,2048]{1,0:T(8,128)}, f32[128,1024]{1,0:T(8,128)}, f32[128,1024]{1,0:T(8,128)}) custom-call(bf16[128,1024]{1,0:T(8,128)(2,1)} %reduce-scatter.4.cloned.1.call-done.qkv_ref), custom_call_target="tpu_custom_call" | custom-call | tf_op jit(solution)/shard_map/finish/pallas_call | solution.py:504
  326.1 1.2 pad_maximum_fusion.2
  327.4 1.3 pad_maximum_fusion.3.pieces_ref
  328.8 3.5 spread_back.1
  332.2 19.1 %reduce-scatter.6.cloned.1.call-done = bf16[352,1024]{1,0:T(8,128)(2,1)} async-done(((bf16[2816,1024]{1,0:T(8,128)(2,1)}), bf16[352,1024]{1,0:T(8,128)(2,1)}) %reduce-scatter.6.cloned.1.call-update) | async-done | bytes 720912 | tf_op jit(solution)/shard_map/reduce_scatter | solution.py:951
  351.4 1.6 slice.88.down_ref
  353.0 2.0 slice.89.out_ref
  354.9 21.7 %share.1 = (bf16[4,96,1024]{2,1,0:T(8,128)(2,1)}, f32[256,1024]{1,0:T(8,128)}) custom-call(bf16[96,1024]{1,0:T(8,128)(2,1)} %slice.88.down_ref, bf16[256,1024]{1,0:T(8,128)(2,1)} %slice.89.out_ref), custom_call_target="tpu_custom_call" | custom-call | tf_op jit(solution)/shard_map/share/pallas_call | solution.py:460
  376.7 2.5 bitcast_convert_fusion
  (142 shorter events, 24.1 us)
Async XLA Ops:
  7.2 1.1 copy-start
  7.2 4.7 %copy-start.20 = (bf16[128,3072]{1,0:T(8,128)(2,1)S(1)}, bf16[128,3072]{1,0:T(8,128)(2,1)}, u32[]{:S(2)}) copy-start(bf16[128,3072]{1,0:T(8,128)(2,1)} %param.27) | copy-start | bytes 2359300
  7.2 49.3 %all-gather.9.cloned.1.call-start = ((), (), s32[]{:S(2)}) async-start(), calls=%async_computation.8 | async-start | bytes 4128768 | tf_op jit(solution)/shard_map/all_gather | solution.py:878
  8.3 4.0 %copy-start.21 = (bf16[128,3072]{1,0:T(8,128)(2,1)S(1)}, bf16[128,3072]{1,0:T(8,128)(2,1)}, u32[]{:S(2)}) copy-start(bf16[128,3072]{1,0:T(8,128)(2,1)} %param.26) | copy-start | bytes 2359300
  11.1 97.7 %all-gather.5.cloned.1.call-start = ((), (), s32[]{:S(2)}) async-start(), calls=%async_computation.3 | async-start | bytes 4718592 | tf_op jit(solution)/shard_map/all_gather | solution.py:891
  11.8 132.1 %all-gather.7.cloned.1.call-start = ((), (), s32[]{:S(2)}) async-start(), calls=%async_computation.4 | async-start | bytes 3538944 | tf_op jit(solution)/shard_map/all_gather | solution.py:892
  12.3 1.4 copy-start.30
  12.3 1.4 copy-start.31
  12.3 1.3 copy-start.32
  12.3 1.3 copy-start.33
  12.3 31.1 %copy-start.34 = (s32[1,8]{1,0:T(1,128)S(1)}, s32[1,8]{1,0:T(1,128)}, u32[]{:S(2)}) copy-start(s32[1,8]{1,0:T(1,128)} %param.16) | copy-start | bytes 100
  12.3 31.2 %copy-start.37 = (s32[1,1024]{1,0:T(1,128)S(1)}, s32[1,1024]{1,0:T(1,128)}, u32[]{:S(2)}) copy-start(s32[1,1024]{1,0:T(1,128)} %param.17) | copy-start | bytes 12292
  13.6 282.2 %reduce-scatter.8.cloned.1.call-start = ((), (), s32[]{:S(2)}) async-start(), calls=%async_computation.7 | async-start | bytes 3538944 | tf_op jit(solution)/shard_map/reduce_scatter | solution.py:944
  44.1 4.4 %copy-start.28 = (s32[1024]{0:T(1024)}, s32[1024]{0:T(1024)S(1)}, u32[]{:S(2)}) copy-start(s32[1024]{0:T(1024)S(1)} %select_reduce_fusion) | copy-start | bytes 12292
  45.2 3.3 copy-start.29
  45.2 3.2 copy-start.9
  58.3 2.4 copy-start.11
  103.2 5.6 %copy-start.4 = (bf16[1,256,1024]{2,1,0:T(8,128)(2,1)S(1)}, bf16[1,256,1024]{2,1,0:T(8,128)(2,1)}, u32[]{:S(2)}) copy-start(bf16[1,256,1024]{2,1,0:T(8,128)(2,1)} %param.15) | copy-start | bytes 1572868
  103.2 5.6 %copy-start.7 = (bf16[256,2048]{1,0:T(8,128)(2,1)S(1)}, bf16[256,2048]{1,0:T(8,128)(2,1)}, u32[]{:S(2)}) copy-start(bf16[256,2048]{1,0:T(8,128)(2,1)} %get-tuple-element.45) | copy-start | bytes 3145732
  144.0 6.1 %copy-start.5 = (f32[1024,768]{1,0:T(8,128)S(1)}, f32[1024,768]{1,0:T(8,128)}, u32[]{:S(2)}) copy-start(f32[1024,768]{1,0:T(8,128)} %fusion.31) | copy-start | bytes 9437188
  150.1 4.1 %copy-start.8 = (bf16[1024,1024]{1,0:T(8,128)(2,1)S(1)}, bf16[1024,1024]{1,0:T(8,128)(2,1)}, u32[]{:S(2)}) copy-start(bf16[1024,1024]{1,0:T(8,128)(2,1)} %shard_map.246) | copy-start | bytes 6291460
  153.1 1.1 copy-start.3
  162.8 1.4 copy-start.13
  162.8 138.8 %reduce-scatter.4.cloned.1.call-start = ((), (), s32[]{:S(2)}) async-start(), calls=%async_computation.5 | async-start | bytes 2359296 | tf_op jit(solution)/shard_map/reduce_scatter | solution.py:966
  164.2 4.7 %copy-start.6 = (bf16[1024,1536]{1,0:T(8,128)(2,1)S(1)}, bf16[1024,1536]{1,0:T(8,128)(2,1)}, u32[]{:S(2)}) copy-start(bf16[1024,1536]{1,0:T(8,128)(2,1)} %pad_maximum_fusion.1) | copy-start | bytes 9437188
  164.2 4.7 %copy-start.36 = (bf16[1024,1536]{0,1:T(8,128)(2,1)S(1)}, bf16[1024,1536]{0,1:T(8,128)(2,1)}, u32[]{:S(2)}) copy-start(bf16[1024,1536]{0,1:T(8,128)(2,1)} %all-gather.7.cloned.1.call-done) | copy-start | bytes 9437188
  173.6 25.2 %copy-start.12 = (bf16[1,256,1024]{2,1,0:T(8,128)(2,1)S(1)}, bf16[1,256,1024]{2,1,0:T(8,128)(2,1)}, u32[]{:S(2)}) copy-start(bf16[1,256,1024]{2,1,0:T(8,128)(2,1)} %param.29) | copy-start | bytes 1572868
  197.1 1.7 copy-start.2
  197.1 2.9 copy-start.35
  200.0 2.3 copy-start.14
  200.0 2.3 copy-start.15
  244.3 1.5 copy-start.26
  244.3 1.6 copy-start.25
  244.3 3.0 copy-start.10
  245.9 1.3 copy-start.22
  251.3 100.0 %reduce-scatter.6.cloned.1.call-start = ((), (), s32[]{:S(2)}) async-start(), calls=%async_computation.6 | async-start | bytes 6488064 | tf_op jit(solution)/shard_map/reduce_scatter | solution.py:951
  251.6 2.7 copy-start.16
  257.4 1.4 copy-start.38
  290.6 4.2 %copy-start.17 = (f32[256,1024]{1,0:T(8,128)S(1)}, f32[256,1024]{1,0:T(8,128)}, u32[]{:S(2)}) copy-start(f32[256,1024]{1,0:T(8,128)} %get-tuple-element.53) | copy-start | bytes 3145732
  295.7 30.4 %copy-start.27 = (bf16[128,1536]{1,0:T(8,128)(2,1)S(1)}, bf16[128,1536]{1,0:T(8,128)(2,1)}, u32[]{:S(2)}) copy-start(bf16[128,1536]{1,0:T(8,128)(2,1)} %reduce-scatter.8.cloned.1.call-done) | copy-start | bytes 1179652
  295.8 30.3 %collective-permute-start.2 = (bf16[128,1536]{1,0:T(8,128)(2,1)}, bf16[128,1536]{1,0:T(8,128)(2,1)S(1)}, u32[]{:S(2)}, u32[]{:S(2)}) collective-permute-start(bf16[128,1536]{1,0:T(8,128)(2,1)} %reduce-scatter.8.cloned.1.call-done), channel_id=1, source_target_pairs={{0,24},{8,0},{16,8},{24,16},{1,25},{9,1},{17,9},{25,17},{2,26},{10... | collective-permute-start | bytes 1179656 | tf_op jit(solution)/shard_map/ppermute | solution.py:971
  297.2 28.9 %collective-permute-start.1 = (bf16[128,1536]{1,0:T(8,128)(2,1)}, bf16[128,1536]{1,0:T(8,128)(2,1)S(1)}, u32[]{:S(2)}, u32[]{:S(2)}) collective-permute-start(bf16[128,1536]{1,0:T(8,128)(2,1)} %reduce-scatter.8.cloned.1.call-done), channel_id=1, source_target_pairs={{0,16},{8,24},{16,0},{24,8},{1,17},{9,25},{17,1},{25,9},{2,18},{10... | collective-permute-start | bytes 1179656 | tf_op jit(solution)/shard_map/ppermute | solution.py:971
  297.8 28.3 %collective-permute-start = (bf16[128,1536]{1,0:T(8,128)(2,1)}, bf16[128,1536]{1,0:T(8,128)(2,1)}, u32[]{:S(2)}, u32[]{:S(2)}) collective-permute-start(bf16[128,1536]{1,0:T(8,128)(2,1)} %reduce-scatter.8.cloned.1.call-done), channel_id=1, source_target_pairs={{0,8},{8,16},{16,24},{24,0},{1,9},{9,17},{17,25},{25,1},{2,10},{10... | collective-permute-start | bytes 1179656 | tf_op jit(solution)/shard_map/ppermute | solution.py:971
  353.0 26.2 %copy-start.18 = (f32[128,2048]{1,0:T(8,128)S(1)}, f32[128,2048]{1,0:T(8,128)}, u32[]{:S(2)}) copy-start(f32[128,2048]{1,0:T(8,128)} %get-tuple-element.126) | copy-start | bytes 3145732
  376.7 3.5 copy-start.24
  379.2 1.8 copy-start.23
  379.2 2.6 copy-start.19
  379.2 3.5 copy-start.1
  (1 other events, 0.6 us)
Sparse Core Ops, SparseCore 0:
  11.2 45.2 all-gather.8
  58.1 45.6 all-gather.4
  106.0 37.9 all-gather.6
  162.9 38.5 reduce-scatter.7
  251.4 34.3 reduce-scatter.3
  288.0 63.3 reduce-scatter.5

commit v7 on v6

--- a/solution.py
+++ b/solution.py
@@ -421,95 +421,102 @@
     )(partial, small)
 
 
-def share_kernel(
-    down_ref, out_ref, down_all, out_final, out_landed, out_mine, out_back,
+def finish_kernel(
+    qkv_ref, joined_ref, qkv_all, down_all, out_all, out_landed, out_mine,
     first_send, first_recv, second_send, second_recv, *sems,
 ):
     greet("seq")
-    n = lax.axis_size("seq")
     me = lax.axis_index("seq")
     piece = out_mine.shape[0]
+    below = out_all.shape[0]
+    count = down_all.shape[1]
     first = start_to_peers(
         "seq",
-        lambda peer: out_ref.at[block_of(peer, piece)],
+        lambda peer: joined_ref.at[block_of(peer, piece)],
         lambda step: out_landed.at[step - 1],
         first_send,
         first_recv,
     )
-    down = gather_by_columns(down_ref, down_all, sems)
+    qkv = gather_by_columns(qkv_ref, qkv_all, sems[:8])
+    down = gather_by_columns(joined_ref.at[pl.ds(below, count)], down_all, sems[8:])
+    qkv.start()
     down.start()
-    down_all[me] = down_ref[...]
-    total = out_ref[block_of(me, piece), :].astype(F32)
+    qkv_all[me] = qkv_ref[...]
+    down_all[me] = joined_ref[below:, :]
+    total = joined_ref[block_of(me, piece), :].astype(F32)
     for step, copy in enumerate(first):
         copy.wait()
         total = total + out_landed[step].astype(F32)
     out_mine[...] = total.astype(BF16)
+    qkv.forward()
+    mine = block_of(me, piece)
+    second = start_to_peers(
+        "seq", lambda peer: out_mine, lambda step: out_all.at[mine], second_send, second_recv
+    )
+    out_all[mine, :] = out_mine[...]
     down.forward()
-    out_final[block_of(me, piece), :] = out_mine[...].astype(F32)
-    second = start_to_peers(
-        "seq", lambda peer: out_mine, lambda step: out_back.at[step - 1], second_send, second_recv
-    )
-    for step, copy in enumerate(second):
+    qkv.finish()
+    down.finish()
+    for copy in second:
         copy.wait()
-        out_final[block_of(lax.rem(me + n - 1 - step, n), piece), :] = out_back[step].astype(F32)
-    down.finish()
-
-
-def share(down, out, n, call_id):
-    rows, width = out.shape
+
+
+def finish(qkv, joined, out_rows, n, call_id):
+    width = joined.shape[1]
+    down_rows = joined.shape[0] - out_rows
     return pl.pallas_call(
-        share_kernel,
+        finish_kernel,
         out_shape=(
-            jax.ShapeDtypeStruct((n,) + down.shape, BF16),
-            jax.ShapeDtypeStruct(out.shape, F32),
+            jax.ShapeDtypeStruct((n,) + qkv.shape, BF16),
+            jax.ShapeDtypeStruct((n, down_rows, width), BF16),
+            jax.ShapeDtypeStruct((out_rows, width), BF16),
         ),
         in_specs=[VMEM_SPEC] * 2,
-        out_specs=(VMEM_SPEC,) * 2,
+        out_specs=(VMEM_SPEC,) * 3,
         scratch_shapes=[
-            pltpu.VMEM((n - 1, rows // n, width), BF16),
-            pltpu.VMEM((rows // n, width), BF16),
-            pltpu.VMEM((n - 1, rows // n, width), BF16),
+            pltpu.VMEM((n - 1, out_rows // n, width), BF16),
+            pltpu.VMEM((out_rows // n, width), BF16),
         ]
         + semaphores(*([n - 1] * 4))
-        + RelayGather.semaphores(n),
+        + RelayGather.semaphores(n) * 2,
         compiler_params=communicating(call_id),
-        name="share",
-    )(down, out)
-
-
-def finish_kernel(qkv_ref, q_final, k_final, v_final, qkv_landed, *sems):
-    greet("seq")
-    n = lax.axis_size("seq")
-    me = lax.axis_index("seq")
+        name="finish",
+    )(qkv, joined)
+
+
+def widen_kernel(qkv_ref, down_ref, out_ref, q_final, k_final, v_final, down_final, out_final):
+    n = qkv_ref.shape[0]
     split = q_final.shape[1] // n
     narrow = k_final.shape[1] // n
-
-    def place(values, owner):
-        values = values.astype(F32)
-        q_final[:, block_of(owner, split)] = values[:, :split]
-        k_final[:, block_of(owner, narrow)] = values[:, split : split + narrow]
-        v_final[:, block_of(owner, narrow)] = values[:, split + narrow :]
-
-    relay = gather_by_columns(qkv_ref, qkv_landed, sems)
-    relay.start()
-    place(qkv_ref[...], me)
-    relay.forward()
-    relay.finish()
-    for step in range(1, n):
-        owner = lax.rem(me + step, n)
-        place(qkv_landed[owner], owner)
-
-
-def finish(qkv, widths, n, call_id):
+    for owner in range(n):
+        values = qkv_ref[owner].astype(F32)
+        q_final[:, owner * split : (owner + 1) * split] = values[:, :split]
+        k_final[:, owner * narrow : (owner + 1) * narrow] = values[:, split : split + narrow]
+        v_final[:, owner * narrow : (owner + 1) * narrow] = values[:, split + narrow :]
+    down_final[...] = down_ref[...].astype(F32)
+    out_final[...] = out_ref[...].astype(F32)
+
+
+def widen(qkv_all, down_all, out_all, widths):
+    n, rows, _ = qkv_all.shape
+    steps = 4
+
+    def by_rows(shape):
+        return pl.BlockSpec((shape[0] // steps, shape[1]), lambda i: (i, 0))
+
+    qkv_spec = pl.BlockSpec((n, rows // steps, qkv_all.shape[2]), lambda i: (0, i, 0))
+    down_spec = pl.BlockSpec((n // steps,) + down_all.shape[1:], lambda i: (i, 0, 0))
+    shapes = [(rows, size) for size in widths]
     return pl.pallas_call(
-        finish_kernel,
-        out_shape=tuple(jax.ShapeDtypeStruct((qkv.shape[0], size), F32) for size in widths),
-        in_specs=[VMEM_SPEC],
-        out_specs=(VMEM_SPEC,) * 3,
-        scratch_shapes=[pltpu.VMEM((n,) + qkv.shape, BF16)] + RelayGather.semaphores(n),
-        compiler_params=communicating(call_id),
-        name="finish",
-    )(qkv)
+        widen_kernel,
+        grid=(steps,),
+        out_shape=tuple(
+            jax.ShapeDtypeStruct(shape, F32) for shape in shapes + [down_all.shape, out_all.shape]
+        ),
+        in_specs=[qkv_spec, down_spec, by_rows(out_all.shape)],
+        out_specs=tuple(by_rows(shape) for shape in shapes) + (down_spec, by_rows(out_all.shape)),
+        name="widen",
+    )(qkv_all, down_all, out_all)
 
 
 def spread_kernel(hidden_piece, pieces_ref, gate_ref, up_ref):
@@ -696,7 +703,7 @@
 def backward_kernel(
     p_ref, q_ref, k_ref, v_ref, q_pre, k_pre, gain_q, gain_k, cos_q, sin_q, cos_k, sin_k,
     grad_own, bulk,
-    dq_ref, dk_ref, dv_ref, dgain_q, dgain_k, bulk_sum,
+    dqkv_ref, dgain_q, dgain_k, bulk_sum,
     k_turned, dk_sum, dv_sum, grads, send, recv, local, *scratch,
 ):
     i, head = pl.program_id(0), pl.program_id(1)
@@ -704,6 +711,7 @@
     seq = lax.axis_size("seq")
     me = lax.axis_index("seq")
     kv = k_turned.shape[0]
+    rows = grads.shape[1]
     span = grads.shape[2]
     first = (i == 0) & (head == 0)
     last = (i == n - 1) & (head == heads - 1)
@@ -759,7 +767,8 @@
     dv_sum[pair] += matrix_product(rounded, grad)
     dq = (matrix_product(k_turned[pair], grad_scores).T * SCALE).astype(BF16).astype(F32)
     dq, gain_rows = rms_backward(q_pre[...], gain_q[...], rope_back(dq, cos_q[...], sin_q[...]))
-    dq_ref[...] = dq.astype(BF16)
+    block = block_of(lax.rem(me + i, seq), rows)
+    dqkv_ref[block, head_columns(head)] = dq.astype(BF16)
     dgain_q[...] += jnp.sum(gain_rows, axis=0, keepdims=True)
 
     @pl.when(last)
@@ -770,9 +779,9 @@
             dk, gain_rows = rms_backward(
                 k_pre[:, own], gain_k[...], rope_back(dk, cos_k[...], sin_k[...])
             )
-            dk_ref[:, own] = dk.astype(BF16)
+            dqkv_ref[:, head_columns(heads + which)] = dk.astype(BF16)
             dgain_k[...] += jnp.sum(gain_rows, axis=0, keepdims=True)
-            dv_ref[:, own] = dv_sum[which].astype(BF16)
+            dqkv_ref[:, head_columns(heads + kv + which)] = dv_sum[which].astype(BF16)
         for step in range(1, seq):
             grad_copy(step).wait_send()
         bulk_relay.finish(bulk_sum)
@@ -795,9 +804,7 @@
         backward_kernel,
         grid=(n, heads),
         out_shape=(
-            jax.ShapeDtypeStruct((rows, heads * HEAD_SIZE), BF16),
-            jax.ShapeDtypeStruct((rows, kv * HEAD_SIZE), BF16),
-            jax.ShapeDtypeStruct((rows, kv * HEAD_SIZE), BF16),
+            jax.ShapeDtypeStruct((rows, (heads + 2 * kv) * HEAD_SIZE), BF16),
             jax.ShapeDtypeStruct((1, HEAD_SIZE), F32),
             jax.ShapeDtypeStruct((1, HEAD_SIZE), F32),
             jax.ShapeDtypeStruct((block, bulk.shape[1]), F32),
@@ -809,7 +816,8 @@
             pl.BlockSpec(bulk.shape, lambda i, h: (0, 0)),
         ],
         out_specs=(
-            q_spec, k_spec, k_spec, gain_spec, gain_spec,
+            pl.BlockSpec((rows, (heads + 2 * kv) * HEAD_SIZE), lambda i, h: (0, 0)),
+            gain_spec, gain_spec,
             pl.BlockSpec((block, bulk.shape[1]), lambda i, h: (0, 0)),
         ),
         scratch_shapes=[
@@ -954,14 +962,12 @@
         ).reshape(-1, width),
         "fsdp", scatter_dimension=0, tiled=True,
     )
-    out_share, down_share = out_down_share[: w_out.shape[0]], out_down_share[w_out.shape[0] :]
     grad_attended = back_matmul(grad_branch, out_weight).astype(BF16)
-    grad_q, grad_k, grad_v, grad_gain_query, grad_gain_key, mlp_sum = attend_backward(
+    grad_qkv, grad_gain_query, grad_gain_key, mlp_sum = attend_backward(
         weights, query, key, value, grad_attended, mlp_partial, q_pre, k_pre, gain_query,
         gain_key, cosine, sine, n, 4,
     )
     output = (middle + mlp_sum).astype(BF16)[None]
-    grad_qkv = jnp.concatenate([grad_q, grad_k, grad_v], axis=1)
     grad_qkv_weight = outer_sum(normalized, grad_qkv).astype(BF16)
     qkv_share = lax.psum_scatter(grad_qkv_weight, "fsdp", scatter_dimension=0, tiled=True)
     gate_up_share, _ = lax.optimization_barrier((gate_up_share, grad_qkv))
@@ -976,13 +982,10 @@
     grad_normed, gain_shares = scatter_last(
         partial.astype(BF16), small_grads, n, shards, 5
     )
-    late_down, late_out, _ = lax.optimization_barrier((down_share, out_share, gain_shares))
-    down_all, final_out = share(late_down, late_out, n, 7)
     gain_shares = gain_shares.reshape(-1)
     grad_inputs, _ = rms_backward(inputs, gain_in, grad_normed)
     input_grad = (grad_middle + grad_inputs).astype(BF16)[None]
 
-    final_down = down_all.astype(F32).reshape(-1, width)
     by_step = jnp.stack(gate_up_all)
     final_gate, final_up = spread_back(
         jnp.stack(
@@ -993,9 +996,11 @@
         ),
         hidden_piece,
     )
-    final_query, final_key, final_value = finish(
-        qkv_share, (HQ * HEAD_SIZE,) + (KEY_VALUE_HEADS * HEAD_SIZE,) * 2, n, 6
-    )
+    qkv_all, down_all, out_all = finish(qkv_share, out_down_share, w_out.shape[0], n, 6)
+    final_query, final_key, final_value, final_down, final_out = widen(
+        qkv_all, down_all, out_all, (HQ * HEAD_SIZE,) + (KEY_VALUE_HEADS * HEAD_SIZE,) * 2
+    )
+    final_down = final_down.reshape(-1, width)
 
     return (
         output,

time: 396 us -> 399 us (level)
  waiting for transfers between devices: 35.9 us -> 60.1 us
  Pallas kernels: 221 us -> 210 us
  local copies, waits for them, and re-layouts: 32.2 us -> 21.4 us
    ppermute x3, waiting for transfers between devices: 0.01 us -> 14.6 us  [on_device(): gate_up_all.append(lax.ppermute(gate_up_share, 'seq', pairs))]
    pallas_call x2, Pallas kernels: 46.3 us -> 34.7 us  [the longest x1 30.4 us: finish(): pl.pallas_call(finish_kernel, out_shape=(jax.ShapeDtypeStruct((n,) + qkv....]
    reduce_scatter x1, waiting for transfers between devices: 19.1 us -> 28.9 us  [on_device(): lax.psum_scatter(jnp.concatenate([grad_out.reshape(shards, -1, width), gr...]
    unnamed x90 -> x64, local copies, waits for them, and re-layouts: 13 us -> 5.86 us
  transfers between devices with their start and end apart: 9 -> 9, of which waited for: 3 -> 5; matrix products, arithmetic and copies ran while one was open for 20% -> 20% of each run, Pallas kernels for 51% -> 45%
where the time goes in v7:
time: 399 us; the launch traced here: 392 us
  Pallas kernels  210 us (53%)
  waiting for transfers between devices  60.1 us (15%)
  matrix products  53.1 us (13%)
  other arithmetic  29.2 us (7%)
  local copies, waits for them, and re-layouts  21.4 us (5%)
  between operations  14.8 us (4%)
  starting transfers between devices  4.08 us (1%)
    pallas_call x1, Pallas kernels, attend_backward(): pl.pallas_call(backward_kernel, grid=(n, heads), out_shape=(jax.ShapeDtyp...  38.8 us
    pallas_call x1, Pallas kernels, attend_forward(): pl.pallas_call(forward_kernel, grid=(n, heads), out_shape=(jax.ShapeDtype...  36.3 us
    pallas_call x1, Pallas kernels, finish(): pl.pallas_call(finish_kernel, out_shape=(jax.ShapeDtypeStruct((n,) + qkv....  30.4 us
    reduce_scatter x1, waiting for transfers between devices, on_device(): lax.psum_scatter(jnp.concatenate([grad_out.reshape(shards, -1, width), gr...  28.9 us
    pallas_call x1, Pallas kernels, gather_first(): pl.pallas_call(gather_first_kernel, out_shape=(jax.ShapeDtypeStruct((n *...  27 us
    pallas_call x1, Pallas kernels, scatter_last(): pl.pallas_call(scatter_last_kernel, out_shape=(jax.ShapeDtypeStruct((rows...  23.7 us
    pallas_call x1, Pallas kernels, scatter_sum(): pl.pallas_call(scatter_kernel, out_shape=jax.ShapeDtypeStruct((rows, widt...  23.5 us
    pallas_call x1, Pallas kernels, gather_rows(): pl.pallas_call(gather_kernel, out_shape=jax.ShapeDtypeStruct((n * rows, w...  22.3 us
  transfers between devices with their start and end apart: 9, of which 5 were waited for; matrix products, arithmetic and copies ran while one was open for 20% of the time, Pallas kernels for 45%

profile of v7, /device:TPU:0, one launch (start us, length us, event | category | flops | bytes accessed | tf_op | source)
XLA Modules:
  0.0 392.5 jit_solution(1160347265375751064)
XLA Ops:
  7.3 1.1 copy-done
  14.2 27.0 %gather_first.1 = (bf16[1024,1024]{1,0:T(8,128)(2,1)}, f32[8,8,128]{2,1,0:T(8,128)}) custom-call(bf16[256,1024]{1,0:T(8,128)(2,1)} %bitcast.78, f32[8,128]{1,0:T(8,128)} %fusion.28.gains_ref), custom_call_target="tpu_custom_call" | custom-call | tf_op jit(solution)/shard_map/gather_first/pallas_call | solution.py:338
  45.3 1.9 fusion.19
  47.2 1.3 pad_maximum_fusion.4
  49.0 7.4 %all-gather.9.cloned.1.call-done = bf16[1792,1024]{1,0:T(8,128)(2,1)} async-done(((bf16[224,1024]{1,0:T(8,128)(2,1)}), bf16[1792,1024]{1,0:T(8,128)(2,1)}) %all-gather.9.cloned.1.call-update) | async-done | bytes 3670032 | tf_op jit(solution)/shard_map/all_gather | solution.py:886
  56.4 1.8 slice.70
  58.2 2.4 fusion.13
  60.6 1.5 slice.71.q_pre
  62.1 1.1 slice.72.k_pre
  64.0 2.7 slice.77
  66.8 36.3 %attend_forward.1 = (bf16[256,2048]{1,0:T(8,128)(2,1)}, bf16[4,1024,1024]{2,1,0:T(8,128)(2,1)}, bf16[1024,512]{1,0:T(8,128)(2,1)}, bf16[1024,256]{1,0:T(8,128)(2,1)}, bf16[1024,1024]{1,0:T(8,128)(2,1)}) custom-call(f32[1024,512]{1,0:T(8,128)} %slice.71.q_pre, f32[1024,256]{1,0:T(8,128)} %slice.72.k_pre, bf16[1024,256]{1,0:T(8,128)(2,1)} %slice.90.v_ref, ...), custom_call_target="tpu_custom_call" | custom-call | tf_op jit(solution)/shard_map/attend_forward/pallas_call | solution.py:665
  103.1 5.6 %fusion.31 = f32[1024,768]{1,0:T(8,128)} fusion(bf16[1024,1024]{1,0:T(8,128)(2,1)} %get-tuple-element.48, bf16[768,1024]{1,0:T(8,128)(2,1)} %bitcast.84), kind=kOutput, calls=%fused_computation.92 | convolution fusion | flops 1610612736 | bytes 6815744 | tf_op jit(solution)/shard_map/dot_general | solution.py:34
  108.7 3.5 multiply_reduce_fusion.2
  113.2 22.3 %shard_map.246 = bf16[1024,1024]{1,0:T(8,128)(2,1)} custom-call(bf16[256,1024]{1,0:T(8,128)(2,1)} %multiply_convert_fusion.3.x_ref), custom_call_target="tpu_custom_call" | custom-call | tf_op jit(solution)/shard_map/pallas_call | solution.py:310
  135.5 8.4 %all-gather.7.cloned.1.call-done = bf16[1024,1536]{0,1:T(8,128)(2,1)} async-done(((bf16[128,1536]{0,1:T(8,128)(2,1)}), bf16[1024,1536]{0,1:T(8,128)(2,1)}) %all-gather.7.cloned.1.call-update) | async-done | bytes 3145744 | tf_op jit(solution)/shard_map/all_gather | solution.py:900
  143.9 6.1 %fusion.32 = f32[1024,1536]{1,0:T(8,128)S(1)} fusion(bf16[1024,1024]{1,0:T(8,128)(2,1)} %shard_map.246, bf16[1024,1536]{0,1:T(8,128)(2,1)} %all-gather.7.cloned.1.call-done), kind=kOutput, calls=%fused_computation.93 | convolution fusion | flops 3221225472 | bytes 11534336 | tf_op jit(solution)/shard_map/dot_general | solution.py:26
  150.1 2.9 multiply_convert_fusion.2
  153.0 1.1 copy-done.2
  154.1 5.3 %convolution_convert_fusion.1 = bf16[1024,1536]{1,0:T(8,128)(2,1)} fusion(bf16[1024,1024]{1,0:T(8,128)(2,1)S(1)} %copy-done.7, bf16[1024,768]{1,0:T(8,128)(2,1)S(1)} %get-tuple-element.76, bf16[1024,768]{1,0:T(8,128)(2,1)S(1)} %get-tuple-element.75), kind=kOutput, calls=%fused_computation.11 | convolution fusion | flops 3229089792 | bytes 8388608 | tf_op jit(solution)/shard_map/dot_general | solution.py:30
  159.4 3.3 pad_maximum_fusion.1
  163.0 1.2 copy-done.11
  164.1 4.7 %convolution_convert_fusion.6 = bf16[768,1024]{1,0:T(8,128)(2,1)} fusion(bf16[1024,768]{1,0:T(8,128)(2,1)S(1)} %copy-done.11, bf16[1024,1024]{1,0:T(8,128)(2,1)} %get-tuple-element.48), kind=kOutput, calls=%fused_computation.26 | convolution fusion | flops 1611399168 | bytes 5242880 | tf_op jit(solution)/shard_map/dot_general | solution.py:30
  168.9 4.7 %convolution_convert_fusion.4.p_ref = bf16[1024,1024]{1,0:T(8,128)(2,1)} fusion(bf16[1024,1536]{1,0:T(8,128)(2,1)S(1)} %copy-done.5, bf16[1024,1536]{0,1:T(8,128)(2,1)S(1)} %copy-done.26), kind=kOutput, calls=%fused_computation.20 | convolution fusion | flops 3222274048 | bytes 8388608 | tf_op jit(solution)/shard_map/dot_general | solution.py:34
  173.5 23.5 %shard_map.247 = f32[256,1024]{1,0:T(8,128)} custom-call(bf16[1024,1024]{1,0:T(8,128)(2,1)} %convolution_convert_fusion.4.p_ref), custom_call_target="tpu_custom_call" | custom-call | tf_op jit(solution)/shard_map/pallas_call | solution.py:363
  197.1 1.7 multiply_reduce_fusion
  198.7 1.5 subtract_add_fusion
  200.3 2.3 convolution_convert_fusion.2.grad_own
  202.6 3.1 convolution_convert_fusion.5.bulk
  205.7 38.8 %attend_backward.1 = (bf16[1024,1024]{1,0:T(8,128)(2,1)}, f32[1,128]{1,0:T(1,128)}, f32[1,128]{1,0:T(1,128)}, f32[256,1024]{1,0:T(8,128)}) custom-call(bf16[4,1024,1024]{2,1,0:T(8,128)(2,1)} %get-tuple-element.45.p_ref, bf16[1024,512]{1,0:T(8,128)(2,1)} %get-tuple-element.46.q_ref, bf16[1024,256]{1,0:T(8,128)(2,1)} %get-tuple-element.47.k_ref, ...), custom_call_target="tpu_custom_call" | custom-call | tf_op jit(solution)/shard_map/attend_backward/pallas_call | solution.py:803
  244.5 6.1 %convolution_convert_fusion.3 = bf16[1024,1024]{1,0:T(8,128)(2,1)} fusion(bf16[1024,1024]{1,0:T(8,128)(2,1)} %get-tuple-element.53, bf16[1024,1024]{1,0:T(8,128)(2,1)} %get-tuple-element.42, f32[1024]{0:T(1024)S(1)} %get-tuple-element.85, f32[1024]{0:T(1024)S(1)} %add_rsqrt_fusion), kind=kOutput, calls=%fused_computation.19 | convolution fusion | flops 2152726528 | bytes 6299648 | tf_op jit(solution)/shard_map/dot_general | solution.py:30
  250.9 2.6 convolution_convert_fusion
  253.6 3.1 pad_maximum_fusion
  258.9 6.6 %fusion.3 = (f32[1024]{0:T(1024)S(1)}, bf16[1024,1024]{1,0:T(8,128)(2,1)}) fusion(bf16[1024,1024]{1,0:T(8,128)(2,1)} %get-tuple-element.42, f32[1024]{0:T(1024)S(1)} %add_rsqrt_fusion, bf16[1024,1024]{1,0:T(8,128)(2,1)} %get-tuple-element.53, bf16[1024,1024]{1,0:T(8,128)(2,1)} %bitcast.82), kind=kOutput, calls=%fused_computation.6 | convolution fusion | flops 2152725504 | bytes 8396800 | tf_op jit(solution)/shard_map/dot_general | solution.py:34
  266.2 23.7 %scatter_last.1 = (f32[256,1024]{1,0:T(8,128)}, f32[8,128]{1,0:T(8,128)}) custom-call(bf16[1024,1024]{1,0:T(8,128)(2,1)} %get-tuple-element.79.p_ref, f32[8,8,128]{2,1,0:T(8,128)} %bitcast.95), custom_call_target="tpu_custom_call" | custom-call | tf_op jit(solution)/shard_map/scatter_last/pallas_call | solution.py:407
  290.0 1.5 fusion.6
  291.5 1.3 slice_bitcast_fusion.2
  292.8 1.3 fusion.30
  294.1 2.1 fusion.15
  296.2 1.5 collective-permute-start.2
  298.3 1.4 collective-permute-start
  299.7 2.4 fusion.16
  302.1 6.4 %collective-permute-done.2 = bf16[128,1536]{1,0:T(8,128)(2,1)S(1)} collective-permute-done((bf16[128,1536]{1,0:T(8,128)(2,1)}, bf16[128,1536]{1,0:T(8,128)(2,1)S(1)}, u32[]{:S(2)}, u32[]{:S(2)}) %collective-permute-start.2) | collective-permute-done | bytes 393248 | tf_op jit(solution)/shard_map/ppermute | solution.py:977
  308.4 8.2 %collective-permute-done.1 = bf16[128,1536]{1,0:T(8,128)(2,1)S(1)} collective-permute-done((bf16[128,1536]{1,0:T(8,128)(2,1)}, bf16[128,1536]{1,0:T(8,128)(2,1)S(1)}, u32[]{:S(2)}, u32[]{:S(2)}) %collective-permute-start.1) | collective-permute-done | bytes 393248 | tf_op jit(solution)/shard_map/ppermute | solution.py:977
  317.0 1.3 pad_maximum_fusion.3.pieces_ref
  318.3 3.5 spread_back.1
  321.8 28.9 %reduce-scatter.6.cloned.1.call-done.joined_ref = bf16[352,1024]{1,0:T(8,128)(2,1)} async-done(((bf16[2816,1024]{1,0:T(8,128)(2,1)}), bf16[352,1024]{1,0:T(8,128)(2,1)}) %reduce-scatter.6.cloned.1.call-update) | async-done | bytes 720912 | tf_op jit(solution)/shard_map/reduce_scatter | solution.py:959
  350.7 30.4 %finish.1 = (bf16[4,128,1024]{2,1,0:T(8,128)(2,1)}, bf16[4,96,1024]{2,1,0:T(8,128)(2,1)}, bf16[256,1024]{1,0:T(8,128)(2,1)}) custom-call(bf16[128,1024]{1,0:T(8,128)(2,1)} %reduce-scatter.4.cloned.1.call-done.qkv_ref, bf16[352,1024]{1,0:T(8,128)(2,1)} %reduce-scatter.6.cloned.1.call-done.joined_ref), custom_call_target="tpu_custom_call" | custom-call | tf_op jit(solution)/shard_map/finish/pallas_call | solution.py:467
  381.1 4.3 %widen.1 = (f32[128,2048]{1,0:T(8,128)}, f32[128,1024]{1,0:T(8,128)}, f32[128,1024]{1,0:T(8,128)}, f32[4,96,1024]{2,1,0:T(8,128)}, f32[256,1024]{1,0:T(8,128)}) custom-call(bf16[4,128,1024]{2,1,0:T(8,128)(2,1)} %get-tuple-element.59.qkv_ref, bf16[4,96,1024]{2,1,0:T(8,128)(2,1)} %get-tuple-element.60.down_ref, bf16[256,1024]{1,0:T(8,128)(2,1)} %get-tuple-element.61.out_ref), custom_call_target="tpu_custom_call" | custom-call | tf_op jit(solution)/shard_map/widen/pallas_call | solution.py:510
  (112 shorter events, 16.4 us)
Async XLA Ops:
  7.2 1.1 copy-start
  7.2 4.6 %copy-start.15 = (bf16[128,3072]{1,0:T(8,128)(2,1)S(1)}, bf16[128,3072]{1,0:T(8,128)(2,1)}, u32[]{:S(2)}) copy-start(bf16[128,3072]{1,0:T(8,128)(2,1)} %param.27) | copy-start | bytes 2359300
  7.2 5.0 %copy-start.16 = (bf16[128,3072]{1,0:T(8,128)(2,1)S(1)}, bf16[128,3072]{1,0:T(8,128)(2,1)}, u32[]{:S(2)}) copy-start(bf16[128,3072]{1,0:T(8,128)(2,1)} %param.26) | copy-start | bytes 2359300
  7.2 49.2 %all-gather.9.cloned.1.call-start = ((), (), s32[]{:S(2)}) async-start(), calls=%async_computation.8 | async-start | bytes 4128768 | tf_op jit(solution)/shard_map/all_gather | solution.py:886
  11.0 2.5 copy-start.20
  11.0 2.5 copy-start.21
  11.0 2.5 copy-start.22
  11.0 2.5 copy-start.23
  11.0 32.4 %copy-start.24 = (s32[1,8]{1,0:T(1,128)S(1)}, s32[1,8]{1,0:T(1,128)}, u32[]{:S(2)}) copy-start(s32[1,8]{1,0:T(1,128)} %param.16) | copy-start | bytes 100
  11.0 32.6 %copy-start.27 = (s32[1,1024]{1,0:T(1,128)S(1)}, s32[1,1024]{1,0:T(1,128)}, u32[]{:S(2)}) copy-start(s32[1,1024]{1,0:T(1,128)} %param.17) | copy-start | bytes 12292
  11.0 97.7 %all-gather.5.cloned.1.call-start = ((), (), s32[]{:S(2)}) async-start(), calls=%async_computation.3 | async-start | bytes 4718592 | tf_op jit(solution)/shard_map/all_gather | solution.py:899
  11.8 132.1 %all-gather.7.cloned.1.call-start = ((), (), s32[]{:S(2)}) async-start(), calls=%async_computation.4 | async-start | bytes 3538944 | tf_op jit(solution)/shard_map/all_gather | solution.py:900
  13.4 282.8 %reduce-scatter.8.cloned.1.call-start = ((), (), s32[]{:S(2)}) async-start(), calls=%async_computation.7 | async-start | bytes 3538944 | tf_op jit(solution)/shard_map/reduce_scatter | solution.py:952
  41.3 7.2 %copy-start.8 = (bf16[1024,1024]{1,0:T(8,128)(2,1)S(1)}, bf16[1024,1024]{1,0:T(8,128)(2,1)}, u32[]{:S(2)}) copy-start(bf16[1024,1024]{1,0:T(8,128)(2,1)} %get-tuple-element.42) | copy-start | bytes 6291460
  44.1 4.9 %copy-start.18 = (s32[1024]{0:T(1024)}, s32[1024]{0:T(1024)S(1)}, u32[]{:S(2)}) copy-start(s32[1024]{0:T(1024)S(1)} %select_reduce_fusion) | copy-start | bytes 12292
  45.3 3.7 copy-start.19
  58.2 2.4 copy-start.9
  103.1 5.6 %copy-start.3 = (bf16[1,256,1024]{2,1,0:T(8,128)(2,1)S(1)}, bf16[1,256,1024]{2,1,0:T(8,128)(2,1)}, u32[]{:S(2)}) copy-start(bf16[1,256,1024]{2,1,0:T(8,128)(2,1)} %param.15) | copy-start | bytes 1572868
  103.1 5.6 %copy-start.6 = (bf16[256,2048]{1,0:T(8,128)(2,1)S(1)}, bf16[256,2048]{1,0:T(8,128)(2,1)}, u32[]{:S(2)}) copy-start(bf16[256,2048]{1,0:T(8,128)(2,1)} %get-tuple-element.44) | copy-start | bytes 3145732
  143.9 6.1 %copy-start.4 = (f32[1024,768]{1,0:T(8,128)S(1)}, f32[1024,768]{1,0:T(8,128)}, u32[]{:S(2)}) copy-start(f32[1024,768]{1,0:T(8,128)} %fusion.31) | copy-start | bytes 9437188
  150.1 4.1 %copy-start.7 = (bf16[1024,1024]{1,0:T(8,128)(2,1)S(1)}, bf16[1024,1024]{1,0:T(8,128)(2,1)}, u32[]{:S(2)}) copy-start(bf16[1024,1024]{1,0:T(8,128)(2,1)} %shard_map.246) | copy-start | bytes 6291460
  153.0 1.1 copy-start.2
  162.7 1.4 copy-start.11
  162.8 159.0 %reduce-scatter.4.cloned.1.call-start = ((), (), s32[]{:S(2)}) async-start(), calls=%async_computation.5 | async-start | bytes 2359296 | tf_op jit(solution)/shard_map/reduce_scatter | solution.py:972
  164.1 4.7 %copy-start.5 = (bf16[1024,1536]{1,0:T(8,128)(2,1)S(1)}, bf16[1024,1536]{1,0:T(8,128)(2,1)}, u32[]{:S(2)}) copy-start(bf16[1024,1536]{1,0:T(8,128)(2,1)} %pad_maximum_fusion.1) | copy-start | bytes 9437188
  164.1 4.7 %copy-start.26 = (bf16[1024,1536]{0,1:T(8,128)(2,1)S(1)}, bf16[1024,1536]{0,1:T(8,128)(2,1)}, u32[]{:S(2)}) copy-start(bf16[1024,1536]{0,1:T(8,128)(2,1)} %all-gather.7.cloned.1.call-done) | copy-start | bytes 9437188
  173.5 25.2 %copy-start.10 = (bf16[1,256,1024]{2,1,0:T(8,128)(2,1)S(1)}, bf16[1,256,1024]{2,1,0:T(8,128)(2,1)}, u32[]{:S(2)}) copy-start(bf16[1,256,1024]{2,1,0:T(8,128)(2,1)} %param.29) | copy-start | bytes 1572868
  197.0 3.2 copy-start.25
  200.3 2.3 copy-start.12
  200.3 2.3 copy-start.13
  250.7 100.0 %reduce-scatter.6.cloned.1.call-start = ((), (), s32[]{:S(2)}) async-start(), calls=%async_computation.6 | async-start | bytes 6488064 | tf_op jit(solution)/shard_map/reduce_scatter | solution.py:959
  250.9 2.7 copy-start.14
  256.7 0.7 copy-start.29
  256.7 1.4 copy-start.28
  296.2 20.4 %copy-start.17 = (bf16[128,1536]{1,0:T(8,128)(2,1)S(1)}, bf16[128,1536]{1,0:T(8,128)(2,1)}, u32[]{:S(2)}) copy-start(bf16[128,1536]{1,0:T(8,128)(2,1)} %reduce-scatter.8.cloned.1.call-done) | copy-start | bytes 1179652
  296.2 12.2 %collective-permute-start.2 = (bf16[128,1536]{1,0:T(8,128)(2,1)}, bf16[128,1536]{1,0:T(8,128)(2,1)S(1)}, u32[]{:S(2)}, u32[]{:S(2)}) collective-permute-start(bf16[128,1536]{1,0:T(8,128)(2,1)} %reduce-scatter.8.cloned.1.call-done), channel_id=1, source_target_pairs={{0,24},{8,0},{16,8},{24,16},{1,25},{9,1},{17,9},{25,17},{2,26},{10... | collective-permute-start | bytes 1179656 | tf_op jit(solution)/shard_map/ppermute | solution.py:977
  297.7 18.9 %collective-permute-start.1 = (bf16[128,1536]{1,0:T(8,128)(2,1)}, bf16[128,1536]{1,0:T(8,128)(2,1)S(1)}, u32[]{:S(2)}, u32[]{:S(2)}) collective-permute-start(bf16[128,1536]{1,0:T(8,128)(2,1)} %reduce-scatter.8.cloned.1.call-done), channel_id=1, source_target_pairs={{0,16},{8,24},{16,0},{24,8},{1,17},{9,25},{17,1},{25,9},{2,18},{10... | collective-permute-start | bytes 1179656 | tf_op jit(solution)/shard_map/ppermute | solution.py:977
  298.3 18.3 %collective-permute-start = (bf16[128,1536]{1,0:T(8,128)(2,1)}, bf16[128,1536]{1,0:T(8,128)(2,1)S(1)}, u32[]{:S(2)}, u32[]{:S(2)}) collective-permute-start(bf16[128,1536]{1,0:T(8,128)(2,1)} %reduce-scatter.8.cloned.1.call-done), channel_id=1, source_target_pairs={{0,8},{8,16},{16,24},{24,0},{1,9},{9,17},{17,25},{25,1},{2,10},{10... | collective-permute-start | bytes 1179656 | tf_op jit(solution)/shard_map/ppermute | solution.py:977
  317.0 68.5 %copy-start.1 = (bf16[384,1024]{1,0:T(8,128)(2,1)S(1)}, bf16[384,1024]{1,0:T(8,128)(2,1)}, u32[]{:S(2)}) copy-start(bf16[384,1024]{1,0:T(8,128)(2,1)} %param.28) | copy-start | bytes 2359300
Sparse Core Ops, SparseCore 0:
  11.1 45.2 all-gather.8
  58.0 45.6 all-gather.4
  105.9 37.9 all-gather.6
  162.9 38.5 reduce-scatter.7
  250.8 34.3 reduce-scatter.3
  287.3 63.3 reduce-scatter.5
